TPU v7x, 512 devices: a whole 4x8x8 slice. The times are simulated.
512 devices in a mesh: dp: 2 (over x_hi), seq: 8 (over y), tensor: 32 (over z, x_lo, core).
Axes of the slice: x: 4 (x_hi: 2, x_lo: 2; x = x_hi * 2 + x_lo), y: 8, z: 8, core: 2. Of those that a mesh axis runs over, the one named last changes fastest.
Arguments:
- activations: bfloat16 [4, 1536, 28672], P('dp', 'seq', 'tensor'), may hold values from -6 to 6
- gradients: bfloat16 [4, 1536, 8192], P('dp', 'seq', 'tensor'), may hold values from -6 to 6
- basis_in: bfloat16 [28672, 2048], P('tensor', 'seq'), may hold values from -0.03125 to 0.03125
- basis_out: bfloat16 [8192, 768], P('tensor', 'seq'), may hold values from -0.0625 to 0.0625
Outputs:
- corrected: float32 [2048, 768], P(('seq', 'tensor'))
All inputs are finite; a program needn't handle non-finite values.
Results may differ from a plain program's by a relative error of at most 0.0034.
Values may be sent and summed in bfloat16 or wider, within the bound.
No kernel may reach another device: no remote copies, remote signals or barrier semaphores. Data moves between devices by JAX's collectives and lax.ppermute only.
A program may use at most 64 MiB of HBM per device.

v0:
```python
import jax
import jax.numpy as jnp
from jax import lax
from jax.experimental.layout import Layout, with_layout_constraint
from jax.sharding import Mesh
from jax.sharding import PartitionSpec as P


TENSOR = ("z", "x", "c")
SEQ_TENSOR = ("seq", "z", "x", "c")
ALL = ("dp", "seq", "z", "x", "c")
F32 = jnp.float32
BF16 = jnp.bfloat16


def exchange(v, axis):
    return lax.ppermute(v, axis, [(0, 1), (1, 0)])


def all_to_all(v, axis):
    return lax.all_to_all(v, axis, 0, 0, tiled=True)


def to_everyone(v, axis):
    return all_to_all(jnp.broadcast_to(v[None], (lax.axis_size(axis), *v.shape)), axis)


def contract_last(a, b):
    return lax.dot_general(
        a, b, (((a.ndim - 1,), (b.ndim - 1,)), ((), ())), preferred_element_type=F32
    )


def contract(a, b):
    return lax.dot_general(a, b, (((1,), (0,)), ((), ())), preferred_element_type=F32)


def seq_order(y):
    shape = (8, 8, 2, 4, 8)
    shard, row, core, slot, at = (lax.broadcasted_iota(jnp.int32, shape, k) for k in range(5))
    away = jnp.where(slot == 3, 4 * core, (slot + 1) * (2 * core - 1))
    picked = ((y + away - shard) % 8 == 0) & (row == at)
    return picked.astype(BF16).reshape(64, 64)


def ring_step(v, cores):
    n = lax.axis_size("seq")
    pairs = [(y * 2 + k, (y + 1 - 2 * k) % n * 2 + k) for y in range(n) for k in cores]
    return lax.ppermute(v, ("seq", "c"), pairs)


def to_core_of_dp(v):
    near = lax.ppermute(v, ("dp", "c"), [(d * 2 + c, c * 2 + d) for d in (0, 1) for c in (0, 1)])
    far = lax.ppermute(
        v, ("dp", "c"), [(d * 2 + c, (1 - c) * 2 + d) for d in (0, 1) for c in (0, 1)]
    )
    return near, far


def body(activations, gradients, basis_in, basis_out):
    d = lax.axis_index("dp")
    c = lax.axis_index("c")
    y = lax.axis_index("seq")
    seqs, length, width = activations.shape
    tokens = seqs * length
    x_own = activations.reshape(tokens, width)
    g_own = gradients.reshape(tokens, -1)

    x_far = exchange(x_own, "dp")

    halves = basis_out.T.reshape(1, 2, -1, basis_out.shape[0])
    spread = jnp.broadcast_to(halves, (8, *halves.shape[1:])).reshape(16, -1, basis_out.shape[0])
    out_cols = all_to_all(spread, ("seq", "c"))
    out_cols = out_cols.reshape(8, 2, -1, basis_out.shape[0])

    shard = with_layout_constraint(basis_in.T, Layout(major_to_minor=(0, 1)))
    half = shard.reshape(16, 2, 8, width)
    half = lax.dynamic_index_in_dim(half, d, 1, keepdims=False).reshape(128, width)
    partner = exchange(half, "c")
    g_other = exchange(g_own, "c")
    block = jnp.concatenate([half, partner], 1)
    step1 = ring_step(block, (0, 1))
    step2 = ring_step(step1, (0, 1))
    step3 = ring_step(step2, (0, 1))
    step4 = ring_step(step3, (1,))

    first = jnp.where(c == 0, g_own, g_other)
    second = jnp.where(c == 0, g_other, g_own)
    width_out = out_cols.shape[0] * out_cols.shape[2]
    grad_partial = contract_last(out_cols[:, 0].reshape(width_out, -1), first) + contract_last(
        out_cols[:, 1].reshape(width_out, -1), second
    )
    grad_parts = all_to_all(grad_partial.reshape(16, -1, tokens), ("z", "x"))
    grad_own = grad_parts.sum(0).astype(BF16)
    grad_half = to_everyone(grad_own, ("z", "x")).reshape(8, -1, tokens)
    near, far = to_core_of_dp(grad_half)
    grads = jnp.where(d == 0, jnp.stack([near, far], 1), jnp.stack([far, near], 1))
    grads = grads.reshape(-1, tokens)

    x_rows = jnp.where(
        d == 0, jnp.concatenate([x_own, x_far], 0), jnp.concatenate([x_far, x_own], 0)
    )
    x_other = exchange(x_rows, "c")
    x_rows = lax.optimization_barrier(jnp.concatenate([x_rows, x_other], 1))
    last = jnp.where(c == 0, block, step4)
    parts = [
        contract_last(k, x_rows).astype(BF16).reshape(16, 8, -1)
        for k in (step1, step2, step3, last)
    ]
    arrived = all_to_all(jnp.stack(parts, 1).reshape(16, 32, -1), ("z", "x"))
    act = arrived.astype(F32).sum(0).astype(BF16)

    left, right = act[:, :tokens], act[:, tokens:]
    mine = jnp.where(c == 0, left, right)
    theirs = exchange(jnp.where(c == 0, right, left), "c")
    zero = jnp.where(c == 0, mine, theirs)
    one = jnp.where(c == 0, theirs, mine)
    act = contract(seq_order(y), jnp.concatenate([zero, one], 0)).astype(BF16)

    of_seq = lax.broadcasted_iota(jnp.int32, (seqs, 1, tokens), 2) // length
    chosen = of_seq == lax.broadcasted_iota(jnp.int32, (seqs, 1, tokens), 0)
    masked = jnp.where(chosen, act[None], jnp.zeros((), BF16))
    partial_blocks = contract_last(masked, grads)
    pieces = partial_blocks.reshape(seqs, 8, 8, -1).swapaxes(0, 1)
    blocks = all_to_all(pieces, "seq").sum(0)
    squared = jnp.sum(blocks * blocks, axis=0)
    near, far = to_core_of_dp(squared)
    return (near + far) / (2 * seqs * 8 * length)


def solution(mesh):
    finer = Mesh(mesh.devices.reshape(2, 8, 8, 2, 2), ALL)
    in_specs = (P("dp", "seq", TENSOR), P("dp", "seq", TENSOR), P(TENSOR, "seq"), P(TENSOR, "seq"))
    out_specs = P(SEQ_TENSOR, None)

    return jax.shard_map(body, mesh=finer, in_specs=in_specs, out_specs=out_specs, check_vma=False)
```

profile of v0, /device:TPU:1, one launch (start us, length us, event | category | flops | bytes accessed | tf_op | source)
XLA Modules:
  0.0 149.5 jit_solution(10599662007997408300)
XLA Ops:
  0.0 5.6 %collective-permute-start.2 = (bf16[384,896]{1,0:T(8,128)(2,1)}, bf16[384,896]{1,0:T(8,128)(2,1)S(1)}, u32[]{:S(2)}, u32[]{:S(2)}) collective-permute-start(bf16[384,896]{1,0:T(8,128)(2,1)} %bitcast.65), channel_id=1, source_target_pairs={{0,256},{256,0},{1,257},{257,1},{2,258},{258,2},{3,259},{259,3},{4... | collective-permute-start | bytes 2064392 | tf_op jit(solution)/shard_map/ppermute | solution.py:17
  5.6 1.6 %broadcast_in_dim.41 = bf16[8,2,48,256]{3,2,1,0:T(8,128)(2,1)} broadcast(bf16[2,48,256]{2,1,0:T(8,128)(2,1)} %bitcast.71), dimensions={1,2,3} | broadcast | bytes 442368 | tf_op jit(solution)/shard_map/broadcast_in_dim | solution.py:72
  7.2 8.1 %all-to-all-start.1 = ((bf16[16,48,256]{2,1,0:T(8,128)(2,1)}), bf16[16,48,256]{2,1,0:T(8,128)(2,1)S(1)}, u32[]{:S(2)}, u32[]{:S(2)}) async-start(bf16[16,48,256]{2,1,0:T(8,128)(2,1)} %bitcast.17), calls=%async_computation.1 | async-start | bytes 786432 | tf_op jit(solution)/shard_map/all_to_all | solution.py:21
  15.3 1.3 copy.17
  16.6 2.0 %collective-permute-start = (bf16[128,896]{1,0:T(8,128)(2,1)S(1)}, bf16[128,896]{1,0:T(8,128)(2,1)S(1)}, u32[]{:S(2)}, u32[]{:S(2)}) collective-permute-start(bf16[128,896]{1,0:T(8,128)(2,1)S(1)} %dynamic-slice_bitcast_fusion), channel_id=1, source_target_pairs={{0,1},{1,0},{2,3},{3,2},{4,5},{5,4},{6,7},{7,6},{8,9},{9,8},{10,11... | collective-permute-start | bytes 688136 | tf_op jit(solution)/shard_map/ppermute | solution.py:17
  18.6 2.3 %collective-permute-start.8 = (bf16[384,256]{1,0:T(8,128)(2,1)}, bf16[384,256]{1,0:T(8,128)(2,1)}, u32[]{:S(2)}, u32[]{:S(2)}) collective-permute-start(bf16[384,256]{1,0:T(8,128)(2,1)} %bitcast.62), channel_id=1, source_target_pairs={{0,1},{1,0},{2,3},{3,2},{4,5},{5,4},{6,7},{7,6},{8,9},{9,8},{10,11... | collective-permute-start | bytes 589832 | tf_op jit(solution)/shard_map/ppermute | solution.py:17
  21.8 4.5 %collective-permute-start.1 = (bf16[128,1792]{1,0:T(8,128)(2,1)}, bf16[128,1792]{1,0:T(8,128)(2,1)}, u32[]{:S(2)}, u32[]{:S(2)}) collective-permute-start(bf16[128,1792]{1,0:T(8,128)(2,1)} %pad_maximum_fusion.1), channel_id=1, source_target_pairs={{0,32},{1,225},{32,64},{33,1},{64,96},{65,33},{96,128},{97,65},{12... | collective-permute-start | bytes 1376264 | tf_op jit(solution)/shard_map/ppermute | solution.py:49
  26.8 1.9 %collective-permute-start.3 = (bf16[768,896]{1,0:T(8,128)(2,1)S(1)}, bf16[768,896]{1,0:T(8,128)(2,1)S(1)}, u32[]{:S(2)}, u32[]{:S(2)}) collective-permute-start(bf16[768,896]{1,0:T(8,128)(2,1)S(1)} %maximum_select_fusion), channel_id=1, source_target_pairs={{0,1},{1,0},{2,3},{3,2},{4,5},{5,4},{6,7},{7,6},{8,9},{9,8},{10,11... | collective-permute-start | bytes 4128776 | tf_op jit(solution)/shard_map/ppermute | solution.py:17
  28.8 1.0 all-to-all-done.1
  30.1 2.1 %convolution_add_fusion = f32[384,384]{0,1:T(8,128)} fusion(f32[384,384]{0,1:T(8,128)S(1)} %fusion.7, bf16[384,256]{1,0:T(8,128)(2,1)S(1)} %bitcast.60, bf16[384,256]{1,0:T(8,128)(2,1)S(1)} %bitcast.64, bf16[384,256]{1,0:T(8,128)(2,1)} %collective-permute-done.8, pred[]{:T(512)S(6)} %eq.44), kind=kOutput, calls=%fused_computation.2 | convolution fusion | flops 75743232 | bytes 1769473 | tf_op jit(solution)/shard_map/dot_general | solution.py:29
  32.2 10.2 %all-to-all-start.2 = ((f32[16,24,384]{2,1,0:T(8,128)}), f32[16,24,384]{2,1,0:T(8,128)S(1)}, u32[]{:S(2)}, u32[]{:S(2)}) async-start(f32[16,24,384]{2,1,0:T(8,128)} %bitcast.22), calls=%async_computation.2 | async-start | bytes 1179648 | tf_op jit(solution)/shard_map/all_to_all | solution.py:21
  42.4 2.1 %collective-permute-start.4 = (bf16[128,1792]{1,0:T(8,128)(2,1)}, bf16[128,1792]{1,0:T(8,128)(2,1)S(1)}, u32[]{:S(2)}, u32[]{:S(2)}) collective-permute-start(bf16[128,1792]{1,0:T(8,128)(2,1)} %collective-permute-done.1), channel_id=1, source_target_pairs={{0,32},{1,225},{32,64},{33,1},{64,96},{65,33},{96,128},{97,65},{12... | collective-permute-start | bytes 1376264 | tf_op jit(solution)/shard_map/ppermute | solution.py:49
  44.5 7.6 %collective-permute-done.4 = bf16[128,1792]{1,0:T(8,128)(2,1)S(1)} collective-permute-done((bf16[128,1792]{1,0:T(8,128)(2,1)}, bf16[128,1792]{1,0:T(8,128)(2,1)S(1)}, u32[]{:S(2)}, u32[]{:S(2)}) %collective-permute-start.4) | collective-permute-done | bytes 458784 | tf_op jit(solution)/shard_map/ppermute | solution.py:49
  52.1 3.3 %collective-permute-start.5 = (bf16[128,1792]{1,0:T(8,128)(2,1)S(1)}, bf16[128,1792]{1,0:T(8,128)(2,1)}, u32[]{:S(2)}, u32[]{:S(2)}) collective-permute-start(bf16[128,1792]{1,0:T(8,128)(2,1)S(1)} %collective-permute-done.4), channel_id=1, source_target_pairs={{0,32},{1,225},{32,64},{33,1},{64,96},{65,33},{96,128},{97,65},{12... | collective-permute-start | bytes 1376264 | tf_op jit(solution)/shard_map/ppermute | solution.py:49
  55.4 6.3 %collective-permute-done.5 = bf16[128,1792]{1,0:T(8,128)(2,1)} collective-permute-done((bf16[128,1792]{1,0:T(8,128)(2,1)S(1)}, bf16[128,1792]{1,0:T(8,128)(2,1)}, u32[]{:S(2)}, u32[]{:S(2)}) %collective-permute-start.5) | collective-permute-done | bytes 458784 | tf_op jit(solution)/shard_map/ppermute | solution.py:49
  61.7 4.2 %collective-permute-start.6 = (bf16[128,1792]{1,0:T(8,128)(2,1)}, bf16[128,1792]{1,0:T(8,128)(2,1)}, u32[]{:S(2)}, u32[]{:S(2)}) collective-permute-start(bf16[128,1792]{1,0:T(8,128)(2,1)} %collective-permute-done.5), channel_id=1, source_target_pairs={{1,225},{33,1},{65,33},{97,65},{129,97},{161,129},{193,161},{225,1... | collective-permute-start | bytes 1376264 | tf_op jit(solution)/shard_map/ppermute | solution.py:49
  66.8 7.6 %all-to-all-start.3 = ((bf16[16,24,384]{2,1,0:T(8,128)(2,1)}), bf16[16,24,384]{2,1,0:T(8,128)(2,1)S(1)}, u32[]{:S(2)}, u32[]{:S(2)}) async-start(bf16[16,24,384]{2,1,0:T(8,128)(2,1)} %broadcast_in_dim.42), calls=%async_computation.3 | async-start | bytes 589824 | tf_op jit(solution)/shard_map/all_to_all | solution.py:21
  74.5 2.1 %fusion.2 = bf16[16,1,8,768]{3,2,1,0:T(8,128)(2,1)S(1)} fusion(bf16[128,1792]{1,0:T(8,128)(2,1)} %collective-permute-done.5, bf16[768,1792]{1,0:T(8,128)(2,1)S(1)} %pad_maximum_fusion), kind=kOutput, calls=%fused_computation.10 | convolution fusion | flops 352419840 | bytes 3407872 | tf_op jit(solution)/shard_map/dot_general | solution.py:29
  76.7 1.0 fusion.1
  77.7 2.1 %fusion = bf16[16,1,8,768]{3,2,1,0:T(8,128)(2,1)S(1)} fusion(bf16[128,1792]{1,0:T(8,128)(2,1)} %collective-permute-done.1, bf16[768,1792]{1,0:T(8,128)(2,1)S(1)} %pad_maximum_fusion), kind=kOutput, calls=%fused_computation.8 | convolution fusion | flops 352419840 | bytes 3407872 | tf_op jit(solution)/shard_map/dot_general | solution.py:29
  79.8 2.1 %fusion.3 = bf16[16,1,8,768]{3,2,1,0:T(8,128)(2,1)S(1)} fusion(bf16[768,1792]{1,0:T(8,128)(2,1)S(1)} %pad_maximum_fusion, bf16[128,1792]{1,0:T(8,128)(2,1)} %collective-permute-done.6, pred[]{:T(512)S(6)} %eq.44, bf16[128,896]{1,0:T(8,128)(2,1)S(1)} %copy-done.7, bf16[128,896]{1,0:T(8,128)(2,1)S(1)} %copy-done.1), kind=kOutput, calls=%fused_computation.11 | convolution fusion | flops 353566720 | bytes 3866625 | tf_op jit(solution)/shard_map/dot_general | solution.py:29
  81.9 1.0 maximum_bitcast_fusion
  82.9 2.0 %all-to-all-done.3 = bf16[16,24,384]{2,1,0:T(8,128)(2,1)S(1)} async-done(((bf16[16,24,384]{2,1,0:T(8,128)(2,1)}), bf16[16,24,384]{2,1,0:T(8,128)(2,1)S(1)}, u32[]{:S(2)}, u32[]{:S(2)}) %all-to-all-start.3) | async-done | bytes 294944 | tf_op jit(solution)/shard_map/all_to_all | solution.py:21
  84.9 5.6 %all-to-all-start = ((bf16[16,32,768]{2,1,0:T(8,128)(2,1)}), bf16[16,32,768]{2,1,0:T(8,128)(2,1)S(1)}, u32[]{:S(2)}, u32[]{:S(2)}) async-start(bf16[16,32,768]{2,1,0:T(8,128)(2,1)} %maximum_bitcast_fusion), calls=%async_computation | async-start | bytes 1572864 | tf_op jit(solution)/shard_map/all_to_all | solution.py:21
  91.1 3.2 %collective-permute-start.10 = (bf16[8,48,384]{2,1,0:T(8,128)(2,1)S(1)}, bf16[8,48,384]{2,1,0:T(8,128)(2,1)S(1)}, u32[]{:S(2)}, u32[]{:S(2)}) collective-permute-start(bf16[8,48,384]{2,1,0:T(8,128)(2,1)S(1)} %bitcast.67), channel_id=1, source_target_pairs={{0,256},{1,0},{256,257},{257,1},{2,258},{3,2},{258,259},{259,3},{4... | collective-permute-start | bytes 884744 | tf_op jit(solution)/shard_map/ppermute | solution.py:54
  94.2 3.5 %collective-permute-start.9 = (bf16[8,48,384]{2,1,0:T(8,128)(2,1)S(1)}, bf16[8,48,384]{2,1,0:T(8,128)(2,1)S(1)}, u32[]{:S(2)}, u32[]{:S(2)}) collective-permute-start(bf16[8,48,384]{2,1,0:T(8,128)(2,1)S(1)} %bitcast.68), channel_id=1, source_target_pairs={{0,0},{1,256},{256,1},{257,257},{2,2},{3,258},{258,3},{259,259},{4... | collective-permute-start | bytes 884744 | tf_op jit(solution)/shard_map/ppermute | solution.py:53
  98.0 13.0 %all-to-all-done = bf16[16,32,768]{2,1,0:T(8,128)(2,1)S(1)} async-done(((bf16[16,32,768]{2,1,0:T(8,128)(2,1)}), bf16[16,32,768]{2,1,0:T(8,128)(2,1)S(1)}, u32[]{:S(2)}, u32[]{:S(2)}) %all-to-all-start) | async-done | bytes 786464 | tf_op jit(solution)/shard_map/all_to_all | solution.py:21
  111.1 5.4 %collective-permute-start.7 = (bf16[32,384]{1,0:T(8,128)(2,1)S(1)}, bf16[32,384]{1,0:T(8,128)(2,1)S(1)}, u32[]{:S(2)}, u32[]{:S(2)}) collective-permute-start(bf16[32,384]{1,0:T(8,128)(2,1)S(1)} %broadcast_select_fusion.2), channel_id=1, source_target_pairs={{0,1},{1,0},{2,3},{3,2},{4,5},{5,4},{6,7},{7,6},{8,9},{9,8},{10,11... | collective-permute-start | bytes 73736 | tf_op jit(solution)/shard_map/ppermute | solution.py:17
  117.9 19.6 %all_to_all.25 = f32[8,2,8,768]{3,2,1,0:T(8,128)S(1)} all-to-all(f32[8,2,8,768]{3,2,1,0:T(8,128)S(1)} %copy.22), channel_id=1, replica_groups=mesh['dp'=2,'seq'=8,'z'=8,'x'=2,'c'=2] {'seq'}, dimensions={0} | all-to-all | bytes 786432 | tf_op jit(solution)/shard_map/all_to_all | solution.py:21
  137.6 5.2 %collective-permute-start.11 = (f32[8,768]{1,0:T(8,128)S(1)}, f32[8,768]{1,0:T(8,128)S(1)}, u32[]{:S(2)}, u32[]{:S(2)}) collective-permute-start(f32[8,768]{1,0:T(8,128)S(1)} %multiply_reduce_fusion), channel_id=1, source_target_pairs={{0,0},{1,256},{256,1},{257,257},{2,2},{3,258},{258,3},{259,259},{4... | collective-permute-start | bytes 73736 | tf_op jit(solution)/shard_map/ppermute | solution.py:53
  142.8 1.9 %collective-permute-start.12 = (f32[8,768]{1,0:T(8,128)S(1)}, f32[8,768]{1,0:T(8,128)S(1)}, u32[]{:S(2)}, u32[]{:S(2)}) collective-permute-start(f32[8,768]{1,0:T(8,128)S(1)} %multiply_reduce_fusion), channel_id=1, source_target_pairs={{0,256},{1,0},{256,257},{257,1},{2,258},{3,2},{258,259},{259,3},{4... | collective-permute-start | bytes 73736 | tf_op jit(solution)/shard_map/ppermute | solution.py:54
  144.7 4.1 %collective-permute-done.12 = f32[8,768]{1,0:T(8,128)S(1)} collective-permute-done((f32[8,768]{1,0:T(8,128)S(1)}, f32[8,768]{1,0:T(8,128)S(1)}, u32[]{:S(2)}, u32[]{:S(2)}) %collective-permute-start.12) | collective-permute-done | bytes 24608 | tf_op jit(solution)/shard_map/ppermute | solution.py:54
  (64 shorter events, 5.7 us)
Async XLA Ops:
  0.0 26.3 %copy-start.3 = (bf16[2,192,896]{2,1,0:T(8,128)(2,1)S(1)}, bf16[2,192,896]{2,1,0:T(8,128)(2,1)}, u32[]{:S(2)}) copy-start(bf16[2,192,896]{2,1,0:T(8,128)(2,1)} %param.4) | copy-start | bytes 2064388
  0.0 26.3 %collective-permute-start.2 = (bf16[384,896]{1,0:T(8,128)(2,1)}, bf16[384,896]{1,0:T(8,128)(2,1)S(1)}, u32[]{:S(2)}, u32[]{:S(2)}) collective-permute-start(bf16[384,896]{1,0:T(8,128)(2,1)} %bitcast.65), channel_id=1, source_target_pairs={{0,256},{256,0},{1,257},{257,1},{2,258},{258,2},{3,259},{259,3},{4... | collective-permute-start | bytes 2064392 | tf_op jit(solution)/shard_map/ppermute | solution.py:17
  7.2 22.6 %all-to-all-start.1 = ((bf16[16,48,256]{2,1,0:T(8,128)(2,1)}), bf16[16,48,256]{2,1,0:T(8,128)(2,1)S(1)}, u32[]{:S(2)}, u32[]{:S(2)}) async-start(bf16[16,48,256]{2,1,0:T(8,128)(2,1)} %bitcast.17), calls=%async_computation.1 | async-start | bytes 786432 | tf_op jit(solution)/shard_map/all_to_all | solution.py:21
  15.3 14.5 %copy-start.2 = (bf16[2,192,256]{2,1,0:T(8,128)(2,1)S(1)}, bf16[2,192,256]{2,1,0:T(8,128)(2,1)}, u32[]{:S(2)}) copy-start(bf16[2,192,256]{2,1,0:T(8,128)(2,1)} %param.5) | copy-start | bytes 589828
  16.6 9.7 %copy-start = (bf16[128,896]{1,0:T(8,128)(2,1)}, bf16[128,896]{1,0:T(8,128)(2,1)S(1)}, u32[]{:S(2)}) copy-start(bf16[128,896]{1,0:T(8,128)(2,1)S(1)} %dynamic-slice_bitcast_fusion) | copy-start | bytes 688132
  16.6 4.4 %collective-permute-start = (bf16[128,896]{1,0:T(8,128)(2,1)S(1)}, bf16[128,896]{1,0:T(8,128)(2,1)S(1)}, u32[]{:S(2)}, u32[]{:S(2)}) collective-permute-start(bf16[128,896]{1,0:T(8,128)(2,1)S(1)} %dynamic-slice_bitcast_fusion), channel_id=1, source_target_pairs={{0,1},{1,0},{2,3},{3,2},{4,5},{5,4},{6,7},{7,6},{8,9},{9,8},{10,11... | collective-permute-start | bytes 688136 | tf_op jit(solution)/shard_map/ppermute | solution.py:17
  18.6 11.1 %collective-permute-start.8 = (bf16[384,256]{1,0:T(8,128)(2,1)}, bf16[384,256]{1,0:T(8,128)(2,1)}, u32[]{:S(2)}, u32[]{:S(2)}) collective-permute-start(bf16[384,256]{1,0:T(8,128)(2,1)} %bitcast.62), channel_id=1, source_target_pairs={{0,1},{1,0},{2,3},{3,2},{4,5},{5,4},{6,7},{7,6},{8,9},{9,8},{10,11... | collective-permute-start | bytes 589832 | tf_op jit(solution)/shard_map/ppermute | solution.py:17
  21.0 5.3 %copy-start.6 = (bf16[128,896]{1,0:T(8,128)(2,1)}, bf16[128,896]{1,0:T(8,128)(2,1)S(1)}, u32[]{:S(2)}) copy-start(bf16[128,896]{1,0:T(8,128)(2,1)S(1)} %collective-permute-done) | copy-start | bytes 688132
  21.8 20.5 %collective-permute-start.1 = (bf16[128,1792]{1,0:T(8,128)(2,1)}, bf16[128,1792]{1,0:T(8,128)(2,1)}, u32[]{:S(2)}, u32[]{:S(2)}) collective-permute-start(bf16[128,1792]{1,0:T(8,128)(2,1)} %pad_maximum_fusion.1), channel_id=1, source_target_pairs={{0,32},{1,225},{32,64},{33,1},{64,96},{65,33},{96,128},{97,65},{12... | collective-permute-start | bytes 1376264 | tf_op jit(solution)/shard_map/ppermute | solution.py:49
  26.8 47.5 %collective-permute-start.3 = (bf16[768,896]{1,0:T(8,128)(2,1)S(1)}, bf16[768,896]{1,0:T(8,128)(2,1)S(1)}, u32[]{:S(2)}, u32[]{:S(2)}) collective-permute-start(bf16[768,896]{1,0:T(8,128)(2,1)S(1)} %maximum_select_fusion), channel_id=1, source_target_pairs={{0,1},{1,0},{2,3},{3,2},{4,5},{5,4},{6,7},{7,6},{8,9},{9,8},{10,11... | collective-permute-start | bytes 4128776 | tf_op jit(solution)/shard_map/ppermute | solution.py:17
  32.2 33.8 %all-to-all-start.2 = ((f32[16,24,384]{2,1,0:T(8,128)}), f32[16,24,384]{2,1,0:T(8,128)S(1)}, u32[]{:S(2)}, u32[]{:S(2)}) async-start(f32[16,24,384]{2,1,0:T(8,128)} %bitcast.22), calls=%async_computation.2 | async-start | bytes 1179648 | tf_op jit(solution)/shard_map/all_to_all | solution.py:21
  42.4 9.7 %collective-permute-start.4 = (bf16[128,1792]{1,0:T(8,128)(2,1)}, bf16[128,1792]{1,0:T(8,128)(2,1)S(1)}, u32[]{:S(2)}, u32[]{:S(2)}) collective-permute-start(bf16[128,1792]{1,0:T(8,128)(2,1)} %collective-permute-done.1), channel_id=1, source_target_pairs={{0,32},{1,225},{32,64},{33,1},{64,96},{65,33},{96,128},{97,65},{12... | collective-permute-start | bytes 1376264 | tf_op jit(solution)/shard_map/ppermute | solution.py:49
  52.1 9.6 %copy-start.4 = (bf16[128,1792]{1,0:T(8,128)(2,1)}, bf16[128,1792]{1,0:T(8,128)(2,1)S(1)}, u32[]{:S(2)}) copy-start(bf16[128,1792]{1,0:T(8,128)(2,1)S(1)} %collective-permute-done.4) | copy-start | bytes 1376260
  52.1 9.6 %collective-permute-start.5 = (bf16[128,1792]{1,0:T(8,128)(2,1)S(1)}, bf16[128,1792]{1,0:T(8,128)(2,1)}, u32[]{:S(2)}, u32[]{:S(2)}) collective-permute-start(bf16[128,1792]{1,0:T(8,128)(2,1)S(1)} %collective-permute-done.4), channel_id=1, source_target_pairs={{0,32},{1,225},{32,64},{33,1},{64,96},{65,33},{96,128},{97,65},{12... | collective-permute-start | bytes 1376264 | tf_op jit(solution)/shard_map/ppermute | solution.py:49
  61.7 18.1 %collective-permute-start.6 = (bf16[128,1792]{1,0:T(8,128)(2,1)}, bf16[128,1792]{1,0:T(8,128)(2,1)}, u32[]{:S(2)}, u32[]{:S(2)}) collective-permute-start(bf16[128,1792]{1,0:T(8,128)(2,1)} %collective-permute-done.5), channel_id=1, source_target_pairs={{1,225},{33,1},{65,33},{97,65},{129,97},{161,129},{193,161},{225,1... | collective-permute-start | bytes 1376264 | tf_op jit(solution)/shard_map/ppermute | solution.py:49
  66.8 18.1 %all-to-all-start.3 = ((bf16[16,24,384]{2,1,0:T(8,128)(2,1)}), bf16[16,24,384]{2,1,0:T(8,128)(2,1)S(1)}, u32[]{:S(2)}, u32[]{:S(2)}) async-start(bf16[16,24,384]{2,1,0:T(8,128)(2,1)} %broadcast_in_dim.42), calls=%async_computation.3 | async-start | bytes 589824 | tf_op jit(solution)/shard_map/all_to_all | solution.py:21
  74.5 2.1 %copy-start.5 = (bf16[128,1792]{1,0:T(8,128)(2,1)S(1)}, bf16[128,1792]{1,0:T(8,128)(2,1)}, u32[]{:S(2)}) copy-start(bf16[128,1792]{1,0:T(8,128)(2,1)} %copy-done.4) | copy-start | bytes 1376260
  76.7 3.1 %copy-start.1 = (bf16[128,896]{1,0:T(8,128)(2,1)S(1)}, bf16[128,896]{1,0:T(8,128)(2,1)}, u32[]{:S(2)}) copy-start(bf16[128,896]{1,0:T(8,128)(2,1)} %copy-done) | copy-start | bytes 688132
  76.7 3.1 %copy-start.7 = (bf16[128,896]{1,0:T(8,128)(2,1)S(1)}, bf16[128,896]{1,0:T(8,128)(2,1)}, u32[]{:S(2)}) copy-start(bf16[128,896]{1,0:T(8,128)(2,1)} %copy-done.6) | copy-start | bytes 688132
  84.9 26.1 %all-to-all-start = ((bf16[16,32,768]{2,1,0:T(8,128)(2,1)}), bf16[16,32,768]{2,1,0:T(8,128)(2,1)S(1)}, u32[]{:S(2)}, u32[]{:S(2)}) async-start(bf16[16,32,768]{2,1,0:T(8,128)(2,1)} %maximum_bitcast_fusion), calls=%async_computation | async-start | bytes 1572864 | tf_op jit(solution)/shard_map/all_to_all | solution.py:21
  91.1 25.4 %collective-permute-start.10 = (bf16[8,48,384]{2,1,0:T(8,128)(2,1)S(1)}, bf16[8,48,384]{2,1,0:T(8,128)(2,1)S(1)}, u32[]{:S(2)}, u32[]{:S(2)}) collective-permute-start(bf16[8,48,384]{2,1,0:T(8,128)(2,1)S(1)} %bitcast.67), channel_id=1, source_target_pairs={{0,256},{1,0},{256,257},{257,1},{2,258},{3,2},{258,259},{259,3},{4... | collective-permute-start | bytes 884744 | tf_op jit(solution)/shard_map/ppermute | solution.py:54
  94.2 22.3 %collective-permute-start.9 = (bf16[8,48,384]{2,1,0:T(8,128)(2,1)S(1)}, bf16[8,48,384]{2,1,0:T(8,128)(2,1)S(1)}, u32[]{:S(2)}, u32[]{:S(2)}) collective-permute-start(bf16[8,48,384]{2,1,0:T(8,128)(2,1)S(1)} %bitcast.68), channel_id=1, source_target_pairs={{0,0},{1,256},{256,1},{257,257},{2,2},{3,258},{258,3},{259,259},{4... | collective-permute-start | bytes 884744 | tf_op jit(solution)/shard_map/ppermute | solution.py:53
  111.1 6.3 %collective-permute-start.7 = (bf16[32,384]{1,0:T(8,128)(2,1)S(1)}, bf16[32,384]{1,0:T(8,128)(2,1)S(1)}, u32[]{:S(2)}, u32[]{:S(2)}) collective-permute-start(bf16[32,384]{1,0:T(8,128)(2,1)S(1)} %broadcast_select_fusion.2), channel_id=1, source_target_pairs={{0,1},{1,0},{2,3},{3,2},{4,5},{5,4},{6,7},{7,6},{8,9},{9,8},{10,11... | collective-permute-start | bytes 73736 | tf_op jit(solution)/shard_map/ppermute | solution.py:17
  137.6 7.1 %collective-permute-start.11 = (f32[8,768]{1,0:T(8,128)S(1)}, f32[8,768]{1,0:T(8,128)S(1)}, u32[]{:S(2)}, u32[]{:S(2)}) collective-permute-start(f32[8,768]{1,0:T(8,128)S(1)} %multiply_reduce_fusion), channel_id=1, source_target_pairs={{0,0},{1,256},{256,1},{257,257},{2,2},{3,258},{258,3},{259,259},{4... | collective-permute-start | bytes 73736 | tf_op jit(solution)/shard_map/ppermute | solution.py:53
  142.8 6.1 %collective-permute-start.12 = (f32[8,768]{1,0:T(8,128)S(1)}, f32[8,768]{1,0:T(8,128)S(1)}, u32[]{:S(2)}, u32[]{:S(2)}) collective-permute-start(f32[8,768]{1,0:T(8,128)S(1)} %multiply_reduce_fusion), channel_id=1, source_target_pairs={{0,256},{1,0},{256,257},{257,1},{2,258},{3,2},{258,259},{259,3},{4... | collective-permute-start | bytes 73736 | tf_op jit(solution)/shard_map/ppermute | solution.py:54
where the time goes:
time: 151 us; the launch traced here: 149 us
  starting transfers between devices  76.6 us (51%)
  waiting for transfers between devices  34.7 us (23%)
  blocking collectives  19.6 us (13%)
  matrix products  10.2 us (7%)
  local copies, waits for them, and re-layouts  4.41 us (3%)
  other arithmetic  3.53 us (2%)
    all_to_all x4, starting transfers between devices, all_to_all(): return lax.all_to_all(v, axis, 0, 0, tiled=True)  31.4 us
    all_to_all x1, blocking collectives, all_to_all(): return lax.all_to_all(v, axis, 0, 0, tiled=True)  19.6 us
    ppermute x5, starting transfers between devices, exchange(): return lax.ppermute(v, axis, [(0, 1), (1, 0)])  17.3 us
    all_to_all x4, waiting for transfers between devices, all_to_all(): return lax.all_to_all(v, axis, 0, 0, tiled=True)  16 us
    ppermute x4, starting transfers between devices, ring_step(): return lax.ppermute(v, ('seq', 'c'), pairs)  14.2 us
    ppermute x4, waiting for transfers between devices, ring_step(): return lax.ppermute(v, ('seq', 'c'), pairs)  13.9 us
    dot_general x7, matrix products, contract_last(): lax.dot_general(a, b, (((a.ndim - 1,), (b.ndim - 1,)), ((), ())), preferr...  9.96 us
    ppermute x2, starting transfers between devices, to_core_of_dp(): lax.ppermute(v, ('dp', 'c'), [(d * 2 + c, c * 2 + d) for d in (0, 1) for...  8.71 us
  transfers between devices with their start and end apart: 17, of which 7 were waited for; matrix products, arithmetic and copies ran while one was open for 11% of the time, Pallas kernels for 0%

commit v1 on v0

--- a/solution.py
+++ b/solution.py
@@ -1,8 +1,10 @@
 import jax
 import jax.numpy as jnp
 from jax import lax
+from jax.experimental import pallas as pl
 from jax.experimental.layout import Layout, with_layout_constraint
 from jax.sharding import Mesh
+from jax.experimental.pallas import tpu as pltpu
 from jax.sharding import PartitionSpec as P
 
 
@@ -41,6 +43,63 @@
     away = jnp.where(slot == 3, 4 * core, (slot + 1) * (2 * core - 1))
     picked = ((y + away - shard) % 8 == 0) & (row == at)
     return picked.astype(BF16).reshape(64, 64)
+
+
+def grad_kernel(core, cols, own, other, out):
+    lower = core[0] == 0
+    rows = cols.shape[0] * cols.shape[2]
+    first = jnp.where(lower, own[...], other[...])
+    second = jnp.where(lower, other[...], own[...])
+    out[...] = contract_last(cols[:, 0].reshape(rows, -1), first) + contract_last(
+        cols[:, 1].reshape(rows, -1), second
+    )
+
+
+def early_kernel(one, two, three, here, there, out):
+    width = here.shape[1]
+    for k, block in enumerate((one, two, three)):
+        found = contract_last(block[:, :width], here[...])
+        found = found + contract_last(block[:, width:], there[...])
+        out[:, k] = found.reshape(16, 8, -1).astype(BF16)
+
+
+def last_kernel(core, own, far, here, there, filled, out):
+    del filled
+    width = here.shape[1]
+    block = jnp.where(core[0] == 0, own[...], far[...])
+    found = contract_last(block[:, :width], here[...])
+    found = found + contract_last(block[:, width:], there[...])
+    out[:, 0] = found.reshape(16, 8, -1).astype(BF16)
+
+
+def projected_parts(c, block, steps, here, there):
+    tokens, width = here.shape
+    lanes = 256
+    whole = pl.BlockSpec(block.shape, lambda n: (0, 0))
+    rows = pl.BlockSpec((lanes, width), lambda n: (n, 0))
+    shape = jax.ShapeDtypeStruct((16, 4, 8, tokens), BF16)
+    filled = pl.pallas_call(
+        early_kernel,
+        grid=(tokens // lanes,),
+        in_specs=[whole, whole, whole, rows, rows],
+        out_specs=pl.BlockSpec((16, 4, 8, lanes), lambda n: (0, 0, 0, n)),
+        out_shape=shape,
+    )(*steps[:3], here, there)
+    return pl.pallas_call(
+        last_kernel,
+        grid=(tokens // lanes,),
+        in_specs=[
+            pl.BlockSpec(memory_space=pltpu.SMEM),
+            whole,
+            whole,
+            rows,
+            rows,
+            pl.BlockSpec(memory_space=pl.ANY),
+        ],
+        out_specs=pl.BlockSpec((16, 1, 8, lanes), lambda n: (0, 3, 0, n)),
+        out_shape=shape,
+        input_output_aliases={5: 0},
+    )(c.reshape(1), block, steps[3], here, there, filled)
 
 
 def ring_step(v, cores):
@@ -84,12 +143,13 @@
     step3 = ring_step(step2, (0, 1))
     step4 = ring_step(step3, (1,))
 
-    first = jnp.where(c == 0, g_own, g_other)
-    second = jnp.where(c == 0, g_other, g_own)
-    width_out = out_cols.shape[0] * out_cols.shape[2]
-    grad_partial = contract_last(out_cols[:, 0].reshape(width_out, -1), first) + contract_last(
-        out_cols[:, 1].reshape(width_out, -1), second
-    )
+    grad_partial = pl.pallas_call(
+        grad_kernel,
+        in_specs=[pl.BlockSpec(memory_space=pltpu.SMEM)]
+        + [pl.BlockSpec(memory_space=pltpu.VMEM)] * 3,
+        out_specs=pl.BlockSpec(memory_space=pltpu.VMEM),
+        out_shape=jax.ShapeDtypeStruct((8 * out_cols.shape[2], tokens), F32),
+    )(c.reshape(1), out_cols, g_own, g_other)
     grad_parts = all_to_all(grad_partial.reshape(16, -1, tokens), ("z", "x"))
     grad_own = grad_parts.sum(0).astype(BF16)
     grad_half = to_everyone(grad_own, ("z", "x")).reshape(8, -1, tokens)
@@ -101,14 +161,9 @@
         d == 0, jnp.concatenate([x_own, x_far], 0), jnp.concatenate([x_far, x_own], 0)
     )
     x_other = exchange(x_rows, "c")
-    x_rows = lax.optimization_barrier(jnp.concatenate([x_rows, x_other], 1))
-    last = jnp.where(c == 0, block, step4)
-    parts = [
-        contract_last(k, x_rows).astype(BF16).reshape(16, 8, -1)
-        for k in (step1, step2, step3, last)
-    ]
-    arrived = all_to_all(jnp.stack(parts, 1).reshape(16, 32, -1), ("z", "x"))
-    act = arrived.astype(F32).sum(0).astype(BF16)
+    parts = projected_parts(c, block, (step1, step2, step3, step4), x_rows, x_other)
+    arrived = all_to_all(parts, ("z", "x"))
+    act = arrived.astype(F32).sum(0).astype(BF16).reshape(32, -1)
 
     left, right = act[:, :tokens], act[:, tokens:]
     mine = jnp.where(c == 0, left, right)
@@ -121,8 +176,8 @@
     chosen = of_seq == lax.broadcasted_iota(jnp.int32, (seqs, 1, tokens), 0)
     masked = jnp.where(chosen, act[None], jnp.zeros((), BF16))
     partial_blocks = contract_last(masked, grads)
-    pieces = partial_blocks.reshape(seqs, 8, 8, -1).swapaxes(0, 1)
-    blocks = all_to_all(pieces, "seq").sum(0)
+    pieces = partial_blocks.astype(BF16).reshape(seqs, 8, 8, -1).swapaxes(0, 1)
+    blocks = all_to_all(pieces, "seq").astype(F32).sum(0)
     squared = jnp.sum(blocks * blocks, axis=0)
     near, far = to_core_of_dp(squared)
     return (near + far) / (2 * seqs * 8 * length)

time: 151 us -> 140 us (0.927)
  Pallas kernels: 0 us -> 12.1 us
  starting transfers between devices: 76.6 us -> 66.3 us
  matrix products: 10.2 us -> 0.53 us
  blocking collectives: 19.6 us -> 13.2 us
  waiting for transfers between devices: 34.7 us -> 38.9 us
  other arithmetic: 3.53 us -> 1.57 us
  local copies, waits for them, and re-layouts: 4.41 us -> 6.21 us
    pallas_call x0 -> x3, Pallas kernels: none -> 12.1 us  [the longest x1 5.6 us: projected_parts(): pl.pallas_call(early_kernel, grid=(tokens // lanes,), in_specs=[whole, wh...]
    all_to_all x4, waiting for transfers between devices: 16 us -> 25.7 us  [all_to_all(): return lax.all_to_all(v, axis, 0, 0, tiled=True)]
    dot_general x7 -> x1, matrix products: 9.96 us -> 0.32 us  [contract_last(): lax.dot_general(a, b, (((a.ndim - 1,), (b.ndim - 1,)), ((), ())), preferr...]
    all_to_all x4, starting transfers between devices: 31.4 us -> 23.9 us  [all_to_all(): return lax.all_to_all(v, axis, 0, 0, tiled=True)]
    ppermute x4, waiting for transfers between devices: 13.9 us -> 6.54 us  [ring_step(): return lax.ppermute(v, ('seq', 'c'), pairs)]
    all_to_all x1, blocking collectives: 19.6 us -> 13.2 us  [all_to_all(): return lax.all_to_all(v, axis, 0, 0, tiled=True)]
    ppermute x4, starting transfers between devices: 14.2 us -> 11.3 us  [ring_step(): return lax.ppermute(v, ('seq', 'c'), pairs)]
    unnamed x17 -> x19, local copies, waits for them, and re-layouts: 1.33 us -> 3.97 us
  transfers between devices with their start and end apart: 17 -> 17, of which waited for: 7 -> 8; matrix products, arithmetic and copies ran while one was open for 11% -> 2% of each run, Pallas kernels for 0% -> 9%
where the time goes in v1:
time: 140 us; the launch traced here: 139 us
  starting transfers between devices  66.3 us (47%)
  waiting for transfers between devices  38.9 us (28%)
  blocking collectives  13.2 us (9%)
  Pallas kernels  12.1 us (9%)
  local copies, waits for them, and re-layouts  6.21 us (4%)
  other arithmetic  1.57 us (1%)
    all_to_all x4, waiting for transfers between devices, all_to_all(): return lax.all_to_all(v, axis, 0, 0, tiled=True)  25.7 us
    all_to_all x4, starting transfers between devices, all_to_all(): return lax.all_to_all(v, axis, 0, 0, tiled=True)  23.9 us
    ppermute x5, starting transfers between devices, exchange(): return lax.ppermute(v, axis, [(0, 1), (1, 0)])  17.7 us
    all_to_all x1, blocking collectives, all_to_all(): return lax.all_to_all(v, axis, 0, 0, tiled=True)  13.2 us
    ppermute x4, starting transfers between devices, ring_step(): return lax.ppermute(v, ('seq', 'c'), pairs)  11.3 us
    ppermute x2, starting transfers between devices, to_core_of_dp(): lax.ppermute(v, ('dp', 'c'), [(d * 2 + c, c * 2 + d) for d in (0, 1) for...  9.56 us
    ppermute x4, waiting for transfers between devices, ring_step(): return lax.ppermute(v, ('seq', 'c'), pairs)  6.54 us
    pallas_call x1, Pallas kernels, projected_parts(): pl.pallas_call(early_kernel, grid=(tokens // lanes,), in_specs=[whole, wh...  5.6 us
  transfers between devices with their start and end apart: 17, of which 8 were waited for; matrix products, arithmetic and copies ran while one was open for 2% of the time, Pallas kernels for 9%

profile of v1, /device:TPU:1, one launch (start us, length us, event | category | flops | bytes accessed | tf_op | source)
XLA Modules:
  0.0 139.2 jit_solution(516862965225584360)
XLA Ops:
  0.0 1.3 copy.11
  1.4 8.9 %collective-permute-start = (bf16[128,896]{1,0:T(8,128)(2,1)S(1)}, bf16[128,896]{1,0:T(8,128)(2,1)S(1)}, u32[]{:S(2)}, u32[]{:S(2)}) collective-permute-start(bf16[128,896]{1,0:T(8,128)(2,1)S(1)} %dynamic-slice_bitcast_fusion), channel_id=1, source_target_pairs={{0,1},{1,0},{2,3},{3,2},{4,5},{5,4},{6,7},{7,6},{8,9},{9,8},{10,11... | collective-permute-start | bytes 688136 | tf_op jit(solution)/shard_map/ppermute | solution.py:19
  11.1 3.4 %all-to-all-start.1 = ((bf16[16,48,256]{2,1,0:T(8,128)(2,1)}), bf16[16,48,256]{2,1,0:T(8,128)(2,1)S(1)}, u32[]{:S(2)}, u32[]{:S(2)}) async-start(bf16[16,48,256]{2,1,0:T(8,128)(2,1)} %bitcast.8), calls=%async_computation.1 | async-start | bytes 786432 | tf_op jit(solution)/shard_map/all_to_all | solution.py:23
  14.5 3.1 %collective-permute-start.5 = (bf16[384,896]{1,0:T(8,128)(2,1)S(1)}, bf16[384,896]{1,0:T(8,128)(2,1)S(1)}, u32[]{:S(2)}, u32[]{:S(2)}) collective-permute-start(bf16[384,896]{1,0:T(8,128)(2,1)S(1)} %bitcast.34), channel_id=1, source_target_pairs={{0,256},{256,0},{1,257},{257,1},{2,258},{258,2},{3,259},{259,3},{4... | collective-permute-start | bytes 2064392 | tf_op jit(solution)/shard_map/ppermute | solution.py:19
  17.7 4.5 %collective-permute-start.1 = (bf16[128,1792]{1,0:T(8,128)(2,1)S(1)}, bf16[128,1792]{1,0:T(8,128)(2,1)}, u32[]{:S(2)}, u32[]{:S(2)}) collective-permute-start(bf16[128,1792]{1,0:T(8,128)(2,1)S(1)} %pad_maximum_fusion.own), channel_id=1, source_target_pairs={{0,32},{1,225},{32,64},{33,1},{64,96},{65,33},{96,128},{97,65},{12... | collective-permute-start | bytes 1376264 | tf_op jit(solution)/shard_map/ppermute | solution.py:108
  22.2 1.9 %collective-permute-start.8 = (bf16[384,256]{1,0:T(8,128)(2,1)S(1)}, bf16[384,256]{1,0:T(8,128)(2,1)S(1)}, u32[]{:S(2)}, u32[]{:S(2)}) collective-permute-start(bf16[384,256]{1,0:T(8,128)(2,1)S(1)} %bitcast.43), channel_id=1, source_target_pairs={{0,1},{1,0},{2,3},{3,2},{4,5},{5,4},{6,7},{7,6},{8,9},{9,8},{10,11... | collective-permute-start | bytes 589832 | tf_op jit(solution)/shard_map/ppermute | solution.py:19
  24.1 1.4 %collective-permute-done.8.other = bf16[384,256]{1,0:T(8,128)(2,1)S(1)} collective-permute-done((bf16[384,256]{1,0:T(8,128)(2,1)S(1)}, bf16[384,256]{1,0:T(8,128)(2,1)S(1)}, u32[]{:S(2)}, u32[]{:S(2)}) %collective-permute-start.8) | collective-permute-done | bytes 196640 | tf_op jit(solution)/shard_map/ppermute | solution.py:19
  25.5 3.4 %all-to-all-done.1 = bf16[16,48,256]{2,1,0:T(8,128)(2,1)S(1)} async-done(((bf16[16,48,256]{2,1,0:T(8,128)(2,1)}), bf16[16,48,256]{2,1,0:T(8,128)(2,1)S(1)}, u32[]{:S(2)}, u32[]{:S(2)}) %all-to-all-start.1) | async-done | bytes 393248 | tf_op jit(solution)/shard_map/all_to_all | solution.py:23
  29.7 2.4 %shard_map.48 = f32[384,384]{1,0:T(8,128)} custom-call(s32[1]{0:T(128)} %bitcast.core, bf16[8,2,48,256]{3,2,1,0:T(8,128)(2,1)} %bitcast.31, bf16[384,256]{1,0:T(8,128)(2,1)} %bitcast.42, bf16[384,256]{1,0:T(8,128)(2,1)} %copy-done.7), custom_call_target="tpu_custom_call" | custom-call | tf_op jit(solution)/shard_map/pallas_call | solution.py:146
  32.1 9.6 %all-to-all-start.2 = ((f32[16,24,384]{2,1,0:T(8,128)}), f32[16,24,384]{2,1,0:T(8,128)S(1)}, u32[]{:S(2)}, u32[]{:S(2)}) async-start(f32[16,24,384]{2,1,0:T(8,128)} %bitcast.29), calls=%async_computation.2 | async-start | bytes 1179648 | tf_op jit(solution)/shard_map/all_to_all | solution.py:23
  41.7 1.9 %collective-permute-start.2 = (bf16[128,1792]{1,0:T(8,128)(2,1)}, bf16[128,1792]{1,0:T(8,128)(2,1)}, u32[]{:S(2)}, u32[]{:S(2)}) collective-permute-start(bf16[128,1792]{1,0:T(8,128)(2,1)} %collective-permute-done.1.one), channel_id=1, source_target_pairs={{0,32},{1,225},{32,64},{33,1},{64,96},{65,33},{96,128},{97,65},{12... | collective-permute-start | bytes 1376264 | tf_op jit(solution)/shard_map/ppermute | solution.py:108
  44.1 1.9 %collective-permute-start.6 = (bf16[768,896]{1,0:T(8,128)(2,1)S(1)}, bf16[768,896]{1,0:T(8,128)(2,1)S(1)}, u32[]{:S(2)}, u32[]{:S(2)}) collective-permute-start(bf16[768,896]{1,0:T(8,128)(2,1)S(1)} %maximum_select_fusion.here), channel_id=1, source_target_pairs={{0,1},{1,0},{2,3},{3,2},{4,5},{5,4},{6,7},{7,6},{8,9},{9,8},{10,11... | collective-permute-start | bytes 4128776 | tf_op jit(solution)/shard_map/ppermute | solution.py:19
  46.1 5.4 %collective-permute-done.2.two = bf16[128,1792]{1,0:T(8,128)(2,1)} collective-permute-done((bf16[128,1792]{1,0:T(8,128)(2,1)}, bf16[128,1792]{1,0:T(8,128)(2,1)}, u32[]{:S(2)}, u32[]{:S(2)}) %collective-permute-start.2) | collective-permute-done | bytes 458784 | tf_op jit(solution)/shard_map/ppermute | solution.py:108
  51.5 3.0 %collective-permute-start.3 = (bf16[128,1792]{1,0:T(8,128)(2,1)}, bf16[128,1792]{1,0:T(8,128)(2,1)}, u32[]{:S(2)}, u32[]{:S(2)}) collective-permute-start(bf16[128,1792]{1,0:T(8,128)(2,1)} %collective-permute-done.2.two), channel_id=1, source_target_pairs={{0,32},{1,225},{32,64},{33,1},{64,96},{65,33},{96,128},{97,65},{12... | collective-permute-start | bytes 1376264 | tf_op jit(solution)/shard_map/ppermute | solution.py:108
  54.5 5.4 %all-to-all-done.2 = f32[16,24,384]{2,1,0:T(8,128)S(1)} async-done(((f32[16,24,384]{2,1,0:T(8,128)}), f32[16,24,384]{2,1,0:T(8,128)S(1)}, u32[]{:S(2)}, u32[]{:S(2)}) %all-to-all-start.2) | async-done | bytes 589856 | tf_op jit(solution)/shard_map/all_to_all | solution.py:23
  60.8 3.6 %all-to-all-start.3 = ((bf16[16,24,384]{2,1,0:T(8,128)(2,1)}), bf16[16,24,384]{2,1,0:T(8,128)(2,1)S(1)}, u32[]{:S(2)}, u32[]{:S(2)}) async-start(bf16[16,24,384]{2,1,0:T(8,128)(2,1)} %broadcast_in_dim.39), calls=%async_computation.3 | async-start | bytes 589824 | tf_op jit(solution)/shard_map/all_to_all | solution.py:23
  64.4 1.9 %collective-permute-start.4 = (bf16[128,1792]{1,0:T(8,128)(2,1)}, bf16[128,1792]{1,0:T(8,128)(2,1)S(1)}, u32[]{:S(2)}, u32[]{:S(2)}) collective-permute-start(bf16[128,1792]{1,0:T(8,128)(2,1)} %collective-permute-done.3.three), channel_id=1, source_target_pairs={{1,225},{33,1},{65,33},{97,65},{129,97},{161,129},{193,161},{225,1... | collective-permute-start | bytes 1376264 | tf_op jit(solution)/shard_map/ppermute | solution.py:108
  66.3 1.1 copy-done.1
  67.4 5.6 %shard_map.46.filled = bf16[16,4,8,768]{3,2,1,0:T(8,128)(2,1)} custom-call(bf16[128,1792]{1,0:T(8,128)(2,1)} %collective-permute-done.1.one, bf16[128,1792]{1,0:T(8,128)(2,1)} %collective-permute-done.2.two, bf16[128,1792]{1,0:T(8,128)(2,1)} %collective-permute-done.3.three, bf16[768,896]{1,0:T(8,128)(2,1)} %copy-done, bf16[768,896]{1,0:T(8,128)(2,1)} %copy-done.1), custom_call_target="tpu_custom_call" | custom-call | tf_op jit(solution)/shard_map/pallas_call | solution.py:81
  73.0 1.1 collective-permute-done.4.far
  74.1 0.8 copy-done.5
  74.9 4.2 %shard_map.47 = bf16[16,4,8,768]{3,2,1,0:T(8,128)(2,1)} custom-call(s32[1]{0:T(128)} %bitcast.core, bf16[128,1792]{1,0:T(8,128)(2,1)} %copy-done.2, bf16[128,1792]{1,0:T(8,128)(2,1)} %copy-done.5, bf16[768,896]{1,0:T(8,128)(2,1)} %copy-done, bf16[768,896]{1,0:T(8,128)(2,1)} %copy-done.1, ...), custom_call_target="tpu_custom_call", output_to_operand_aliasing={{}: (5, {})} | custom-call | tf_op jit(solution)/shard_map/pallas_call | solution.py:88
  79.0 7.3 %all-to-all-start = ((bf16[16,4,8,768]{3,2,1,0:T(8,128)(2,1)}), bf16[16,4,8,768]{3,2,1,0:T(8,128)(2,1)S(1)}, u32[]{:S(2)}, u32[]{:S(2)}) async-start(bf16[16,4,8,768]{3,2,1,0:T(8,128)(2,1)} %shard_map.47), calls=%async_computation | async-start | bytes 1572864 | tf_op jit(solution)/shard_map/all_to_all | solution.py:23
  87.0 3.5 %collective-permute-start.9 = (bf16[8,48,384]{2,1,0:T(8,128)(2,1)S(1)}, bf16[8,48,384]{2,1,0:T(8,128)(2,1)S(1)}, u32[]{:S(2)}, u32[]{:S(2)}) collective-permute-start(bf16[8,48,384]{2,1,0:T(8,128)(2,1)S(1)} %bitcast.38), channel_id=1, source_target_pairs={{0,0},{1,256},{256,1},{257,257},{2,2},{3,258},{258,3},{259,259},{4... | collective-permute-start | bytes 884744 | tf_op jit(solution)/shard_map/ppermute | solution.py:112
  90.5 1.9 %collective-permute-start.10 = (bf16[8,48,384]{2,1,0:T(8,128)(2,1)S(1)}, bf16[8,48,384]{2,1,0:T(8,128)(2,1)S(1)}, u32[]{:S(2)}, u32[]{:S(2)}) collective-permute-start(bf16[8,48,384]{2,1,0:T(8,128)(2,1)S(1)} %bitcast.39), channel_id=1, source_target_pairs={{0,256},{1,0},{256,257},{257,1},{2,258},{3,2},{258,259},{259,3},{4... | collective-permute-start | bytes 884744 | tf_op jit(solution)/shard_map/ppermute | solution.py:113
  92.6 16.8 %all-to-all-done = bf16[16,4,8,768]{3,2,1,0:T(8,128)(2,1)S(1)} async-done(((bf16[16,4,8,768]{3,2,1,0:T(8,128)(2,1)}), bf16[16,4,8,768]{3,2,1,0:T(8,128)(2,1)S(1)}, u32[]{:S(2)}, u32[]{:S(2)}) %all-to-all-start) | async-done | bytes 786464 | tf_op jit(solution)/shard_map/all_to_all | solution.py:23
  109.5 1.9 %collective-permute-start.7 = (bf16[32,384]{1,0:T(8,128)(2,1)S(1)}, bf16[32,384]{1,0:T(8,128)(2,1)S(1)}, u32[]{:S(2)}, u32[]{:S(2)}) collective-permute-start(bf16[32,384]{1,0:T(8,128)(2,1)S(1)} %broadcast_select_fusion.2), channel_id=1, source_target_pairs={{0,1},{1,0},{2,3},{3,2},{4,5},{5,4},{6,7},{7,6},{8,9},{9,8},{10,11... | collective-permute-start | bytes 73736 | tf_op jit(solution)/shard_map/ppermute | solution.py:19
  111.6 1.1 collective-permute-done.7
  113.2 13.2 %all_to_all.25 = bf16[8,2,8,768]{3,2,1,0:T(8,128)(2,1)S(1)} all-to-all(bf16[8,2,8,768]{3,2,1,0:T(8,128)(2,1)S(1)} %bitcast.33), channel_id=1, replica_groups=mesh['dp'=2,'seq'=8,'z'=8,'x'=2,'c'=2] {'seq'}, dimensions={0} | all-to-all | bytes 393216 | tf_op jit(solution)/shard_map/all_to_all | solution.py:23
  126.4 6.1 %collective-permute-start.11 = (f32[8,768]{1,0:T(8,128)S(1)}, f32[8,768]{1,0:T(8,128)S(1)}, u32[]{:S(2)}, u32[]{:S(2)}) collective-permute-start(f32[8,768]{1,0:T(8,128)S(1)} %multiply_reduce_fusion), channel_id=1, source_target_pairs={{0,0},{1,256},{256,1},{257,257},{2,2},{3,258},{258,3},{259,259},{4... | collective-permute-start | bytes 73736 | tf_op jit(solution)/shard_map/ppermute | solution.py:112
  132.5 1.9 %collective-permute-start.12 = (f32[8,768]{1,0:T(8,128)S(1)}, f32[8,768]{1,0:T(8,128)S(1)}, u32[]{:S(2)}, u32[]{:S(2)}) collective-permute-start(f32[8,768]{1,0:T(8,128)S(1)} %multiply_reduce_fusion), channel_id=1, source_target_pairs={{0,256},{1,0},{256,257},{257,1},{2,258},{3,2},{258,259},{259,3},{4... | collective-permute-start | bytes 73736 | tf_op jit(solution)/shard_map/ppermute | solution.py:113
  134.5 4.1 %collective-permute-done.12 = f32[8,768]{1,0:T(8,128)S(1)} collective-permute-done((f32[8,768]{1,0:T(8,128)S(1)}, f32[8,768]{1,0:T(8,128)S(1)}, u32[]{:S(2)}, u32[]{:S(2)}) %collective-permute-start.12) | collective-permute-done | bytes 24608 | tf_op jit(solution)/shard_map/ppermute | solution.py:113
  (60 shorter events, 5.1 us)
Async XLA Ops:
  0.0 10.3 %copy-start.8 = (bf16[256,96]{0,1:T(8,128)(2,1)S(1)}, bf16[256,96]{0,1:T(8,128)(2,1)}, u32[]{:S(2)}) copy-start(bf16[256,96]{0,1:T(8,128)(2,1)} %param.7) | copy-start | bytes 147460
  0.0 14.5 %copy-start.4 = (bf16[2,192,896]{2,1,0:T(8,128)(2,1)S(1)}, bf16[2,192,896]{2,1,0:T(8,128)(2,1)}, u32[]{:S(2)}) copy-start(bf16[2,192,896]{2,1,0:T(8,128)(2,1)} %param.4) | copy-start | bytes 2064388
  1.3 20.8 %copy-start.6 = (bf16[2,192,256]{2,1,0:T(8,128)(2,1)S(1)}, bf16[2,192,256]{2,1,0:T(8,128)(2,1)}, u32[]{:S(2)}) copy-start(bf16[2,192,256]{2,1,0:T(8,128)(2,1)} %param.5) | copy-start | bytes 589828
  1.4 16.2 %collective-permute-start = (bf16[128,896]{1,0:T(8,128)(2,1)S(1)}, bf16[128,896]{1,0:T(8,128)(2,1)S(1)}, u32[]{:S(2)}, u32[]{:S(2)}) collective-permute-start(bf16[128,896]{1,0:T(8,128)(2,1)S(1)} %dynamic-slice_bitcast_fusion), channel_id=1, source_target_pairs={{0,1},{1,0},{2,3},{3,2},{4,5},{5,4},{6,7},{7,6},{8,9},{9,8},{10,11... | collective-permute-start | bytes 688136 | tf_op jit(solution)/shard_map/ppermute | solution.py:19
  11.1 17.9 %all-to-all-start.1 = ((bf16[16,48,256]{2,1,0:T(8,128)(2,1)}), bf16[16,48,256]{2,1,0:T(8,128)(2,1)S(1)}, u32[]{:S(2)}, u32[]{:S(2)}) async-start(bf16[16,48,256]{2,1,0:T(8,128)(2,1)} %bitcast.8), calls=%async_computation.1 | async-start | bytes 786432 | tf_op jit(solution)/shard_map/all_to_all | solution.py:23
  14.5 29.1 %collective-permute-start.5 = (bf16[384,896]{1,0:T(8,128)(2,1)S(1)}, bf16[384,896]{1,0:T(8,128)(2,1)S(1)}, u32[]{:S(2)}, u32[]{:S(2)}) collective-permute-start(bf16[384,896]{1,0:T(8,128)(2,1)S(1)} %bitcast.34), channel_id=1, source_target_pairs={{0,256},{256,0},{1,257},{257,1},{2,258},{258,2},{3,259},{259,3},{4... | collective-permute-start | bytes 2064392 | tf_op jit(solution)/shard_map/ppermute | solution.py:19
  17.7 25.9 %copy-start.2 = (bf16[128,1792]{1,0:T(8,128)(2,1)}, bf16[128,1792]{1,0:T(8,128)(2,1)S(1)}, u32[]{:S(2)}) copy-start(bf16[128,1792]{1,0:T(8,128)(2,1)S(1)} %pad_maximum_fusion.own) | copy-start | bytes 1376260
  17.7 24.0 %collective-permute-start.1 = (bf16[128,1792]{1,0:T(8,128)(2,1)S(1)}, bf16[128,1792]{1,0:T(8,128)(2,1)}, u32[]{:S(2)}, u32[]{:S(2)}) collective-permute-start(bf16[128,1792]{1,0:T(8,128)(2,1)S(1)} %pad_maximum_fusion.own), channel_id=1, source_target_pairs={{0,32},{1,225},{32,64},{33,1},{64,96},{65,33},{96,128},{97,65},{12... | collective-permute-start | bytes 1376264 | tf_op jit(solution)/shard_map/ppermute | solution.py:108
  22.2 3.3 %collective-permute-start.8 = (bf16[384,256]{1,0:T(8,128)(2,1)S(1)}, bf16[384,256]{1,0:T(8,128)(2,1)S(1)}, u32[]{:S(2)}, u32[]{:S(2)}) collective-permute-start(bf16[384,256]{1,0:T(8,128)(2,1)S(1)} %bitcast.43), channel_id=1, source_target_pairs={{0,1},{1,0},{2,3},{3,2},{4,5},{5,4},{6,7},{7,6},{8,9},{9,8},{10,11... | collective-permute-start | bytes 589832 | tf_op jit(solution)/shard_map/ppermute | solution.py:19
  25.5 3.4 %copy-start.7 = (bf16[384,256]{1,0:T(8,128)(2,1)}, bf16[384,256]{1,0:T(8,128)(2,1)S(1)}, u32[]{:S(2)}) copy-start(bf16[384,256]{1,0:T(8,128)(2,1)S(1)} %collective-permute-done.8.other) | copy-start | bytes 589828
  28.9 0.8 copy-start.3
  32.1 27.9 %all-to-all-start.2 = ((f32[16,24,384]{2,1,0:T(8,128)}), f32[16,24,384]{2,1,0:T(8,128)S(1)}, u32[]{:S(2)}, u32[]{:S(2)}) async-start(f32[16,24,384]{2,1,0:T(8,128)} %bitcast.29), calls=%async_computation.2 | async-start | bytes 1179648 | tf_op jit(solution)/shard_map/all_to_all | solution.py:23
  41.7 9.8 %collective-permute-start.2 = (bf16[128,1792]{1,0:T(8,128)(2,1)}, bf16[128,1792]{1,0:T(8,128)(2,1)}, u32[]{:S(2)}, u32[]{:S(2)}) collective-permute-start(bf16[128,1792]{1,0:T(8,128)(2,1)} %collective-permute-done.1.one), channel_id=1, source_target_pairs={{0,32},{1,225},{32,64},{33,1},{64,96},{65,33},{96,128},{97,65},{12... | collective-permute-start | bytes 1376264 | tf_op jit(solution)/shard_map/ppermute | solution.py:108
  44.1 22.2 %copy-start = (bf16[768,896]{1,0:T(8,128)(2,1)}, bf16[768,896]{1,0:T(8,128)(2,1)S(1)}, u32[]{:S(2)}) copy-start(bf16[768,896]{1,0:T(8,128)(2,1)S(1)} %maximum_select_fusion.here) | copy-start | bytes 4128772
  44.1 22.2 %collective-permute-start.6 = (bf16[768,896]{1,0:T(8,128)(2,1)S(1)}, bf16[768,896]{1,0:T(8,128)(2,1)S(1)}, u32[]{:S(2)}, u32[]{:S(2)}) collective-permute-start(bf16[768,896]{1,0:T(8,128)(2,1)S(1)} %maximum_select_fusion.here), channel_id=1, source_target_pairs={{0,1},{1,0},{2,3},{3,2},{4,5},{5,4},{6,7},{7,6},{8,9},{9,8},{10,11... | collective-permute-start | bytes 4128776 | tf_op jit(solution)/shard_map/ppermute | solution.py:19
  51.5 12.9 %collective-permute-start.3 = (bf16[128,1792]{1,0:T(8,128)(2,1)}, bf16[128,1792]{1,0:T(8,128)(2,1)}, u32[]{:S(2)}, u32[]{:S(2)}) collective-permute-start(bf16[128,1792]{1,0:T(8,128)(2,1)} %collective-permute-done.2.two), channel_id=1, source_target_pairs={{0,32},{1,225},{32,64},{33,1},{64,96},{65,33},{96,128},{97,65},{12... | collective-permute-start | bytes 1376264 | tf_op jit(solution)/shard_map/ppermute | solution.py:108
  60.8 18.3 %all-to-all-start.3 = ((bf16[16,24,384]{2,1,0:T(8,128)(2,1)}), bf16[16,24,384]{2,1,0:T(8,128)(2,1)S(1)}, u32[]{:S(2)}, u32[]{:S(2)}) async-start(bf16[16,24,384]{2,1,0:T(8,128)(2,1)} %broadcast_in_dim.39), calls=%async_computation.3 | async-start | bytes 589824 | tf_op jit(solution)/shard_map/all_to_all | solution.py:23
  64.4 9.7 %collective-permute-start.4 = (bf16[128,1792]{1,0:T(8,128)(2,1)}, bf16[128,1792]{1,0:T(8,128)(2,1)S(1)}, u32[]{:S(2)}, u32[]{:S(2)}) collective-permute-start(bf16[128,1792]{1,0:T(8,128)(2,1)} %collective-permute-done.3.three), channel_id=1, source_target_pairs={{1,225},{33,1},{65,33},{97,65},{129,97},{161,129},{193,161},{225,1... | collective-permute-start | bytes 1376264 | tf_op jit(solution)/shard_map/ppermute | solution.py:108
  66.3 1.1 copy-start.1
  74.1 0.8 copy-start.5
  79.0 30.4 %all-to-all-start = ((bf16[16,4,8,768]{3,2,1,0:T(8,128)(2,1)}), bf16[16,4,8,768]{3,2,1,0:T(8,128)(2,1)S(1)}, u32[]{:S(2)}, u32[]{:S(2)}) async-start(bf16[16,4,8,768]{3,2,1,0:T(8,128)(2,1)} %shard_map.47), calls=%async_computation | async-start | bytes 1572864 | tf_op jit(solution)/shard_map/all_to_all | solution.py:23
  87.0 24.5 %collective-permute-start.9 = (bf16[8,48,384]{2,1,0:T(8,128)(2,1)S(1)}, bf16[8,48,384]{2,1,0:T(8,128)(2,1)S(1)}, u32[]{:S(2)}, u32[]{:S(2)}) collective-permute-start(bf16[8,48,384]{2,1,0:T(8,128)(2,1)S(1)} %bitcast.38), channel_id=1, source_target_pairs={{0,0},{1,256},{256,1},{257,257},{2,2},{3,258},{258,3},{259,259},{4... | collective-permute-start | bytes 884744 | tf_op jit(solution)/shard_map/ppermute | solution.py:112
  90.5 21.0 %collective-permute-start.10 = (bf16[8,48,384]{2,1,0:T(8,128)(2,1)S(1)}, bf16[8,48,384]{2,1,0:T(8,128)(2,1)S(1)}, u32[]{:S(2)}, u32[]{:S(2)}) collective-permute-start(bf16[8,48,384]{2,1,0:T(8,128)(2,1)S(1)} %bitcast.39), channel_id=1, source_target_pairs={{0,256},{1,0},{256,257},{257,1},{2,258},{3,2},{258,259},{259,3},{4... | collective-permute-start | bytes 884744 | tf_op jit(solution)/shard_map/ppermute | solution.py:113
  109.5 3.1 %collective-permute-start.7 = (bf16[32,384]{1,0:T(8,128)(2,1)S(1)}, bf16[32,384]{1,0:T(8,128)(2,1)S(1)}, u32[]{:S(2)}, u32[]{:S(2)}) collective-permute-start(bf16[32,384]{1,0:T(8,128)(2,1)S(1)} %broadcast_select_fusion.2), channel_id=1, source_target_pairs={{0,1},{1,0},{2,3},{3,2},{4,5},{5,4},{6,7},{7,6},{8,9},{9,8},{10,11... | collective-permute-start | bytes 73736 | tf_op jit(solution)/shard_map/ppermute | solution.py:19
  126.4 8.0 %collective-permute-start.11 = (f32[8,768]{1,0:T(8,128)S(1)}, f32[8,768]{1,0:T(8,128)S(1)}, u32[]{:S(2)}, u32[]{:S(2)}) collective-permute-start(f32[8,768]{1,0:T(8,128)S(1)} %multiply_reduce_fusion), channel_id=1, source_target_pairs={{0,0},{1,256},{256,1},{257,257},{2,2},{3,258},{258,3},{259,259},{4... | collective-permute-start | bytes 73736 | tf_op jit(solution)/shard_map/ppermute | solution.py:112
  132.5 6.1 %collective-permute-start.12 = (f32[8,768]{1,0:T(8,128)S(1)}, f32[8,768]{1,0:T(8,128)S(1)}, u32[]{:S(2)}, u32[]{:S(2)}) collective-permute-start(f32[8,768]{1,0:T(8,128)S(1)} %multiply_reduce_fusion), channel_id=1, source_target_pairs={{0,256},{1,0},{256,257},{257,1},{2,258},{3,2},{258,259},{259,3},{4... | collective-permute-start | bytes 73736 | tf_op jit(solution)/shard_map/ppermute | solution.py:113

commit v2 on v1

--- a/solution.py
+++ b/solution.py
@@ -23,10 +23,6 @@
     return lax.all_to_all(v, axis, 0, 0, tiled=True)
 
 
-def to_everyone(v, axis):
-    return all_to_all(jnp.broadcast_to(v[None], (lax.axis_size(axis), *v.shape)), axis)
-
-
 def contract_last(a, b):
     return lax.dot_general(
         a, b, (((a.ndim - 1,), (b.ndim - 1,)), ((), ())), preferred_element_type=F32
@@ -50,26 +46,26 @@
     rows = cols.shape[0] * cols.shape[2]
     first = jnp.where(lower, own[...], other[...])
     second = jnp.where(lower, other[...], own[...])
-    out[...] = contract_last(cols[:, 0].reshape(rows, -1), first) + contract_last(
-        cols[:, 1].reshape(rows, -1), second
-    )
+    found = contract_last(cols[:, 0].reshape(rows, -1), first)
+    found = found + contract_last(cols[:, 1].reshape(rows, -1), second)
+    out[...] = found.astype(BF16)
+
+
+def product(block, here, there):
+    width = here.shape[1]
+    found = contract_last(here[...], block[:, :width])
+    found = found + contract_last(there[...], block[:, width:])
+    return found.T.reshape(16, 8, -1).astype(BF16)
 
 
 def early_kernel(one, two, three, here, there, out):
-    width = here.shape[1]
     for k, block in enumerate((one, two, three)):
-        found = contract_last(block[:, :width], here[...])
-        found = found + contract_last(block[:, width:], there[...])
-        out[:, k] = found.reshape(16, 8, -1).astype(BF16)
+        out[:, k] = product(block[...], here, there)
 
 
 def last_kernel(core, own, far, here, there, filled, out):
     del filled
-    width = here.shape[1]
-    block = jnp.where(core[0] == 0, own[...], far[...])
-    found = contract_last(block[:, :width], here[...])
-    found = found + contract_last(block[:, width:], there[...])
-    out[:, 0] = found.reshape(16, 8, -1).astype(BF16)
+    out[:, 0] = product(jnp.where(core[0] == 0, own[...], far[...]), here, there)
 
 
 def projected_parts(c, block, steps, here, there):
@@ -106,6 +102,14 @@
     n = lax.axis_size("seq")
     pairs = [(y * 2 + k, (y + 1 - 2 * k) % n * 2 + k) for y in range(n) for k in cores]
     return lax.ppermute(v, ("seq", "c"), pairs)
+
+
+def doubled(v, axis, bit):
+    n = lax.axis_size(axis)
+    other = lax.ppermute(v, axis, [(i, i ^ bit) for i in range(n)])
+    low = lax.axis_index(axis) & bit == 0
+    both = jnp.where(low, jnp.stack([v, other], 1), jnp.stack([other, v], 1))
+    return both.reshape(-1, *v.shape[1:])
 
 
 def to_core_of_dp(v):
@@ -148,11 +152,13 @@
         in_specs=[pl.BlockSpec(memory_space=pltpu.SMEM)]
         + [pl.BlockSpec(memory_space=pltpu.VMEM)] * 3,
         out_specs=pl.BlockSpec(memory_space=pltpu.VMEM),
-        out_shape=jax.ShapeDtypeStruct((8 * out_cols.shape[2], tokens), F32),
+        out_shape=jax.ShapeDtypeStruct((8 * out_cols.shape[2], tokens), BF16),
     )(c.reshape(1), out_cols, g_own, g_other)
     grad_parts = all_to_all(grad_partial.reshape(16, -1, tokens), ("z", "x"))
-    grad_own = grad_parts.sum(0).astype(BF16)
-    grad_half = to_everyone(grad_own, ("z", "x")).reshape(8, -1, tokens)
+    grad_half = grad_parts.astype(F32).sum(0).astype(BF16)[None]
+    for axis, bit in (("z", 4), ("z", 2), ("z", 1), ("x", 1)):
+        grad_half = doubled(grad_half, axis, bit)
+    grad_half = grad_half.reshape(8, -1, tokens)
     near, far = to_core_of_dp(grad_half)
     grads = jnp.where(d == 0, jnp.stack([near, far], 1), jnp.stack([far, near], 1))
     grads = grads.reshape(-1, tokens)

time: 140 us -> 169 us (1.21)
  waiting for transfers between devices: 38.9 us -> 56.3 us
  starting transfers between devices: 66.3 us -> 78.1 us
    ppermute x0 -> x4, waiting for transfers between devices: none -> 26.2 us  [doubled(): other = lax.ppermute(v, axis, [(i, i ^ bit) for i in range(n)])]
    all_to_all x4 -> x3, waiting for transfers between devices: 25.7 us -> 6.48 us  [all_to_all(): return lax.all_to_all(v, axis, 0, 0, tiled=True)]
    ppermute x0 -> x4, starting transfers between devices: none -> 14.4 us  [doubled(): other = lax.ppermute(v, axis, [(i, i ^ bit) for i in range(n)])]
    ppermute x5, waiting for transfers between devices: 2.46 us -> 6.71 us  [exchange(): return lax.ppermute(v, axis, [(0, 1), (1, 0)])]
    ppermute x2, waiting for transfers between devices: 4.14 us -> 7.92 us  [to_core_of_dp(): lax.ppermute(v, ('dp', 'c'), [(d * 2 + c, (1 - c) * 2 + d) for d in (0, 1...]
    all_to_all x4 -> x3, starting transfers between devices: 23.9 us -> 20.3 us  [all_to_all(): return lax.all_to_all(v, axis, 0, 0, tiled=True)]
    ppermute x4, waiting for transfers between devices: 6.54 us -> 8.27 us  [ring_step(): return lax.ppermute(v, ('seq', 'c'), pairs)]
    unnamed x19 -> x17, local copies, waits for them, and re-layouts: 3.97 us -> 3.97 us
  transfers between devices with their start and end apart: 17 -> 20, of which waited for: 8 -> 12; matrix products, arithmetic and copies ran while one was open for 2% -> 1% of each run, Pallas kernels for 9% -> 7%
where the time goes in v2:
time: 169 us; the launch traced here: 168 us
  starting transfers between devices  78.1 us (46%)
  waiting for transfers between devices  56.3 us (33%)
  blocking collectives  13 us (8%)
  Pallas kernels  12 us (7%)
  local copies, waits for them, and re-layouts  5.45 us (3%)
  other arithmetic  1.74 us (1%)
    ppermute x4, waiting for transfers between devices, doubled(): other = lax.ppermute(v, axis, [(i, i ^ bit) for i in range(n)])  26.2 us
    all_to_all x3, starting transfers between devices, all_to_all(): return lax.all_to_all(v, axis, 0, 0, tiled=True)  20.3 us
    ppermute x5, starting transfers between devices, exchange(): return lax.ppermute(v, axis, [(0, 1), (1, 0)])  17.7 us
    ppermute x4, starting transfers between devices, doubled(): other = lax.ppermute(v, axis, [(i, i ^ bit) for i in range(n)])  14.4 us
    all_to_all x1, blocking collectives, all_to_all(): return lax.all_to_all(v, axis, 0, 0, tiled=True)  13 us
    ppermute x4, starting transfers between devices, ring_step(): return lax.ppermute(v, ('seq', 'c'), pairs)  12.4 us
    ppermute x2, starting transfers between devices, to_core_of_dp(): lax.ppermute(v, ('dp', 'c'), [(d * 2 + c, c * 2 + d) for d in (0, 1) for...  9.48 us
    ppermute x4, waiting for transfers between devices, ring_step(): return lax.ppermute(v, ('seq', 'c'), pairs)  8.27 us
  transfers between devices with their start and end apart: 20, of which 12 were waited for; matrix products, arithmetic and copies ran while one was open for 1% of the time, Pallas kernels for 7%

profile of v2, /device:TPU:1, one launch (start us, length us, event | category | flops | bytes accessed | tf_op | source)
XLA Modules:
  0.0 167.6 jit_solution(16622082344155571700)
XLA Ops:
  1.4 8.7 %collective-permute-start = (bf16[128,896]{1,0:T(8,128)(2,1)S(1)}, bf16[128,896]{1,0:T(8,128)(2,1)S(1)}, u32[]{:S(2)}, u32[]{:S(2)}) collective-permute-start(bf16[128,896]{1,0:T(8,128)(2,1)S(1)} %dynamic-slice_bitcast_fusion), channel_id=1, source_target_pairs={{0,1},{1,0},{2,3},{3,2},{4,5},{5,4},{6,7},{7,6},{8,9},{9,8},{10,11... | collective-permute-start | bytes 688136 | tf_op jit(solution)/shard_map/ppermute | solution.py:19
  10.1 1.9 %collective-permute-start.5 = (bf16[384,896]{1,0:T(8,128)(2,1)S(1)}, bf16[384,896]{1,0:T(8,128)(2,1)S(1)}, u32[]{:S(2)}, u32[]{:S(2)}) collective-permute-start(bf16[384,896]{1,0:T(8,128)(2,1)S(1)} %bitcast.44), channel_id=1, source_target_pairs={{0,256},{256,0},{1,257},{257,1},{2,258},{258,2},{3,259},{259,3},{4... | collective-permute-start | bytes 2064392 | tf_op jit(solution)/shard_map/ppermute | solution.py:19
  12.1 2.5 %collective-permute-start.1 = (bf16[128,1792]{1,0:T(8,128)(2,1)S(1)}, bf16[128,1792]{1,0:T(8,128)(2,1)}, u32[]{:S(2)}, u32[]{:S(2)}) collective-permute-start(bf16[128,1792]{1,0:T(8,128)(2,1)S(1)} %pad_maximum_fusion.own), channel_id=1, source_target_pairs={{0,32},{1,225},{32,64},{33,1},{64,96},{65,33},{96,128},{97,65},{12... | collective-permute-start | bytes 1376264 | tf_op jit(solution)/shard_map/ppermute | solution.py:104
  14.6 7.1 %collective-permute-done.1.one = bf16[128,1792]{1,0:T(8,128)(2,1)} collective-permute-done((bf16[128,1792]{1,0:T(8,128)(2,1)S(1)}, bf16[128,1792]{1,0:T(8,128)(2,1)}, u32[]{:S(2)}, u32[]{:S(2)}) %collective-permute-start.1) | collective-permute-done | bytes 458784 | tf_op jit(solution)/shard_map/ppermute | solution.py:104
  21.8 3.6 %collective-permute-start.2 = (bf16[128,1792]{1,0:T(8,128)(2,1)}, bf16[128,1792]{1,0:T(8,128)(2,1)}, u32[]{:S(2)}, u32[]{:S(2)}) collective-permute-start(bf16[128,1792]{1,0:T(8,128)(2,1)} %collective-permute-done.1.one), channel_id=1, source_target_pairs={{0,32},{1,225},{32,64},{33,1},{64,96},{65,33},{96,128},{97,65},{12... | collective-permute-start | bytes 1376264 | tf_op jit(solution)/shard_map/ppermute | solution.py:104
  25.3 5.2 %collective-permute-done.5 = bf16[384,896]{1,0:T(8,128)(2,1)S(1)} collective-permute-done((bf16[384,896]{1,0:T(8,128)(2,1)S(1)}, bf16[384,896]{1,0:T(8,128)(2,1)S(1)}, u32[]{:S(2)}, u32[]{:S(2)}) %collective-permute-start.5) | collective-permute-done | bytes 688160 | tf_op jit(solution)/shard_map/ppermute | solution.py:19
  31.0 2.8 %collective-permute-start.6 = (bf16[768,896]{1,0:T(8,128)(2,1)S(1)}, bf16[768,896]{1,0:T(8,128)(2,1)S(1)}, u32[]{:S(2)}, u32[]{:S(2)}) collective-permute-start(bf16[768,896]{1,0:T(8,128)(2,1)S(1)} %maximum_select_fusion.here), channel_id=1, source_target_pairs={{0,1},{1,0},{2,3},{3,2},{4,5},{5,4},{6,7},{7,6},{8,9},{9,8},{10,11... | collective-permute-start | bytes 4128776 | tf_op jit(solution)/shard_map/ppermute | solution.py:19
  34.6 3.4 %all-to-all-start.1 = ((bf16[16,48,256]{2,1,0:T(8,128)(2,1)}), bf16[16,48,256]{2,1,0:T(8,128)(2,1)S(1)}, u32[]{:S(2)}, u32[]{:S(2)}) async-start(bf16[16,48,256]{2,1,0:T(8,128)(2,1)} %bitcast.8), calls=%async_computation.1 | async-start | bytes 786432 | tf_op jit(solution)/shard_map/all_to_all | solution.py:23
  38.1 4.5 %collective-permute-start.3 = (bf16[128,1792]{1,0:T(8,128)(2,1)}, bf16[128,1792]{1,0:T(8,128)(2,1)}, u32[]{:S(2)}, u32[]{:S(2)}) collective-permute-start(bf16[128,1792]{1,0:T(8,128)(2,1)} %collective-permute-done.2.two), channel_id=1, source_target_pairs={{0,32},{1,225},{32,64},{33,1},{64,96},{65,33},{96,128},{97,65},{12... | collective-permute-start | bytes 1376264 | tf_op jit(solution)/shard_map/ppermute | solution.py:104
  42.5 1.9 %collective-permute-start.8 = (bf16[384,256]{1,0:T(8,128)(2,1)S(1)}, bf16[384,256]{1,0:T(8,128)(2,1)}, u32[]{:S(2)}, u32[]{:S(2)}) collective-permute-start(bf16[384,256]{1,0:T(8,128)(2,1)S(1)} %bitcast.57), channel_id=1, source_target_pairs={{0,1},{1,0},{2,3},{3,2},{4,5},{5,4},{6,7},{7,6},{8,9},{9,8},{10,11... | collective-permute-start | bytes 589832 | tf_op jit(solution)/shard_map/ppermute | solution.py:19
  46.0 6.5 %all-to-all-done.1 = bf16[16,48,256]{2,1,0:T(8,128)(2,1)S(1)} async-done(((bf16[16,48,256]{2,1,0:T(8,128)(2,1)}), bf16[16,48,256]{2,1,0:T(8,128)(2,1)S(1)}, u32[]{:S(2)}, u32[]{:S(2)}) %all-to-all-start.1) | async-done | bytes 393248 | tf_op jit(solution)/shard_map/all_to_all | solution.py:23
  53.2 2.3 %shard_map.48 = bf16[384,384]{1,0:T(8,128)(2,1)} custom-call(s32[1]{0:T(128)} %bitcast.core, bf16[8,2,48,256]{3,2,1,0:T(8,128)(2,1)} %bitcast.40, bf16[384,256]{1,0:T(8,128)(2,1)} %bitcast.56, bf16[384,256]{1,0:T(8,128)(2,1)} %collective-permute-done.8.other), custom_call_target="tpu_custom_call" | custom-call | tf_op jit(solution)/shard_map/pallas_call | solution.py:150
  55.5 9.6 %all-to-all-start.2 = ((bf16[16,24,384]{2,1,0:T(8,128)(2,1)}), bf16[16,24,384]{2,1,0:T(8,128)(2,1)S(1)}, u32[]{:S(2)}, u32[]{:S(2)}) async-start(bf16[16,24,384]{2,1,0:T(8,128)(2,1)} %bitcast.41), calls=%async_computation.2 | async-start | bytes 589824 | tf_op jit(solution)/shard_map/all_to_all | solution.py:23
  68.1 5.5 %shard_map.46.filled = bf16[16,4,8,768]{3,2,1,0:T(8,128)(2,1)} custom-call(bf16[128,1792]{1,0:T(8,128)(2,1)} %collective-permute-done.1.one, bf16[128,1792]{1,0:T(8,128)(2,1)} %collective-permute-done.2.two, bf16[128,1792]{1,0:T(8,128)(2,1)} %collective-permute-done.3.three, bf16[768,896]{1,0:T(8,128)(2,1)} %copy-done, bf16[768,896]{1,0:T(8,128)(2,1)} %copy-done.1), custom_call_target="tpu_custom_call" | custom-call | tf_op jit(solution)/shard_map/pallas_call | solution.py:77
  75.6 4.3 %shard_map.47 = bf16[16,4,8,768]{3,2,1,0:T(8,128)(2,1)} custom-call(s32[1]{0:T(128)} %bitcast.core, bf16[128,1792]{1,0:T(8,128)(2,1)} %copy-done.2, bf16[128,1792]{1,0:T(8,128)(2,1)} %copy-done.5, bf16[768,896]{1,0:T(8,128)(2,1)} %copy-done, bf16[768,896]{1,0:T(8,128)(2,1)} %copy-done.1, ...), custom_call_target="tpu_custom_call", output_to_operand_aliasing={{}: (5, {})} | custom-call | tf_op jit(solution)/shard_map/pallas_call | solution.py:84
  79.9 7.3 %all-to-all-start = ((bf16[16,4,8,768]{3,2,1,0:T(8,128)(2,1)}), bf16[16,4,8,768]{3,2,1,0:T(8,128)(2,1)S(1)}, u32[]{:S(2)}, u32[]{:S(2)}) async-start(bf16[16,4,8,768]{3,2,1,0:T(8,128)(2,1)} %shard_map.47), calls=%async_computation | async-start | bytes 1572864 | tf_op jit(solution)/shard_map/all_to_all | solution.py:23
  87.3 7.2 %collective-permute-start.9 = (bf16[1,24,384]{2,1,0:T(8,128)(2,1)S(1)}, bf16[1,24,384]{2,1,0:T(8,128)(2,1)S(1)}, u32[]{:S(2)}, u32[]{:S(2)}) collective-permute-start(bf16[1,24,384]{2,1,0:T(8,128)(2,1)S(1)} %bitcast.58), channel_id=1, source_target_pairs={{0,16},{4,20},{8,24},{12,28},{16,0},{20,4},{24,8},{28,12},{1,17},{... | collective-permute-start | bytes 55304 | tf_op jit(solution)/shard_map/ppermute | solution.py:109
  95.0 14.7 %collective-permute-done.9 = bf16[1,24,384]{2,1,0:T(8,128)(2,1)S(1)} collective-permute-done((bf16[1,24,384]{2,1,0:T(8,128)(2,1)S(1)}, bf16[1,24,384]{2,1,0:T(8,128)(2,1)S(1)}, u32[]{:S(2)}, u32[]{:S(2)}) %collective-permute-start.9) | collective-permute-done | bytes 18464 | tf_op jit(solution)/shard_map/ppermute | solution.py:109
  109.6 2.0 %collective-permute-start.10 = (bf16[2,24,384]{2,1,0:T(8,128)(2,1)S(1)}, bf16[2,24,384]{2,1,0:T(8,128)(2,1)S(1)}, u32[]{:S(2)}, u32[]{:S(2)}) collective-permute-start(bf16[2,24,384]{2,1,0:T(8,128)(2,1)S(1)} %maximum_select_fusion.6), channel_id=1, source_target_pairs={{0,8},{4,12},{8,0},{12,4},{16,24},{20,28},{24,16},{28,20},{1,9},{5... | collective-permute-start | bytes 110600 | tf_op jit(solution)/shard_map/ppermute | solution.py:109
  111.7 4.4 %collective-permute-done.10 = bf16[2,24,384]{2,1,0:T(8,128)(2,1)S(1)} collective-permute-done((bf16[2,24,384]{2,1,0:T(8,128)(2,1)S(1)}, bf16[2,24,384]{2,1,0:T(8,128)(2,1)S(1)}, u32[]{:S(2)}, u32[]{:S(2)}) %collective-permute-start.10) | collective-permute-done | bytes 36896 | tf_op jit(solution)/shard_map/ppermute | solution.py:109
  116.1 1.9 %collective-permute-start.11 = (bf16[4,24,384]{2,1,0:T(8,128)(2,1)S(1)}, bf16[4,24,384]{2,1,0:T(8,128)(2,1)S(1)}, u32[]{:S(2)}, u32[]{:S(2)}) collective-permute-start(bf16[4,24,384]{2,1,0:T(8,128)(2,1)S(1)} %bitcast.52), channel_id=1, source_target_pairs={{0,4},{4,0},{8,12},{12,8},{16,20},{20,16},{24,28},{28,24},{1,5},{5... | collective-permute-start | bytes 221192 | tf_op jit(solution)/shard_map/ppermute | solution.py:109
  118.0 3.5 %collective-permute-done.11 = bf16[4,24,384]{2,1,0:T(8,128)(2,1)S(1)} collective-permute-done((bf16[4,24,384]{2,1,0:T(8,128)(2,1)S(1)}, bf16[4,24,384]{2,1,0:T(8,128)(2,1)S(1)}, u32[]{:S(2)}, u32[]{:S(2)}) %collective-permute-start.11) | collective-permute-done | bytes 73760 | tf_op jit(solution)/shard_map/ppermute | solution.py:109
  121.6 3.3 %collective-permute-start.12 = (bf16[8,24,384]{2,1,0:T(8,128)(2,1)S(1)}, bf16[8,24,384]{2,1,0:T(8,128)(2,1)S(1)}, u32[]{:S(2)}, u32[]{:S(2)}) collective-permute-start(bf16[8,24,384]{2,1,0:T(8,128)(2,1)S(1)} %bitcast.46), channel_id=1, source_target_pairs={{0,2},{2,0},{1,3},{3,1},{4,6},{6,4},{5,7},{7,5},{8,10},{10,8},{9,1... | collective-permute-start | bytes 442376 | tf_op jit(solution)/shard_map/ppermute | solution.py:109
  124.9 3.7 %collective-permute-done.12 = bf16[8,24,384]{2,1,0:T(8,128)(2,1)S(1)} collective-permute-done((bf16[8,24,384]{2,1,0:T(8,128)(2,1)S(1)}, bf16[8,24,384]{2,1,0:T(8,128)(2,1)S(1)}, u32[]{:S(2)}, u32[]{:S(2)}) %collective-permute-start.12) | collective-permute-done | bytes 147488 | tf_op jit(solution)/shard_map/ppermute | solution.py:109
  128.7 5.4 %collective-permute-start.13 = (bf16[8,48,384]{2,1,0:T(8,128)(2,1)S(1)}, bf16[8,48,384]{2,1,0:T(8,128)(2,1)S(1)}, u32[]{:S(2)}, u32[]{:S(2)}) collective-permute-start(bf16[8,48,384]{2,1,0:T(8,128)(2,1)S(1)} %bitcast.50), channel_id=1, source_target_pairs={{0,0},{1,256},{256,1},{257,257},{2,2},{3,258},{258,3},{259,259},{4... | collective-permute-start | bytes 884744 | tf_op jit(solution)/shard_map/ppermute | solution.py:116
  134.1 1.9 %collective-permute-start.14 = (bf16[8,48,384]{2,1,0:T(8,128)(2,1)S(1)}, bf16[8,48,384]{2,1,0:T(8,128)(2,1)S(1)}, u32[]{:S(2)}, u32[]{:S(2)}) collective-permute-start(bf16[8,48,384]{2,1,0:T(8,128)(2,1)S(1)} %bitcast.51), channel_id=1, source_target_pairs={{0,256},{1,0},{256,257},{257,1},{2,258},{3,2},{258,259},{259,3},{4... | collective-permute-start | bytes 884744 | tf_op jit(solution)/shard_map/ppermute | solution.py:117
  136.3 2.3 %collective-permute-start.7 = (bf16[32,384]{1,0:T(8,128)(2,1)S(1)}, bf16[32,384]{1,0:T(8,128)(2,1)S(1)}, u32[]{:S(2)}, u32[]{:S(2)}) collective-permute-start(bf16[32,384]{1,0:T(8,128)(2,1)S(1)} %broadcast_select_fusion.2), channel_id=1, source_target_pairs={{0,1},{1,0},{2,3},{3,2},{4,5},{5,4},{6,7},{7,6},{8,9},{9,8},{10,11... | collective-permute-start | bytes 73736 | tf_op jit(solution)/shard_map/ppermute | solution.py:19
  138.7 4.4 %collective-permute-done.14 = bf16[8,48,384]{2,1,0:T(8,128)(2,1)S(1)} collective-permute-done((bf16[8,48,384]{2,1,0:T(8,128)(2,1)S(1)}, bf16[8,48,384]{2,1,0:T(8,128)(2,1)S(1)}, u32[]{:S(2)}, u32[]{:S(2)}) %collective-permute-start.14) | collective-permute-done | bytes 294944 | tf_op jit(solution)/shard_map/ppermute | solution.py:117
  143.7 13.0 %all_to_all.20 = bf16[8,2,8,768]{3,2,1,0:T(8,128)(2,1)S(1)} all-to-all(bf16[8,2,8,768]{3,2,1,0:T(8,128)(2,1)S(1)} %bitcast.43), channel_id=1, replica_groups=mesh['dp'=2,'seq'=8,'z'=8,'x'=2,'c'=2] {'seq'}, dimensions={0} | all-to-all | bytes 393216 | tf_op jit(solution)/shard_map/all_to_all | solution.py:23
  156.8 4.1 %collective-permute-start.15 = (f32[8,768]{1,0:T(8,128)S(1)}, f32[8,768]{1,0:T(8,128)S(1)}, u32[]{:S(2)}, u32[]{:S(2)}) collective-permute-start(f32[8,768]{1,0:T(8,128)S(1)} %multiply_reduce_fusion), channel_id=1, source_target_pairs={{0,0},{1,256},{256,1},{257,257},{2,2},{3,258},{258,3},{259,259},{4... | collective-permute-start | bytes 73736 | tf_op jit(solution)/shard_map/ppermute | solution.py:116
  160.9 1.9 %collective-permute-start.16 = (f32[8,768]{1,0:T(8,128)S(1)}, f32[8,768]{1,0:T(8,128)S(1)}, u32[]{:S(2)}, u32[]{:S(2)}) collective-permute-start(f32[8,768]{1,0:T(8,128)S(1)} %multiply_reduce_fusion), channel_id=1, source_target_pairs={{0,256},{1,0},{256,257},{257,1},{2,258},{3,2},{258,259},{259,3},{4... | collective-permute-start | bytes 73736 | tf_op jit(solution)/shard_map/ppermute | solution.py:117
  163.5 3.5 %collective-permute-done.16 = f32[8,768]{1,0:T(8,128)S(1)} collective-permute-done((f32[8,768]{1,0:T(8,128)S(1)}, f32[8,768]{1,0:T(8,128)S(1)}, u32[]{:S(2)}, u32[]{:S(2)}) %collective-permute-start.16) | collective-permute-done | bytes 24608 | tf_op jit(solution)/shard_map/ppermute | solution.py:117
  (68 shorter events, 13.0 us)
Async XLA Ops:
  0.0 10.1 %copy-start.4 = (bf16[2,192,896]{2,1,0:T(8,128)(2,1)S(1)}, bf16[2,192,896]{2,1,0:T(8,128)(2,1)}, u32[]{:S(2)}) copy-start(bf16[2,192,896]{2,1,0:T(8,128)(2,1)} %param.4) | copy-start | bytes 2064388
  1.4 10.7 %collective-permute-start = (bf16[128,896]{1,0:T(8,128)(2,1)S(1)}, bf16[128,896]{1,0:T(8,128)(2,1)S(1)}, u32[]{:S(2)}, u32[]{:S(2)}) collective-permute-start(bf16[128,896]{1,0:T(8,128)(2,1)S(1)} %dynamic-slice_bitcast_fusion), channel_id=1, source_target_pairs={{0,1},{1,0},{2,3},{3,2},{4,5},{5,4},{6,7},{7,6},{8,9},{9,8},{10,11... | collective-permute-start | bytes 688136 | tf_op jit(solution)/shard_map/ppermute | solution.py:19
  10.1 20.4 %collective-permute-start.5 = (bf16[384,896]{1,0:T(8,128)(2,1)S(1)}, bf16[384,896]{1,0:T(8,128)(2,1)S(1)}, u32[]{:S(2)}, u32[]{:S(2)}) collective-permute-start(bf16[384,896]{1,0:T(8,128)(2,1)S(1)} %bitcast.44), channel_id=1, source_target_pairs={{0,256},{256,0},{1,257},{257,1},{2,258},{258,2},{3,259},{259,3},{4... | collective-permute-start | bytes 2064392 | tf_op jit(solution)/shard_map/ppermute | solution.py:19
  12.1 18.9 %copy-start.2 = (bf16[128,1792]{1,0:T(8,128)(2,1)}, bf16[128,1792]{1,0:T(8,128)(2,1)S(1)}, u32[]{:S(2)}) copy-start(bf16[128,1792]{1,0:T(8,128)(2,1)S(1)} %pad_maximum_fusion.own) | copy-start | bytes 1376260
  12.1 9.6 %collective-permute-start.1 = (bf16[128,1792]{1,0:T(8,128)(2,1)S(1)}, bf16[128,1792]{1,0:T(8,128)(2,1)}, u32[]{:S(2)}, u32[]{:S(2)}) collective-permute-start(bf16[128,1792]{1,0:T(8,128)(2,1)S(1)} %pad_maximum_fusion.own), channel_id=1, source_target_pairs={{0,32},{1,225},{32,64},{33,1},{64,96},{65,33},{96,128},{97,65},{12... | collective-permute-start | bytes 1376264 | tf_op jit(solution)/shard_map/ppermute | solution.py:104
  14.6 19.2 %copy-start.7 = (bf16[256,96]{0,1:T(8,128)(2,1)S(1)}, bf16[256,96]{0,1:T(8,128)(2,1)}, u32[]{:S(2)}) copy-start(bf16[256,96]{0,1:T(8,128)(2,1)} %param.7) | copy-start | bytes 147460
  14.6 27.9 %copy-start.6 = (bf16[2,192,256]{2,1,0:T(8,128)(2,1)S(1)}, bf16[2,192,256]{2,1,0:T(8,128)(2,1)}, u32[]{:S(2)}) copy-start(bf16[2,192,256]{2,1,0:T(8,128)(2,1)} %param.5) | copy-start | bytes 589828
  21.8 16.3 %collective-permute-start.2 = (bf16[128,1792]{1,0:T(8,128)(2,1)}, bf16[128,1792]{1,0:T(8,128)(2,1)}, u32[]{:S(2)}, u32[]{:S(2)}) collective-permute-start(bf16[128,1792]{1,0:T(8,128)(2,1)} %collective-permute-done.1.one), channel_id=1, source_target_pairs={{0,32},{1,225},{32,64},{33,1},{64,96},{65,33},{96,128},{97,65},{12... | collective-permute-start | bytes 1376264 | tf_op jit(solution)/shard_map/ppermute | solution.py:104
  31.0 24.5 %copy-start = (bf16[768,896]{1,0:T(8,128)(2,1)}, bf16[768,896]{1,0:T(8,128)(2,1)S(1)}, u32[]{:S(2)}) copy-start(bf16[768,896]{1,0:T(8,128)(2,1)S(1)} %maximum_select_fusion.here) | copy-start | bytes 4128772
  31.0 36.0 %collective-permute-start.6 = (bf16[768,896]{1,0:T(8,128)(2,1)S(1)}, bf16[768,896]{1,0:T(8,128)(2,1)S(1)}, u32[]{:S(2)}, u32[]{:S(2)}) collective-permute-start(bf16[768,896]{1,0:T(8,128)(2,1)S(1)} %maximum_select_fusion.here), channel_id=1, source_target_pairs={{0,1},{1,0},{2,3},{3,2},{4,5},{5,4},{6,7},{7,6},{8,9},{9,8},{10,11... | collective-permute-start | bytes 4128776 | tf_op jit(solution)/shard_map/ppermute | solution.py:19
  34.6 17.9 %all-to-all-start.1 = ((bf16[16,48,256]{2,1,0:T(8,128)(2,1)}), bf16[16,48,256]{2,1,0:T(8,128)(2,1)S(1)}, u32[]{:S(2)}, u32[]{:S(2)}) async-start(bf16[16,48,256]{2,1,0:T(8,128)(2,1)} %bitcast.8), calls=%async_computation.1 | async-start | bytes 786432 | tf_op jit(solution)/shard_map/all_to_all | solution.py:23
  38.1 27.0 %collective-permute-start.3 = (bf16[128,1792]{1,0:T(8,128)(2,1)}, bf16[128,1792]{1,0:T(8,128)(2,1)}, u32[]{:S(2)}, u32[]{:S(2)}) collective-permute-start(bf16[128,1792]{1,0:T(8,128)(2,1)} %collective-permute-done.2.two), channel_id=1, source_target_pairs={{0,32},{1,225},{32,64},{33,1},{64,96},{65,33},{96,128},{97,65},{12... | collective-permute-start | bytes 1376264 | tf_op jit(solution)/shard_map/ppermute | solution.py:104
  42.5 3.5 %collective-permute-start.8 = (bf16[384,256]{1,0:T(8,128)(2,1)S(1)}, bf16[384,256]{1,0:T(8,128)(2,1)}, u32[]{:S(2)}, u32[]{:S(2)}) collective-permute-start(bf16[384,256]{1,0:T(8,128)(2,1)S(1)} %bitcast.57), channel_id=1, source_target_pairs={{0,1},{1,0},{2,3},{3,2},{4,5},{5,4},{6,7},{7,6},{8,9},{9,8},{10,11... | collective-permute-start | bytes 589832 | tf_op jit(solution)/shard_map/ppermute | solution.py:19
  52.5 0.7 copy-start.3
  55.5 24.4 %all-to-all-start.2 = ((bf16[16,24,384]{2,1,0:T(8,128)(2,1)}), bf16[16,24,384]{2,1,0:T(8,128)(2,1)S(1)}, u32[]{:S(2)}, u32[]{:S(2)}) async-start(bf16[16,24,384]{2,1,0:T(8,128)(2,1)} %bitcast.41), calls=%async_computation.2 | async-start | bytes 589824 | tf_op jit(solution)/shard_map/all_to_all | solution.py:23
  65.1 9.7 %collective-permute-start.4 = (bf16[128,1792]{1,0:T(8,128)(2,1)}, bf16[128,1792]{1,0:T(8,128)(2,1)S(1)}, u32[]{:S(2)}, u32[]{:S(2)}) collective-permute-start(bf16[128,1792]{1,0:T(8,128)(2,1)} %collective-permute-done.3.three), channel_id=1, source_target_pairs={{1,225},{33,1},{65,33},{97,65},{129,97},{161,129},{193,161},{225,1... | collective-permute-start | bytes 1376264 | tf_op jit(solution)/shard_map/ppermute | solution.py:104
  67.0 1.1 copy-start.1
  74.8 0.8 copy-start.5
  79.9 56.3 %all-to-all-start = ((bf16[16,4,8,768]{3,2,1,0:T(8,128)(2,1)}), bf16[16,4,8,768]{3,2,1,0:T(8,128)(2,1)S(1)}, u32[]{:S(2)}, u32[]{:S(2)}) async-start(bf16[16,4,8,768]{3,2,1,0:T(8,128)(2,1)} %shard_map.47), calls=%async_computation | async-start | bytes 1572864 | tf_op jit(solution)/shard_map/all_to_all | solution.py:23
  87.3 22.4 %collective-permute-start.9 = (bf16[1,24,384]{2,1,0:T(8,128)(2,1)S(1)}, bf16[1,24,384]{2,1,0:T(8,128)(2,1)S(1)}, u32[]{:S(2)}, u32[]{:S(2)}) collective-permute-start(bf16[1,24,384]{2,1,0:T(8,128)(2,1)S(1)} %bitcast.58), channel_id=1, source_target_pairs={{0,16},{4,20},{8,24},{12,28},{16,0},{20,4},{24,8},{28,12},{1,17},{... | collective-permute-start | bytes 55304 | tf_op jit(solution)/shard_map/ppermute | solution.py:109
  109.6 6.4 %collective-permute-start.10 = (bf16[2,24,384]{2,1,0:T(8,128)(2,1)S(1)}, bf16[2,24,384]{2,1,0:T(8,128)(2,1)S(1)}, u32[]{:S(2)}, u32[]{:S(2)}) collective-permute-start(bf16[2,24,384]{2,1,0:T(8,128)(2,1)S(1)} %maximum_select_fusion.6), channel_id=1, source_target_pairs={{0,8},{4,12},{8,0},{12,4},{16,24},{20,28},{24,16},{28,20},{1,9},{5... | collective-permute-start | bytes 110600 | tf_op jit(solution)/shard_map/ppermute | solution.py:109
  116.1 5.5 %collective-permute-start.11 = (bf16[4,24,384]{2,1,0:T(8,128)(2,1)S(1)}, bf16[4,24,384]{2,1,0:T(8,128)(2,1)S(1)}, u32[]{:S(2)}, u32[]{:S(2)}) collective-permute-start(bf16[4,24,384]{2,1,0:T(8,128)(2,1)S(1)} %bitcast.52), channel_id=1, source_target_pairs={{0,4},{4,0},{8,12},{12,8},{16,20},{20,16},{24,28},{28,24},{1,5},{5... | collective-permute-start | bytes 221192 | tf_op jit(solution)/shard_map/ppermute | solution.py:109
  121.6 7.0 %collective-permute-start.12 = (bf16[8,24,384]{2,1,0:T(8,128)(2,1)S(1)}, bf16[8,24,384]{2,1,0:T(8,128)(2,1)S(1)}, u32[]{:S(2)}, u32[]{:S(2)}) collective-permute-start(bf16[8,24,384]{2,1,0:T(8,128)(2,1)S(1)} %bitcast.46), channel_id=1, source_target_pairs={{0,2},{2,0},{1,3},{3,1},{4,6},{6,4},{5,7},{7,5},{8,10},{10,8},{9,1... | collective-permute-start | bytes 442376 | tf_op jit(solution)/shard_map/ppermute | solution.py:109
  128.7 10.0 %collective-permute-start.13 = (bf16[8,48,384]{2,1,0:T(8,128)(2,1)S(1)}, bf16[8,48,384]{2,1,0:T(8,128)(2,1)S(1)}, u32[]{:S(2)}, u32[]{:S(2)}) collective-permute-start(bf16[8,48,384]{2,1,0:T(8,128)(2,1)S(1)} %bitcast.50), channel_id=1, source_target_pairs={{0,0},{1,256},{256,1},{257,257},{2,2},{3,258},{258,3},{259,259},{4... | collective-permute-start | bytes 884744 | tf_op jit(solution)/shard_map/ppermute | solution.py:116
  134.1 9.0 %collective-permute-start.14 = (bf16[8,48,384]{2,1,0:T(8,128)(2,1)S(1)}, bf16[8,48,384]{2,1,0:T(8,128)(2,1)S(1)}, u32[]{:S(2)}, u32[]{:S(2)}) collective-permute-start(bf16[8,48,384]{2,1,0:T(8,128)(2,1)S(1)} %bitcast.51), channel_id=1, source_target_pairs={{0,256},{1,0},{256,257},{257,1},{2,258},{3,2},{258,259},{259,3},{4... | collective-permute-start | bytes 884744 | tf_op jit(solution)/shard_map/ppermute | solution.py:117
  136.3 6.8 %collective-permute-start.7 = (bf16[32,384]{1,0:T(8,128)(2,1)S(1)}, bf16[32,384]{1,0:T(8,128)(2,1)S(1)}, u32[]{:S(2)}, u32[]{:S(2)}) collective-permute-start(bf16[32,384]{1,0:T(8,128)(2,1)S(1)} %broadcast_select_fusion.2), channel_id=1, source_target_pairs={{0,1},{1,0},{2,3},{3,2},{4,5},{5,4},{6,7},{7,6},{8,9},{9,8},{10,11... | collective-permute-start | bytes 73736 | tf_op jit(solution)/shard_map/ppermute | solution.py:19
  156.8 6.7 %collective-permute-start.15 = (f32[8,768]{1,0:T(8,128)S(1)}, f32[8,768]{1,0:T(8,128)S(1)}, u32[]{:S(2)}, u32[]{:S(2)}) collective-permute-start(f32[8,768]{1,0:T(8,128)S(1)} %multiply_reduce_fusion), channel_id=1, source_target_pairs={{0,0},{1,256},{256,1},{257,257},{2,2},{3,258},{258,3},{259,259},{4... | collective-permute-start | bytes 73736 | tf_op jit(solution)/shard_map/ppermute | solution.py:116
  160.9 6.1 %collective-permute-start.16 = (f32[8,768]{1,0:T(8,128)S(1)}, f32[8,768]{1,0:T(8,128)S(1)}, u32[]{:S(2)}, u32[]{:S(2)}) collective-permute-start(f32[8,768]{1,0:T(8,128)S(1)} %multiply_reduce_fusion), channel_id=1, source_target_pairs={{0,256},{1,0},{256,257},{257,1},{2,258},{3,2},{258,259},{259,3},{4... | collective-permute-start | bytes 73736 | tf_op jit(solution)/shard_map/ppermute | solution.py:117

commit v3 on v0

v3 whole, which is shorter than its diff:
```python
import jax
import jax.numpy as jnp
from jax import lax
from jax.experimental import pallas as pl
from jax.experimental.layout import Layout, with_layout_constraint
from jax.sharding import Mesh
from jax.experimental.pallas import tpu as pltpu
from jax.sharding import PartitionSpec as P


TENSOR = ("z", "x", "c")
SEQ_TENSOR = ("seq", "z", "x", "c")
ALL = ("dp", "seq", "z", "x", "c")
F32 = jnp.float32
BF16 = jnp.bfloat16


def exchange(v, axis):
    return lax.ppermute(v, axis, [(0, 1), (1, 0)])


def all_to_all(v, axis):
    return lax.all_to_all(v, axis, 0, 0, tiled=True)


def to_everyone(v, axis):
    return all_to_all(jnp.broadcast_to(v[None], (lax.axis_size(axis), *v.shape)), axis)


def contract_last(a, b):
    return lax.dot_general(
        a, b, (((a.ndim - 1,), (b.ndim - 1,)), ((), ())), preferred_element_type=F32
    )


def grad_kernel(core, cols, own, other, out):
    lower = core[0] == 0
    rows = cols.shape[0] * cols.shape[2]
    width = own.shape[1]
    parts = own.shape[0] // other.shape[0]
    start = other.shape[1] - parts * width
    theirs = [other[:, start + k * width : start + (k + 1) * width] for k in range(parts)]
    theirs = jnp.concatenate(theirs, 0)
    first = jnp.where(lower, own[...], theirs)
    second = jnp.where(lower, theirs, own[...])
    out[...] = contract_last(cols[:, 0].reshape(rows, -1), first) + contract_last(
        cols[:, 1].reshape(rows, -1), second
    )


def body(activations, gradients, basis_in, basis_out):
    c = lax.axis_index("c")
    seqs, length, width = activations.shape
    tokens = seqs * length
    x_own = activations.reshape(tokens, width)
    g_own = gradients.reshape(tokens, -1)

    shard = with_layout_constraint(basis_in.T, Layout(major_to_minor=(0, 1)))
    shard = shard.reshape(16, 2, 8, width)
    half = lax.dynamic_index_in_dim(shard, c, 1, keepdims=False).reshape(128, width)
    other = lax.dynamic_index_in_dim(shard, 1 - c, 1, keepdims=False).reshape(128, width)
    folded = [g_own[k * 128 : (k + 1) * 128] for k in range(tokens // 128)]
    partner = exchange(jnp.concatenate([other, *folded], 1), "c")
    block = jnp.concatenate([half, partner[:, :width]], 1)
    columns = lax.all_gather(block, "seq", axis=0, tiled=True)
    x_other = exchange(x_own, "c")

    halves = basis_out.T.reshape(1, 2, -1, basis_out.shape[0])
    spread = jnp.broadcast_to(halves, (8, *halves.shape[1:])).reshape(16, -1, basis_out.shape[0])
    out_cols = all_to_all(spread, ("seq", "c"))
    out_cols = out_cols.reshape(8, 2, -1, basis_out.shape[0])

    grad_partial = pl.pallas_call(
        grad_kernel,
        in_specs=[pl.BlockSpec(memory_space=pltpu.SMEM)]
        + [pl.BlockSpec(memory_space=pltpu.VMEM)] * 3,
        out_specs=pl.BlockSpec(memory_space=pltpu.VMEM),
        out_shape=jax.ShapeDtypeStruct((8 * out_cols.shape[2], tokens), F32),
    )(c.reshape(1), out_cols, g_own, partner)
    grad_parts = all_to_all(grad_partial.reshape(16, -1, tokens), ("z", "x"))
    grad_own = grad_parts.sum(0).astype(BF16)
    grad_half = to_everyone(grad_own, ("z", "x")).reshape(8, -1, tokens)
    grad_rest = exchange(grad_half, "c")
    grads = jnp.where(
        c == 0, jnp.stack([grad_half, grad_rest], 1), jnp.stack([grad_rest, grad_half], 1)
    ).reshape(-1, tokens)

    x_rows = lax.optimization_barrier(jnp.concatenate([x_own, x_other], 1))
    parts = contract_last(columns, x_rows).astype(BF16)
    parts = parts.reshape(8, 16, 8, tokens).swapaxes(0, 1)
    arrived = all_to_all(parts, ("z", "x"))
    act = arrived.astype(F32).sum(0).astype(BF16).reshape(64, tokens)

    of_seq = lax.broadcasted_iota(jnp.int32, (seqs, 1, tokens), 2) // length
    chosen = of_seq == lax.broadcasted_iota(jnp.int32, (seqs, 1, tokens), 0)
    masked = jnp.where(chosen, act[None], jnp.zeros((), BF16))
    partial_blocks = contract_last(masked, grads)
    pieces = partial_blocks.astype(BF16).reshape(seqs, 8, 8, -1).swapaxes(0, 1)
    blocks = all_to_all(pieces, "seq").astype(F32).sum(0)
    squared = jnp.sum(blocks * blocks, axis=0)
    far = exchange(squared, "dp")
    return (squared + far) / (2 * seqs * 8 * length)


def solution(mesh):
    finer = Mesh(mesh.devices.reshape(2, 8, 8, 2, 2), ALL)
    in_specs = (P("dp", "seq", TENSOR), P("dp", "seq", TENSOR), P(TENSOR, "seq"), P(TENSOR, "seq"))
    out_specs = P(SEQ_TENSOR, None)

    return jax.shard_map(body, mesh=finer, in_specs=in_specs, out_specs=out_specs, check_vma=False)
```

time: 151 us -> 142 us (0.940)
  the two profiles are of different devices: /device:TPU:1 before, /device:TPU:4 now
where the time goes in v3:
time: 142 us; the launch traced here: 141 us
  waiting for transfers between devices  52 us (37%)
  blocking collectives  32.9 us (23%)
  starting transfers between devices  29.5 us (21%)
  between operations  13.6 us (10%)
  matrix products  4.43 us (3%)
  local copies, waits for them, and re-layouts  4.07 us (3%)
  Pallas kernels  2.5 us (2%)
  other arithmetic  1.93 us (1%)
    all_to_all x3, waiting for transfers between devices, all_to_all(): return lax.all_to_all(v, axis, 0, 0, tiled=True)  44.2 us
    all_to_all x2, blocking collectives, all_to_all(): return lax.all_to_all(v, axis, 0, 0, tiled=True)  32.9 us
    all_to_all x3, starting transfers between devices, all_to_all(): return lax.all_to_all(v, axis, 0, 0, tiled=True)  19.8 us
    ppermute x4, starting transfers between devices, exchange(): return lax.ppermute(v, axis, [(0, 1), (1, 0)])  9.73 us
    ppermute x4, waiting for transfers between devices, exchange(): return lax.ppermute(v, axis, [(0, 1), (1, 0)])  7.82 us
    dot_general x2, matrix products, contract_last(): lax.dot_general(a, b, (((a.ndim - 1,), (b.ndim - 1,)), ((), ())), preferr...  4.43 us
  transfers between devices with their start and end apart: 8, of which 6 were waited for; matrix products, arithmetic and copies ran while one was open for 4% of the time, Pallas kernels for 2%

profile of v3, /device:TPU:4, one launch (start us, length us, event | category | flops | bytes accessed | tf_op | source)
XLA Modules:
  0.0 140.9 jit_solution(2362398451093818925)
XLA Ops:
  6.5 1.3 copy.13
  7.8 0.9 fusion.9
  8.7 0.1 dynamic-slice_bitcast_fusion.1
  8.8 0.0 copy-start.2
  8.9 1.9 %collective-permute-start = (bf16[128,1664]{1,0:T(8,128)(2,1)S(1)}, bf16[128,1664]{1,0:T(8,128)(2,1)S(1)}, u32[]{:S(2)}, u32[]{:S(2)}) collective-permute-start(bf16[128,1664]{1,0:T(8,128)(2,1)S(1)} %pad_maximum_fusion.2), channel_id=1, source_target_pairs={{0,1},{1,0},{2,3},{3,2},{4,5},{5,4},{6,7},{7,6},{8,9},{9,8},{10,11... | collective-permute-start | bytes 1277960 | tf_op jit(solution)/shard_map/ppermute | solution.py:19
  10.8 1.7 %collective-permute-done.other = bf16[128,1664]{1,0:T(8,128)(2,1)S(1)} collective-permute-done((bf16[128,1664]{1,0:T(8,128)(2,1)S(1)}, bf16[128,1664]{1,0:T(8,128)(2,1)S(1)}, u32[]{:S(2)}, u32[]{:S(2)}) %collective-permute-start) | collective-permute-done | bytes 426016 | tf_op jit(solution)/shard_map/ppermute | solution.py:19
  12.5 0.9 pad_maximum_fusion.1
  13.4 0.0 all-gather.2.cloned.1.call-update
  13.5 20.7 %all_to_all.25 = bf16[16,48,256]{2,1,0:T(8,128)(2,1)} all-to-all(bf16[16,48,256]{2,1,0:T(8,128)(2,1)S(1)} %bitcast.42), channel_id=1, replica_groups=mesh['dp'=2,'seq'=8,'z'=8,'x'=2,'c'=2] {'seq','c'}, dimensions={0} | all-to-all | bytes 786432 | tf_op jit(solution)/shard_map/all_to_all | solution.py:23
  34.2 2.5 %shard_map.46 = f32[384,384]{1,0:T(8,128)} custom-call(s32[1]{0:T(128)} %bitcast.10.core, bf16[8,2,48,256]{3,2,1,0:T(8,128)(2,1)} %bitcast.43, bf16[384,256]{1,0:T(8,128)(2,1)} %bitcast.49, bf16[128,1664]{1,0:T(8,128)(2,1)} %copy-done), custom_call_target="tpu_custom_call" | custom-call | tf_op jit(solution)/shard_map/pallas_call | solution.py:73
  36.7 12.0 %all-to-all-start.2 = ((f32[16,24,384]{2,1,0:T(8,128)}), f32[16,24,384]{2,1,0:T(8,128)S(1)}, u32[]{:S(2)}, u32[]{:S(2)}) async-start(f32[16,24,384]{2,1,0:T(8,128)} %bitcast.40), calls=%async_computation.2 | async-start | bytes 1179648 | tf_op jit(solution)/shard_map/all_to_all | solution.py:23
  48.7 3.2 %collective-permute-start.1 = (bf16[384,896]{1,0:T(8,128)(2,1)S(1)}, bf16[384,896]{1,0:T(8,128)(2,1)S(1)}, u32[]{:S(2)}, u32[]{:S(2)}) collective-permute-start(bf16[384,896]{1,0:T(8,128)(2,1)S(1)} %bitcast.50), channel_id=1, source_target_pairs={{0,1},{1,0},{2,3},{3,2},{4,5},{5,4},{6,7},{7,6},{8,9},{9,8},{10,11... | collective-permute-start | bytes 2064392 | tf_op jit(solution)/shard_map/ppermute | solution.py:19
  52.0 15.6 %all-to-all-done.2 = f32[16,24,384]{2,1,0:T(8,128)S(1)} async-done(((f32[16,24,384]{2,1,0:T(8,128)}), f32[16,24,384]{2,1,0:T(8,128)S(1)}, u32[]{:S(2)}, u32[]{:S(2)}) %all-to-all-start.2) | async-done | bytes 589856 | tf_op jit(solution)/shard_map/all_to_all | solution.py:23
  67.6 0.7 broadcast_in_dim.41
  68.4 4.2 %all-to-all-start.3 = ((bf16[16,24,384]{2,1,0:T(8,128)(2,1)}), bf16[16,24,384]{2,1,0:T(8,128)(2,1)S(1)}, u32[]{:S(2)}, u32[]{:S(2)}) async-start(bf16[16,24,384]{2,1,0:T(8,128)(2,1)} %broadcast_in_dim.41), calls=%async_computation.3 | async-start | bytes 589824 | tf_op jit(solution)/shard_map/all_to_all | solution.py:23
  72.5 0.0 collective-permute-done.1
  72.6 0.1 pad_maximum_fusion
  72.7 0.0 all-gather.2.cloned.1.call-done
  72.7 4.1 %convolution_convert_fusion = bf16[1024,384]{1,0:T(8,128)(2,1)S(1)} fusion(bf16[1024,1792]{1,0:T(8,128)(2,1)} %all-gather.2.cloned.1.call-done, bf16[384,1792]{1,0:T(8,128)(2,1)S(1)} %pad_maximum_fusion), kind=kOutput, calls=%fused_computation | convolution fusion | flops 1409679360 | bytes 5832704 | tf_op jit(solution)/shard_map/dot_general | solution.py:31
  76.8 1.0 copy.22
  77.8 8.4 %all-to-all-done.3 = bf16[16,24,384]{2,1,0:T(8,128)(2,1)S(1)} async-done(((bf16[16,24,384]{2,1,0:T(8,128)(2,1)}), bf16[16,24,384]{2,1,0:T(8,128)(2,1)S(1)}, u32[]{:S(2)}, u32[]{:S(2)}) %all-to-all-start.3) | async-done | bytes 294944 | tf_op jit(solution)/shard_map/all_to_all | solution.py:23
  86.2 3.6 %all-to-all-start = ((bf16[16,8,8,384]{3,2,1,0:T(8,128)(2,1)}), bf16[16,8,8,384]{3,2,1,0:T(8,128)(2,1)S(1)}, u32[]{:S(2)}, u32[]{:S(2)}) async-start(bf16[16,8,8,384]{3,2,1,0:T(8,128)(2,1)} %bitcast.37), calls=%async_computation | async-start | bytes 1572864 | tf_op jit(solution)/shard_map/all_to_all | solution.py:23
  89.9 1.9 %collective-permute-start.2 = (bf16[8,48,384]{2,1,0:T(8,128)(2,1)S(1)}, bf16[8,48,384]{2,1,0:T(8,128)(2,1)S(1)}, u32[]{:S(2)}, u32[]{:S(2)}) collective-permute-start(bf16[8,48,384]{2,1,0:T(8,128)(2,1)S(1)} %bitcast.44), channel_id=1, source_target_pairs={{0,1},{1,0},{2,3},{3,2},{4,5},{5,4},{6,7},{7,6},{8,9},{9,8},{10,11... | collective-permute-start | bytes 884744 | tf_op jit(solution)/shard_map/ppermute | solution.py:19
  91.8 1.5 %collective-permute-done.2 = bf16[8,48,384]{2,1,0:T(8,128)(2,1)S(1)} collective-permute-done((bf16[8,48,384]{2,1,0:T(8,128)(2,1)S(1)}, bf16[8,48,384]{2,1,0:T(8,128)(2,1)S(1)}, u32[]{:S(2)}, u32[]{:S(2)}) %collective-permute-start.2) | collective-permute-done | bytes 294944 | tf_op jit(solution)/shard_map/ppermute | solution.py:19
  93.4 0.1 maximum_select_fusion
  93.4 20.1 %all-to-all-done = bf16[16,8,8,384]{3,2,1,0:T(8,128)(2,1)S(1)} async-done(((bf16[16,8,8,384]{3,2,1,0:T(8,128)(2,1)}), bf16[16,8,8,384]{3,2,1,0:T(8,128)(2,1)S(1)}, u32[]{:S(2)}, u32[]{:S(2)}) %all-to-all-start) | async-done | bytes 786464 | tf_op jit(solution)/shard_map/all_to_all | solution.py:23
  113.6 0.1 reduce_sum.39
  113.7 0.3 fusion
  114.0 12.2 %all_to_all.26 = bf16[8,2,8,768]{3,2,1,0:T(8,128)(2,1)S(1)} all-to-all(bf16[8,2,8,768]{3,2,1,0:T(8,128)(2,1)S(1)} %bitcast.47), channel_id=1, replica_groups=mesh['dp'=2,'seq'=8,'z'=8,'x'=2,'c'=2] {'seq'}, dimensions={0} | all-to-all | bytes 393216 | tf_op jit(solution)/shard_map/all_to_all | solution.py:23
  126.2 2.7 %collective-permute-start.3 = (f32[8,768]{1,0:T(8,128)S(1)}, f32[8,768]{1,0:T(8,128)S(1)}, u32[]{:S(2)}, u32[]{:S(2)}) collective-permute-start(f32[8,768]{1,0:T(8,128)S(1)} %multiply_reduce_fusion), channel_id=1, source_target_pairs={{0,256},{256,0},{1,257},{257,1},{2,258},{258,2},{3,259},{259,3},{4... | collective-permute-start | bytes 73736 | tf_op jit(solution)/shard_map/ppermute | solution.py:19
  128.9 4.6 %collective-permute-done.3 = f32[8,768]{1,0:T(8,128)S(1)} collective-permute-done((f32[8,768]{1,0:T(8,128)S(1)}, f32[8,768]{1,0:T(8,128)S(1)}, u32[]{:S(2)}, u32[]{:S(2)}) %collective-permute-start.3) | collective-permute-done | bytes 24608 | tf_op jit(solution)/shard_map/ppermute | solution.py:19
  133.5 0.6 add_multiply_fusion
  (16 shorter events, 0.2 us)
Async XLA Ops:
  6.5 66.1 %all-gather.2.cloned.1.call-start = ((), (), s32[]{:S(2)}) async-start(), calls=%async_computation.5 | async-start | bytes 4128768 | tf_op jit(solution)/shard_map/all_gather | solution.py:65
  8.8 4.7 %copy-start.2 = (bf16[256,96]{0,1:T(8,128)(2,1)S(1)}, bf16[256,96]{0,1:T(8,128)(2,1)}, u32[]{:S(2)}) copy-start(bf16[256,96]{0,1:T(8,128)(2,1)} %param.7) | copy-start | bytes 147460
  8.9 3.7 %collective-permute-start = (bf16[128,1664]{1,0:T(8,128)(2,1)S(1)}, bf16[128,1664]{1,0:T(8,128)(2,1)S(1)}, u32[]{:S(2)}, u32[]{:S(2)}) collective-permute-start(bf16[128,1664]{1,0:T(8,128)(2,1)S(1)} %pad_maximum_fusion.2), channel_id=1, source_target_pairs={{0,1},{1,0},{2,3},{3,2},{4,5},{5,4},{6,7},{7,6},{8,9},{9,8},{10,11... | collective-permute-start | bytes 1277960 | tf_op jit(solution)/shard_map/ppermute | solution.py:19
  12.5 21.7 %copy-start = (bf16[128,1664]{1,0:T(8,128)(2,1)}, bf16[128,1664]{1,0:T(8,128)(2,1)S(1)}, u32[]{:S(2)}) copy-start(bf16[128,1664]{1,0:T(8,128)(2,1)S(1)} %collective-permute-done.other) | copy-start | bytes 1277956
  34.2 14.5 %copy-start.1 = (bf16[2,192,896]{2,1,0:T(8,128)(2,1)S(1)}, bf16[2,192,896]{2,1,0:T(8,128)(2,1)}, u32[]{:S(2)}) copy-start(bf16[2,192,896]{2,1,0:T(8,128)(2,1)} %param.4) | copy-start | bytes 2064388
  36.7 30.8 %all-to-all-start.2 = ((f32[16,24,384]{2,1,0:T(8,128)}), f32[16,24,384]{2,1,0:T(8,128)S(1)}, u32[]{:S(2)}, u32[]{:S(2)}) async-start(f32[16,24,384]{2,1,0:T(8,128)} %bitcast.40), calls=%async_computation.2 | async-start | bytes 1179648 | tf_op jit(solution)/shard_map/all_to_all | solution.py:23
  48.7 23.8 %collective-permute-start.1 = (bf16[384,896]{1,0:T(8,128)(2,1)S(1)}, bf16[384,896]{1,0:T(8,128)(2,1)S(1)}, u32[]{:S(2)}, u32[]{:S(2)}) collective-permute-start(bf16[384,896]{1,0:T(8,128)(2,1)S(1)} %bitcast.50), channel_id=1, source_target_pairs={{0,1},{1,0},{2,3},{3,2},{4,5},{5,4},{6,7},{7,6},{8,9},{9,8},{10,11... | collective-permute-start | bytes 2064392 | tf_op jit(solution)/shard_map/ppermute | solution.py:19
  68.4 17.9 %all-to-all-start.3 = ((bf16[16,24,384]{2,1,0:T(8,128)(2,1)}), bf16[16,24,384]{2,1,0:T(8,128)(2,1)S(1)}, u32[]{:S(2)}, u32[]{:S(2)}) async-start(bf16[16,24,384]{2,1,0:T(8,128)(2,1)} %broadcast_in_dim.41), calls=%async_computation.3 | async-start | bytes 589824 | tf_op jit(solution)/shard_map/all_to_all | solution.py:23
  86.2 27.3 %all-to-all-start = ((bf16[16,8,8,384]{3,2,1,0:T(8,128)(2,1)}), bf16[16,8,8,384]{3,2,1,0:T(8,128)(2,1)S(1)}, u32[]{:S(2)}, u32[]{:S(2)}) async-start(bf16[16,8,8,384]{3,2,1,0:T(8,128)(2,1)} %bitcast.37), calls=%async_computation | async-start | bytes 1572864 | tf_op jit(solution)/shard_map/all_to_all | solution.py:23
  89.9 3.5 %collective-permute-start.2 = (bf16[8,48,384]{2,1,0:T(8,128)(2,1)S(1)}, bf16[8,48,384]{2,1,0:T(8,128)(2,1)S(1)}, u32[]{:S(2)}, u32[]{:S(2)}) collective-permute-start(bf16[8,48,384]{2,1,0:T(8,128)(2,1)S(1)} %bitcast.44), channel_id=1, source_target_pairs={{0,1},{1,0},{2,3},{3,2},{4,5},{5,4},{6,7},{7,6},{8,9},{9,8},{10,11... | collective-permute-start | bytes 884744 | tf_op jit(solution)/shard_map/ppermute | solution.py:19
  126.2 7.2 %collective-permute-start.3 = (f32[8,768]{1,0:T(8,128)S(1)}, f32[8,768]{1,0:T(8,128)S(1)}, u32[]{:S(2)}, u32[]{:S(2)}) collective-permute-start(f32[8,768]{1,0:T(8,128)S(1)} %multiply_reduce_fusion), channel_id=1, source_target_pairs={{0,256},{256,0},{1,257},{257,1},{2,258},{258,2},{3,259},{259,3},{4... | collective-permute-start | bytes 73736 | tf_op jit(solution)/shard_map/ppermute | solution.py:19
Sparse Core Ops, SparseCore 0:
  13.6 56.7 all-gather.1

commit v4 on v3

v4 whole, which is shorter than its diff:
```python
import jax
import jax.numpy as jnp
from jax import lax
from jax.experimental import pallas as pl
from jax.experimental.layout import Layout, with_layout_constraint
from jax.sharding import Mesh
from jax.experimental.pallas import tpu as pltpu
from jax.sharding import PartitionSpec as P


TENSOR = ("z", "x", "c")
SEQ_TENSOR = ("seq", "z", "x", "c")
ALL = ("dp", "seq", "z", "x", "c")
F32 = jnp.float32
BF16 = jnp.bfloat16


def exchange(v, axis):
    return lax.ppermute(v, axis, [(0, 1), (1, 0)])


def all_to_all(v, axis):
    return lax.all_to_all(v, axis, 0, 0, tiled=True)


def to_everyone(v, axis):
    return all_to_all(jnp.broadcast_to(v[None], (lax.axis_size(axis), *v.shape)), axis)


def contract_last(a, b):
    return lax.dot_general(
        a, b, (((a.ndim - 1,), (b.ndim - 1,)), ((), ())), preferred_element_type=F32
    )


def grad_kernel(cols, own, beside, pair, out):
    rows = cols.shape[0] * cols.shape[2]
    found = jnp.zeros(out.shape, F32)
    for k, features in enumerate((own[...], pair[0], beside[...], pair[1])):
        columns = cols[:, k].astype(F32).reshape(rows, -1).astype(BF16)
        found = found + contract_last(columns, features)
    out[...] = found


def body(activations, gradients, basis_in, basis_out):
    x = lax.axis_index("x")
    c = lax.axis_index("c")
    seqs, length, width = activations.shape
    tokens = seqs * length
    narrow = basis_out.shape[0]
    x_own = activations.reshape(tokens, width)
    g_own = gradients.reshape(tokens, narrow)

    shard = with_layout_constraint(basis_in.T, Layout(major_to_minor=(0, 1)))
    shard = shard.reshape(8, 4, 8, width).swapaxes(0, 1).reshape(4, 64, width)
    small = jnp.pad(basis_out.T.reshape(4, 24, narrow), ((0, 0), (0, 0), (0, width - narrow)))
    quarter = all_to_all(jnp.concatenate([shard, small], 1), ("x", "c"))
    near = [
        lax.dynamic_index_in_dim(quarter, (x * 2 + c) ^ k, 0, keepdims=False) for k in range(4)
    ]
    block = jnp.concatenate([piece[:64] for piece in near], 1)
    columns = lax.all_gather(block, "seq", axis=0, tiled=True)
    small = jnp.stack([piece[64:, :narrow] for piece in near])

    g_beside = exchange(g_own, "x")
    g_pair = exchange(jnp.stack([g_own, g_beside]), "c")
    x_beside = exchange(x_own, "x")
    x_pair = exchange(jnp.stack([x_own, x_beside]), "c")

    out_cols = to_everyone(small, "seq")
    grad_partial = pl.pallas_call(
        grad_kernel,
        in_specs=[pl.BlockSpec(memory_space=pltpu.VMEM)] * 4,
        out_specs=pl.BlockSpec(memory_space=pltpu.VMEM),
        out_shape=jax.ShapeDtypeStruct((8 * 24, tokens), F32),
    )(out_cols, g_own, g_beside, g_pair)
    grad_parts = all_to_all(grad_partial.reshape(8, 24, tokens), "z")
    grad_own = grad_parts.sum(0).astype(BF16)
    grad_quarter = to_everyone(grad_own, "z")
    rest = exchange(grad_quarter, "x")
    grad_half = jnp.where(x == 0, jnp.stack([grad_quarter, rest]), jnp.stack([rest, grad_quarter]))
    rest = exchange(grad_half, "c")
    grads = jnp.where(c == 0, jnp.stack([grad_half, rest]), jnp.stack([rest, grad_half]))
    grads = grads.transpose(2, 1, 0, 3, 4).reshape(-1, tokens)

    x_rows = jnp.concatenate([x_own, x_pair[0], x_beside, x_pair[1]], 1)
    x_rows = lax.optimization_barrier(x_rows)
    parts = contract_last(columns, x_rows).astype(BF16)
    parts = parts.reshape(8, 8, 8, tokens).swapaxes(0, 1)
    arrived = all_to_all(parts, "z")
    act = arrived.astype(F32).sum(0).astype(BF16).reshape(64, tokens)

    of_seq = lax.broadcasted_iota(jnp.int32, (seqs, 1, tokens), 2) // length
    chosen = of_seq == lax.broadcasted_iota(jnp.int32, (seqs, 1, tokens), 0)
    masked = jnp.where(chosen, act[None], jnp.zeros((), BF16))
    partial_blocks = contract_last(masked, grads)
    pieces = partial_blocks.astype(BF16).reshape(seqs, 8, 8, -1).swapaxes(0, 1)
    blocks = all_to_all(pieces, "seq").astype(F32).sum(0)
    squared = jnp.sum(blocks * blocks, axis=0)
    far = exchange(squared, "dp")
    return (squared + far) / (2 * seqs * 8 * length)


def solution(mesh):
    finer = Mesh(mesh.devices.reshape(2, 8, 8, 2, 2), ALL)
    in_specs = (P("dp", "seq", TENSOR), P("dp", "seq", TENSOR), P(TENSOR, "seq"), P(TENSOR, "seq"))
    out_specs = P(SEQ_TENSOR, None)

    return jax.shard_map(body, mesh=finer, in_specs=in_specs, out_specs=out_specs, check_vma=False)
```

time: 142 us -> 154 us (1.085)
  the two profiles are of different devices: /device:TPU:4 before, /device:TPU:6 now
where the time goes in v4:
time: 154 us; the launch traced here: 153 us
  blocking collectives  41.8 us (27%)
  waiting for transfers between devices  40.2 us (26%)
  starting transfers between devices  37.2 us (24%)
  between operations  13.7 us (9%)
  other arithmetic  8.5 us (6%)
  local copies, waits for them, and re-layouts  4.59 us (3%)
  matrix products  4.42 us (3%)
  Pallas kernels  2.42 us (2%)
    all_to_all x2, blocking collectives, all_to_all(): return lax.all_to_all(v, axis, 0, 0, tiled=True)  41.8 us
    all_to_all x4, waiting for transfers between devices, all_to_all(): return lax.all_to_all(v, axis, 0, 0, tiled=True)  24.5 us
    all_to_all x4, starting transfers between devices, all_to_all(): return lax.all_to_all(v, axis, 0, 0, tiled=True)  18.8 us
    ppermute x7, starting transfers between devices, exchange(): return lax.ppermute(v, axis, [(0, 1), (1, 0)])  18.4 us
    ppermute x7, waiting for transfers between devices, exchange(): return lax.ppermute(v, axis, [(0, 1), (1, 0)])  15.7 us
    dot_general x2, matrix products, contract_last(): lax.dot_general(a, b, (((a.ndim - 1,), (b.ndim - 1,)), ((), ())), preferr...  4.42 us
  transfers between devices with their start and end apart: 12, of which 7 were waited for; matrix products, arithmetic and copies ran while one was open for 8% of the time, Pallas kernels for 2%

profile of v4, /device:TPU:6, one launch (start us, length us, event | category | flops | bytes accessed | tf_op | source)
XLA Modules:
  0.0 152.8 jit_solution(16966796130005035964)
XLA Ops:
  6.5 1.3 copy.18
  7.9 1.7 %fusion.2 = bf16[4,88,896]{2,1,0:T(8,128)(2,1)} fusion(bf16[4,24,256]{2,1,0:T(8,128)(2,1)} %bitcast.81, bf16[4,64,896]{2,1,0:T(8,128)(2,1)S(1)} %bitcast.74), kind=kLoop, calls=%fused_computation.9 | loop fusion | flops 1892352 | bytes 1138688 | tf_op jit(solution)/shard_map/concatenate | solution.py:57
  9.6 4.3 %all-to-all-start = ((bf16[4,88,896]{2,1,0:T(8,128)(2,1)}), bf16[4,88,896]{2,1,0:T(8,128)(2,1)S(1)}, u32[]{:S(2)}, u32[]{:S(2)}) async-start(bf16[4,88,896]{2,1,0:T(8,128)(2,1)} %fusion.2), calls=%async_computation | async-start | bytes 1261568 | tf_op jit(solution)/shard_map/all_to_all | solution.py:23
  13.9 8.3 %all-to-all-done = bf16[4,88,896]{2,1,0:T(8,128)(2,1)S(1)} async-done(((bf16[4,88,896]{2,1,0:T(8,128)(2,1)}), bf16[4,88,896]{2,1,0:T(8,128)(2,1)S(1)}, u32[]{:S(2)}, u32[]{:S(2)}) %all-to-all-start) | async-done | bytes 630816 | tf_op jit(solution)/shard_map/all_to_all | solution.py:23
  22.3 0.8 pad_maximum_fusion.2
  23.1 3.5 %collective-permute-start.2 = (bf16[384,256]{1,0:T(8,128)(2,1)}, bf16[384,256]{1,0:T(8,128)(2,1)}, u32[]{:S(2)}, u32[]{:S(2)}) collective-permute-start(bf16[384,256]{1,0:T(8,128)(2,1)} %bitcast.26.own), channel_id=1, source_target_pairs={{0,2},{2,0},{1,3},{3,1},{4,6},{6,4},{5,7},{7,5},{8,10},{10,8},{9,1... | collective-permute-start | bytes 589832 | tf_op jit(solution)/shard_map/ppermute | solution.py:19
  26.6 2.3 %collective-permute-start = (bf16[384,896]{1,0:T(8,128)(2,1)S(1)}, bf16[384,896]{1,0:T(8,128)(2,1)S(1)}, u32[]{:S(2)}, u32[]{:S(2)}) collective-permute-start(bf16[384,896]{1,0:T(8,128)(2,1)S(1)} %bitcast.69), channel_id=1, source_target_pairs={{0,2},{2,0},{1,3},{3,1},{4,6},{6,4},{5,7},{7,5},{8,10},{10,8},{9,1... | collective-permute-start | bytes 2064392 | tf_op jit(solution)/shard_map/ppermute | solution.py:19
  29.1 0.8 broadcast_in_dim.38
  29.9 7.1 %all-to-all-start.2 = ((bf16[8,4,24,256]{3,2,1,0:T(8,128)(2,1)}), bf16[8,4,24,256]{3,2,1,0:T(8,128)(2,1)S(1)}, u32[]{:S(2)}, u32[]{:S(2)}) async-start(bf16[8,4,24,256]{3,2,1,0:T(8,128)(2,1)} %broadcast_in_dim.38), calls=%async_computation.2 | async-start | bytes 786432 | tf_op jit(solution)/shard_map/all_to_all | solution.py:23
  37.0 9.7 %collective-permute-done = bf16[384,896]{1,0:T(8,128)(2,1)S(1)} collective-permute-done((bf16[384,896]{1,0:T(8,128)(2,1)S(1)}, bf16[384,896]{1,0:T(8,128)(2,1)S(1)}, u32[]{:S(2)}, u32[]{:S(2)}) %collective-permute-start) | collective-permute-done | bytes 688160 | tf_op jit(solution)/shard_map/ppermute | solution.py:19
  46.6 1.3 pad_maximum_fusion.1
  48.0 1.9 %collective-permute-start.1 = (bf16[2,384,896]{2,1,0:T(8,128)(2,1)}, bf16[2,384,896]{2,1,0:T(8,128)(2,1)S(1)}, u32[]{:S(2)}, u32[]{:S(2)}) collective-permute-start(bf16[2,384,896]{2,1,0:T(8,128)(2,1)} %pad_maximum_fusion.1), channel_id=1, source_target_pairs={{0,1},{1,0},{2,3},{3,2},{4,5},{5,4},{6,7},{7,6},{8,9},{9,8},{10,11... | collective-permute-start | bytes 4128776 | tf_op jit(solution)/shard_map/ppermute | solution.py:19
  49.9 1.1 pad_maximum_fusion.3
  50.9 2.4 %collective-permute-start.3 = (bf16[2,384,256]{2,1,0:T(8,128)(2,1)S(1)}, bf16[2,384,256]{2,1,0:T(8,128)(2,1)}, u32[]{:S(2)}, u32[]{:S(2)}) collective-permute-start(bf16[2,384,256]{2,1,0:T(8,128)(2,1)S(1)} %pad_maximum_fusion.3), channel_id=1, source_target_pairs={{0,1},{1,0},{2,3},{3,2},{4,5},{5,4},{6,7},{7,6},{8,9},{9,8},{10,11... | collective-permute-start | bytes 1179656 | tf_op jit(solution)/shard_map/ppermute | solution.py:19
  53.4 1.5 collective-permute-done.3.pair
  54.8 0.8 copy-done.3
  55.6 2.4 %shard_map.46 = f32[192,384]{1,0:T(8,128)} custom-call(bf16[8,4,24,256]{3,2,1,0:T(8,128)(2,1)} %copy-done.3, bf16[384,256]{1,0:T(8,128)(2,1)} %bitcast.26.own, bf16[384,256]{1,0:T(8,128)(2,1)} %collective-permute-done.2.beside, bf16[2,384,256]{2,1,0:T(8,128)(2,1)} %collective-permute-done.3.pair), custom_call_target="tpu_custom_call" | custom-call | tf_op jit(solution)/shard_map/pallas_call | solution.py:71
  58.0 23.4 %all_to_all.30 = f32[8,24,384]{2,1,0:T(8,128)S(1)} all-to-all(f32[8,24,384]{2,1,0:T(8,128)} %bitcast.76), channel_id=1, replica_groups=mesh['dp'=2,'seq'=8,'z'=8,'x'=2,'c'=2] {'z'}, dimensions={0} | all-to-all | bytes 589824 | tf_op jit(solution)/shard_map/all_to_all | solution.py:23
  81.5 0.7 broadcast_in_dim.39
  82.2 4.0 %all-to-all-start.4 = ((bf16[8,24,384]{2,1,0:T(8,128)(2,1)}), bf16[8,24,384]{2,1,0:T(8,128)(2,1)}, u32[]{:S(2)}, u32[]{:S(2)}) async-start(bf16[8,24,384]{2,1,0:T(8,128)(2,1)} %broadcast_in_dim.39), calls=%async_computation.4 | async-start | bytes 294912 | tf_op jit(solution)/shard_map/all_to_all | solution.py:23
  86.2 9.2 %all-to-all-done.4 = bf16[8,24,384]{2,1,0:T(8,128)(2,1)} async-done(((bf16[8,24,384]{2,1,0:T(8,128)(2,1)}), bf16[8,24,384]{2,1,0:T(8,128)(2,1)}, u32[]{:S(2)}, u32[]{:S(2)}) %all-to-all-start.4) | async-done | bytes 147488 | tf_op jit(solution)/shard_map/all_to_all | solution.py:23
  95.4 3.3 %collective-permute-start.4 = (bf16[8,24,384]{2,1,0:T(8,128)(2,1)}, bf16[8,24,384]{2,1,0:T(8,128)(2,1)}, u32[]{:S(2)}, u32[]{:S(2)}) collective-permute-start(bf16[8,24,384]{2,1,0:T(8,128)(2,1)} %all-to-all-done.4), channel_id=1, source_target_pairs={{0,2},{2,0},{1,3},{3,1},{4,6},{6,4},{5,7},{7,5},{8,10},{10,8},{9,1... | collective-permute-start | bytes 442376 | tf_op jit(solution)/shard_map/ppermute | solution.py:19
  99.1 4.1 %convolution_convert_fusion = bf16[512,384]{1,0:T(8,128)(2,1)S(1)} fusion(bf16[512,3584]{1,0:T(8,128)(2,1)} %all-gather.2.cloned.1.call-done, bf16[384,3584]{1,0:T(8,128)(2,1)S(1)} %pad_maximum_fusion), kind=kOutput, calls=%fused_computation.4 | convolution fusion | flops 1409482752 | bytes 6815744 | tf_op jit(solution)/shard_map/dot_general | solution.py:31
  103.3 0.8 copy.30
  104.1 3.5 %all-to-all-start.1 = ((bf16[8,8,8,384]{3,2,1,0:T(8,128)(2,1)}), bf16[8,8,8,384]{3,2,1,0:T(8,128)(2,1)S(1)}, u32[]{:S(2)}, u32[]{:S(2)}) async-start(bf16[8,8,8,384]{3,2,1,0:T(8,128)(2,1)} %bitcast.67), calls=%async_computation.1 | async-start | bytes 786432 | tf_op jit(solution)/shard_map/all_to_all | solution.py:23
  107.6 1.2 maximum_select_fusion.1
  108.8 1.9 %collective-permute-start.5 = (bf16[2,8,24,384]{3,2,0,1:T(8,128)(2,1)S(1)}, bf16[2,8,24,384]{3,2,0,1:T(8,128)(2,1)S(1)}, u32[]{:S(2)}, u32[]{:S(2)}) collective-permute-start(bf16[2,8,24,384]{3,2,0,1:T(8,128)(2,1)S(1)} %maximum_select_fusion.1), channel_id=1, source_target_pairs={{0,1},{1,0},{2,3},{3,2},{4,5},{5,4},{6,7},{7,6},{8,9},{9,8},{10,11... | collective-permute-start | bytes 884744 | tf_op jit(solution)/shard_map/ppermute | solution.py:19
  110.7 1.2 pad_maximum_fusion.4
  112.4 6.9 %all-to-all-done.1 = bf16[8,8,8,384]{3,2,1,0:T(8,128)(2,1)S(1)} async-done(((bf16[8,8,8,384]{3,2,1,0:T(8,128)(2,1)}), bf16[8,8,8,384]{3,2,1,0:T(8,128)(2,1)S(1)}, u32[]{:S(2)}, u32[]{:S(2)}) %all-to-all-start.1) | async-done | bytes 393248 | tf_op jit(solution)/shard_map/all_to_all | solution.py:23
  119.7 18.4 %all_to_all.31 = bf16[8,2,8,768]{3,2,1,0:T(8,128)(2,1)S(1)} all-to-all(bf16[8,2,8,768]{3,2,1,0:T(8,128)(2,1)S(1)} %bitcast.77), channel_id=1, replica_groups=mesh['dp'=2,'seq'=8,'z'=8,'x'=2,'c'=2] {'seq'}, dimensions={0} | all-to-all | bytes 393216 | tf_op jit(solution)/shard_map/all_to_all | solution.py:23
  138.1 3.0 %collective-permute-start.6 = (f32[8,768]{1,0:T(8,128)S(1)}, f32[8,768]{1,0:T(8,128)S(1)}, u32[]{:S(2)}, u32[]{:S(2)}) collective-permute-start(f32[8,768]{1,0:T(8,128)S(1)} %multiply_reduce_fusion), channel_id=1, source_target_pairs={{0,256},{256,0},{1,257},{257,1},{2,258},{258,2},{3,259},{259,3},{4... | collective-permute-start | bytes 73736 | tf_op jit(solution)/shard_map/ppermute | solution.py:19
  141.2 4.2 %collective-permute-done.6 = f32[8,768]{1,0:T(8,128)S(1)} collective-permute-done((f32[8,768]{1,0:T(8,128)S(1)}, f32[8,768]{1,0:T(8,128)S(1)}, u32[]{:S(2)}, u32[]{:S(2)}) %collective-permute-start.6) | collective-permute-done | bytes 24608 | tf_op jit(solution)/shard_map/ppermute | solution.py:19
  (35 shorter events, 2.2 us)
Async XLA Ops:
  7.8 18.8 %copy-start = (bf16[2,192,896]{2,1,0:T(8,128)(2,1)S(1)}, bf16[2,192,896]{2,1,0:T(8,128)(2,1)}, u32[]{:S(2)}) copy-start(bf16[2,192,896]{2,1,0:T(8,128)(2,1)} %param.4) | copy-start | bytes 2064388
  9.6 12.6 %all-to-all-start = ((bf16[4,88,896]{2,1,0:T(8,128)(2,1)}), bf16[4,88,896]{2,1,0:T(8,128)(2,1)S(1)}, u32[]{:S(2)}, u32[]{:S(2)}) async-start(bf16[4,88,896]{2,1,0:T(8,128)(2,1)} %fusion.2), calls=%async_computation | async-start | bytes 1261568 | tf_op jit(solution)/shard_map/all_to_all | solution.py:23
  13.9 85.3 %all-gather.2.cloned.1.call-start = ((), (), s32[]{:S(2)}) async-start(), calls=%async_computation.6 | async-start | bytes 4128768 | tf_op jit(solution)/shard_map/all_gather | solution.py:62
  23.1 26.8 %collective-permute-start.2 = (bf16[384,256]{1,0:T(8,128)(2,1)}, bf16[384,256]{1,0:T(8,128)(2,1)}, u32[]{:S(2)}, u32[]{:S(2)}) collective-permute-start(bf16[384,256]{1,0:T(8,128)(2,1)} %bitcast.26.own), channel_id=1, source_target_pairs={{0,2},{2,0},{1,3},{3,1},{4,6},{6,4},{5,7},{7,5},{8,10},{10,8},{9,1... | collective-permute-start | bytes 589832 | tf_op jit(solution)/shard_map/ppermute | solution.py:19
  26.6 20.0 %collective-permute-start = (bf16[384,896]{1,0:T(8,128)(2,1)S(1)}, bf16[384,896]{1,0:T(8,128)(2,1)S(1)}, u32[]{:S(2)}, u32[]{:S(2)}) collective-permute-start(bf16[384,896]{1,0:T(8,128)(2,1)S(1)} %bitcast.69), channel_id=1, source_target_pairs={{0,2},{2,0},{1,3},{3,1},{4,6},{6,4},{5,7},{7,5},{8,10},{10,8},{9,1... | collective-permute-start | bytes 2064392 | tf_op jit(solution)/shard_map/ppermute | solution.py:19
  29.9 25.0 %all-to-all-start.2 = ((bf16[8,4,24,256]{3,2,1,0:T(8,128)(2,1)}), bf16[8,4,24,256]{3,2,1,0:T(8,128)(2,1)S(1)}, u32[]{:S(2)}, u32[]{:S(2)}) async-start(bf16[8,4,24,256]{3,2,1,0:T(8,128)(2,1)} %broadcast_in_dim.38), calls=%async_computation.2 | async-start | bytes 786432 | tf_op jit(solution)/shard_map/all_to_all | solution.py:23
  46.6 34.8 %copy-start.1 = (bf16[384,896]{1,0:T(8,128)(2,1)}, bf16[384,896]{1,0:T(8,128)(2,1)S(1)}, u32[]{:S(2)}) copy-start(bf16[384,896]{1,0:T(8,128)(2,1)S(1)} %collective-permute-done) | copy-start | bytes 2064388
  48.0 50.8 %collective-permute-start.1 = (bf16[2,384,896]{2,1,0:T(8,128)(2,1)}, bf16[2,384,896]{2,1,0:T(8,128)(2,1)S(1)}, u32[]{:S(2)}, u32[]{:S(2)}) collective-permute-start(bf16[2,384,896]{2,1,0:T(8,128)(2,1)} %pad_maximum_fusion.1), channel_id=1, source_target_pairs={{0,1},{1,0},{2,3},{3,2},{4,5},{5,4},{6,7},{7,6},{8,9},{9,8},{10,11... | collective-permute-start | bytes 4128776 | tf_op jit(solution)/shard_map/ppermute | solution.py:19
  50.9 3.9 %collective-permute-start.3 = (bf16[2,384,256]{2,1,0:T(8,128)(2,1)S(1)}, bf16[2,384,256]{2,1,0:T(8,128)(2,1)}, u32[]{:S(2)}, u32[]{:S(2)}) collective-permute-start(bf16[2,384,256]{2,1,0:T(8,128)(2,1)S(1)} %pad_maximum_fusion.3), channel_id=1, source_target_pairs={{0,1},{1,0},{2,3},{3,2},{4,5},{5,4},{6,7},{7,6},{8,9},{9,8},{10,11... | collective-permute-start | bytes 1179656 | tf_op jit(solution)/shard_map/ppermute | solution.py:19
  54.8 0.8 copy-start.3
  82.2 13.2 %all-to-all-start.4 = ((bf16[8,24,384]{2,1,0:T(8,128)(2,1)}), bf16[8,24,384]{2,1,0:T(8,128)(2,1)}, u32[]{:S(2)}, u32[]{:S(2)}) async-start(bf16[8,24,384]{2,1,0:T(8,128)(2,1)} %broadcast_in_dim.39), calls=%async_computation.4 | async-start | bytes 294912 | tf_op jit(solution)/shard_map/all_to_all | solution.py:23
  95.4 3.5 %copy-start.2 = (bf16[384,896]{1,0:T(8,128)(2,1)S(1)}, bf16[384,896]{1,0:T(8,128)(2,1)}, u32[]{:S(2)}) copy-start(bf16[384,896]{1,0:T(8,128)(2,1)} %copy-done.1) | copy-start | bytes 2064388
  95.4 12.2 %collective-permute-start.4 = (bf16[8,24,384]{2,1,0:T(8,128)(2,1)}, bf16[8,24,384]{2,1,0:T(8,128)(2,1)}, u32[]{:S(2)}, u32[]{:S(2)}) collective-permute-start(bf16[8,24,384]{2,1,0:T(8,128)(2,1)} %all-to-all-done.4), channel_id=1, source_target_pairs={{0,2},{2,0},{1,3},{3,1},{4,6},{6,4},{5,7},{7,5},{8,10},{10,8},{9,1... | collective-permute-start | bytes 442376 | tf_op jit(solution)/shard_map/ppermute | solution.py:19
  104.1 15.3 %all-to-all-start.1 = ((bf16[8,8,8,384]{3,2,1,0:T(8,128)(2,1)}), bf16[8,8,8,384]{3,2,1,0:T(8,128)(2,1)S(1)}, u32[]{:S(2)}, u32[]{:S(2)}) async-start(bf16[8,8,8,384]{3,2,1,0:T(8,128)(2,1)} %bitcast.67), calls=%async_computation.1 | async-start | bytes 786432 | tf_op jit(solution)/shard_map/all_to_all | solution.py:23
  108.8 3.5 %collective-permute-start.5 = (bf16[2,8,24,384]{3,2,0,1:T(8,128)(2,1)S(1)}, bf16[2,8,24,384]{3,2,0,1:T(8,128)(2,1)S(1)}, u32[]{:S(2)}, u32[]{:S(2)}) collective-permute-start(bf16[2,8,24,384]{3,2,0,1:T(8,128)(2,1)S(1)} %maximum_select_fusion.1), channel_id=1, source_target_pairs={{0,1},{1,0},{2,3},{3,2},{4,5},{5,4},{6,7},{7,6},{8,9},{9,8},{10,11... | collective-permute-start | bytes 884744 | tf_op jit(solution)/shard_map/ppermute | solution.py:19
  138.1 7.2 %collective-permute-start.6 = (f32[8,768]{1,0:T(8,128)S(1)}, f32[8,768]{1,0:T(8,128)S(1)}, u32[]{:S(2)}, u32[]{:S(2)}) collective-permute-start(f32[8,768]{1,0:T(8,128)S(1)} %multiply_reduce_fusion), channel_id=1, source_target_pairs={{0,256},{256,0},{1,257},{257,1},{2,258},{258,2},{3,259},{259,3},{4... | collective-permute-start | bytes 73736 | tf_op jit(solution)/shard_map/ppermute | solution.py:19
Sparse Core Ops, SparseCore 0:
  23.2 60.2 all-gather.1

commit v5 on v4

v5 whole, which is shorter than its diff:
```python
import jax
import jax.numpy as jnp
from jax import lax
from jax.experimental import pallas as pl
from jax.experimental.layout import Layout, with_layout_constraint
from jax.sharding import Mesh
from jax.experimental.pallas import tpu as pltpu
from jax.sharding import PartitionSpec as P


TENSOR = ("z", "x", "c")
SEQ_TENSOR = ("seq", "z", "x", "c")
ALL = ("dp", "seq", "z", "x", "c")
F32 = jnp.float32
BF16 = jnp.bfloat16


def exchange(v, axis):
    return lax.ppermute(v, axis, [(0, 1), (1, 0)])


def all_to_all(v, axis):
    return lax.all_to_all(v, axis, 0, 0, tiled=True)


def to_everyone(v, axis):
    return all_to_all(jnp.broadcast_to(v[None], (lax.axis_size(axis), *v.shape)), axis)


def contract_last(a, b):
    return lax.dot_general(
        a, b, (((a.ndim - 1,), (b.ndim - 1,)), ((), ())), preferred_element_type=F32
    )


def to_owner(v, across):
    pairs = []
    for d in range(2):
        for pair in range(4):
            for a in range(2):
                for b in range(2):
                    source = (d * 8 + pair * 2 + b) * 2 + a
                    pairs.append((source, ((d ^ across) * 8 + pair * 2 + a) * 2 + b))
    return lax.ppermute(v, ("dp", "seq", "x"), pairs)


def grad_kernel(place, cols, own, beside, pair, out):
    rows = cols.shape[0] * cols.shape[2]
    found = jnp.zeros(out.shape, F32)
    for k, features in enumerate((own[...], pair[0], beside[...], pair[1])):
        columns = cols[:, pl.ds(place[k], 1)].astype(F32).reshape(rows, -1).astype(BF16)
        found = found + contract_last(columns, features)
    out[...] = found


def body(activations, gradients, basis_in, basis_out):
    d = lax.axis_index("dp")
    x = lax.axis_index("x")
    c = lax.axis_index("c")
    seqs, length, width = activations.shape
    tokens = seqs * length
    x_own = activations.reshape(tokens, width)
    narrow = basis_out.shape[0]
    g_own = gradients.reshape(tokens, narrow)

    shard = with_layout_constraint(basis_in.T, Layout(major_to_minor=(0, 1)))
    shard = shard.reshape(8, 4, 8, width)
    half = lax.dynamic_index_in_dim(shard, d * 2 + c, 1, keepdims=False).reshape(64, width)
    other = lax.dynamic_index_in_dim(shard, d * 2 + 1 - c, 1, keepdims=False).reshape(64, width)
    partner = exchange(other, "c")
    block = jnp.concatenate([half, partner], 1)
    columns = lax.all_gather(block, "seq", axis=0, tiled=True)
    x_far = exchange(x_own, "dp")

    spread = jnp.broadcast_to(basis_out.T.reshape(1, 4, 24, narrow), (8, 4, 24, narrow))
    out_cols = all_to_all(spread.reshape(32, 24, narrow), ("seq", "x", "c"))
    out_cols = out_cols.reshape(8, 4, 24, narrow)
    g_beside = exchange(g_own, "x")
    g_pair = exchange(jnp.stack([g_own, g_beside]), "c")

    place = (x * 2 + c) ^ jnp.arange(4, dtype=jnp.int32)
    grad_partial = pl.pallas_call(
        grad_kernel,
        in_specs=[pl.BlockSpec(memory_space=pltpu.SMEM)]
        + [pl.BlockSpec(memory_space=pltpu.VMEM)] * 4,
        out_specs=pl.BlockSpec(memory_space=pltpu.VMEM),
        out_shape=jax.ShapeDtypeStruct((8 * 24, tokens), F32),
    )(place, out_cols, g_own, g_beside, g_pair)
    grad_parts = all_to_all(grad_partial.reshape(8, 24, tokens), "z")
    grad_parts, x_far = lax.optimization_barrier((grad_parts, x_far))
    x_rows = jnp.concatenate([x_own, x_far], 0)
    x_other = exchange(x_rows, "c")
    grad_own = grad_parts.sum(0).astype(BF16)
    grad_quarter = to_everyone(grad_own, "z")
    rest = exchange(grad_quarter, "x")
    grad_half = jnp.where(x == 0, jnp.stack([grad_quarter, rest]), jnp.stack([rest, grad_quarter]))
    rest = exchange(grad_half, "c")
    grads = jnp.where(c == 0, jnp.stack([grad_half, rest]), jnp.stack([rest, grad_half]))
    grads = grads.transpose(2, 1, 0, 3, 4).reshape(-1, tokens)

    x_rows = lax.optimization_barrier(jnp.concatenate([x_rows, x_other], 1))
    parts = contract_last(columns, x_rows).astype(BF16)
    parts = parts.reshape(4, 2, 8, 8, -1).transpose(2, 1, 0, 3, 4)
    arrived = all_to_all(parts.reshape(16, 4, 8, -1), ("z", "x"))
    act = arrived.astype(F32).sum(0).astype(BF16).reshape(32, -1)

    mine = act[:, :tokens]
    theirs = exchange(act[:, tokens:], "dp")
    act = jnp.where(d == 0, jnp.stack([mine, theirs]), jnp.stack([theirs, mine]))
    act = act.reshape(2, 4, 8, tokens).swapaxes(0, 1).reshape(64, tokens)

    of_seq = lax.broadcasted_iota(jnp.int32, (seqs, 1, tokens), 2) // length
    chosen = of_seq == lax.broadcasted_iota(jnp.int32, (seqs, 1, tokens), 0)
    masked = jnp.where(chosen, act[None], jnp.zeros((), BF16))
    partial_blocks = contract_last(masked, grads)
    pieces = partial_blocks.astype(BF16).reshape(seqs, 8, 8, -1).swapaxes(0, 1)
    blocks = all_to_all(pieces, "seq").astype(F32).sum(0)
    squared = jnp.sum(blocks * blocks, axis=0)
    near, far = (to_owner(squared, across) for across in (0, 1))
    return (near + far) / (2 * seqs * 8 * length)


def solution(mesh):
    finer = Mesh(mesh.devices.reshape(2, 8, 8, 2, 2), ALL)
    in_specs = (P("dp", "seq", TENSOR), P("dp", "seq", TENSOR), P(TENSOR, "seq"), P(TENSOR, "seq"))
    out_specs = P(SEQ_TENSOR, None)

    return jax.shard_map(body, mesh=finer, in_specs=in_specs, out_specs=out_specs, check_vma=False)
```

time: 154 us -> 155 us (level)
  the two profiles are of different devices: /device:TPU:6 before, /device:TPU:8 now
where the time goes in v5:
time: 155 us; the launch traced here: 154 us
  starting transfers between devices  54.8 us (35%)
  waiting for transfers between devices  52.1 us (34%)
  blocking collectives  15.5 us (10%)
  between operations  13.7 us (9%)
  other arithmetic  6.2 us (4%)
  local copies, waits for them, and re-layouts  5.5 us (4%)
  matrix products  3.43 us (2%)
  Pallas kernels  2.45 us (2%)
    all_to_all x4, starting transfers between devices, all_to_all(): return lax.all_to_all(v, axis, 0, 0, tiled=True)  27.1 us
    all_to_all x4, waiting for transfers between devices, all_to_all(): return lax.all_to_all(v, axis, 0, 0, tiled=True)  25.8 us
    ppermute x8, starting transfers between devices, exchange(): return lax.ppermute(v, axis, [(0, 1), (1, 0)])  21.5 us
    ppermute x8, waiting for transfers between devices, exchange(): return lax.ppermute(v, axis, [(0, 1), (1, 0)])  21.1 us
    all_to_all x1, blocking collectives, all_to_all(): return lax.all_to_all(v, axis, 0, 0, tiled=True)  15.5 us
    ppermute x2, starting transfers between devices, to_owner(): return lax.ppermute(v, ('dp', 'seq', 'x'), pairs)  6.16 us
    ppermute x2, waiting for transfers between devices, to_owner(): return lax.ppermute(v, ('dp', 'seq', 'x'), pairs)  5.07 us
    dot_general x2, matrix products, contract_last(): lax.dot_general(a, b, (((a.ndim - 1,), (b.ndim - 1,)), ((), ())), preferr...  3.43 us
  transfers between devices with their start and end apart: 15, of which 10 were waited for; matrix products, arithmetic and copies ran while one was open for 7% of the time, Pallas kernels for 2%

profile of v5, /device:TPU:8, one launch (start us, length us, event | category | flops | bytes accessed | tf_op | source)
XLA Modules:
  0.0 153.7 jit_solution(7561721567389831865)
XLA Ops:
  6.5 1.3 copy.17
  7.9 1.9 %collective-permute-start = (bf16[64,896]{1,0:T(8,128)(2,1)S(1)}, bf16[64,896]{1,0:T(8,128)(2,1)S(1)}, u32[]{:S(2)}, u32[]{:S(2)}) collective-permute-start(bf16[64,896]{1,0:T(8,128)(2,1)S(1)} %get-tuple-element.10), channel_id=1, source_target_pairs={{0,1},{1,0},{2,3},{3,2},{4,5},{5,4},{6,7},{7,6},{8,9},{9,8},{10,11... | collective-permute-start | bytes 344072 | tf_op jit(solution)/shard_map/ppermute | solution.py:19
  9.8 1.3 collective-permute-done
  11.9 1.6 %broadcast_in_dim.37 = bf16[8,4,24,256]{3,2,1,0:T(8,128)(2,1)} broadcast(bf16[4,24,256]{2,1,0:T(8,128)(2,1)} %bitcast.64), dimensions={1,2,3} | broadcast | bytes 442368 | tf_op jit(solution)/shard_map/broadcast_in_dim | solution.py:75
  13.4 9.3 %all-to-all-start = ((bf16[32,24,256]{2,1,0:T(8,128)(2,1)}), bf16[32,24,256]{2,1,0:T(8,128)(2,1)S(1)}, u32[]{:S(2)}, u32[]{:S(2)}) async-start(bf16[32,24,256]{2,1,0:T(8,128)(2,1)} %bitcast.8), calls=%async_computation | async-start | bytes 786432 | tf_op jit(solution)/shard_map/all_to_all | solution.py:23
  22.8 3.4 %collective-permute-start.1 = (bf16[384,256]{1,0:T(8,128)(2,1)S(1)}, bf16[384,256]{1,0:T(8,128)(2,1)S(1)}, u32[]{:S(2)}, u32[]{:S(2)}) collective-permute-start(bf16[384,256]{1,0:T(8,128)(2,1)S(1)} %bitcast.56), channel_id=1, source_target_pairs={{0,2},{2,0},{1,3},{3,1},{4,6},{6,4},{5,7},{7,5},{8,10},{10,8},{9,1... | collective-permute-start | bytes 589832 | tf_op jit(solution)/shard_map/ppermute | solution.py:19
  26.2 8.1 %collective-permute-done.1.beside = bf16[384,256]{1,0:T(8,128)(2,1)S(1)} collective-permute-done((bf16[384,256]{1,0:T(8,128)(2,1)S(1)}, bf16[384,256]{1,0:T(8,128)(2,1)S(1)}, u32[]{:S(2)}, u32[]{:S(2)}) %collective-permute-start.1) | collective-permute-done | bytes 196640 | tf_op jit(solution)/shard_map/ppermute | solution.py:19
  34.3 1.9 %collective-permute-start.2 = (bf16[2,384,256]{2,1,0:T(8,128)(2,1)S(1)}, bf16[2,384,256]{2,1,0:T(8,128)(2,1)S(1)}, u32[]{:S(2)}, u32[]{:S(2)}) collective-permute-start(bf16[2,384,256]{2,1,0:T(8,128)(2,1)S(1)} %pad_maximum_fusion.2), channel_id=1, source_target_pairs={{0,1},{1,0},{2,3},{3,2},{4,5},{5,4},{6,7},{7,6},{8,9},{9,8},{10,11... | collective-permute-start | bytes 1179656 | tf_op jit(solution)/shard_map/ppermute | solution.py:19
  36.2 3.9 %collective-permute-start.3 = (bf16[384,896]{1,0:T(8,128)(2,1)S(1)}, bf16[384,896]{1,0:T(8,128)(2,1)S(1)}, u32[]{:S(2)}, u32[]{:S(2)}) collective-permute-start(bf16[384,896]{1,0:T(8,128)(2,1)S(1)} %bitcast.46), channel_id=1, source_target_pairs={{0,256},{256,0},{1,257},{257,1},{2,258},{258,2},{3,259},{259,3},{4... | collective-permute-start | bytes 2064392 | tf_op jit(solution)/shard_map/ppermute | solution.py:19
  41.6 2.4 %shard_map.46 = f32[192,384]{1,0:T(8,128)} custom-call(s32[4]{0:T(128)} %iota_xor_fusion.place, bf16[8,4,24,256]{3,2,1,0:T(8,128)(2,1)} %bitcast.50, bf16[384,256]{1,0:T(8,128)(2,1)} %bitcast.55, bf16[384,256]{1,0:T(8,128)(2,1)} %copy-done.4, bf16[2,384,256]{2,1,0:T(8,128)(2,1)} %copy-done.5), custom_call_target="tpu_custom_call" | custom-call | tf_op jit(solution)/shard_map/pallas_call | solution.py:82
  44.0 10.2 %all-to-all-start.1 = ((f32[8,24,384]{2,1,0:T(8,128)}), f32[8,24,384]{2,1,0:T(8,128)S(1)}, u32[]{:S(2)}, u32[]{:S(2)}) async-start(f32[8,24,384]{2,1,0:T(8,128)} %bitcast.51), calls=%async_computation.1 | async-start | bytes 589824 | tf_op jit(solution)/shard_map/all_to_all | solution.py:23
  54.2 3.3 %collective-permute-done.3 = bf16[384,896]{1,0:T(8,128)(2,1)S(1)} collective-permute-done((bf16[384,896]{1,0:T(8,128)(2,1)S(1)}, bf16[384,896]{1,0:T(8,128)(2,1)S(1)}, u32[]{:S(2)}, u32[]{:S(2)}) %collective-permute-start.3) | collective-permute-done | bytes 688160 | tf_op jit(solution)/shard_map/ppermute | solution.py:19
  57.5 9.7 %all-to-all-done.1 = f32[8,24,384]{2,1,0:T(8,128)S(1)} async-done(((f32[8,24,384]{2,1,0:T(8,128)}), f32[8,24,384]{2,1,0:T(8,128)S(1)}, u32[]{:S(2)}, u32[]{:S(2)}) %all-to-all-start.1) | async-done | bytes 294944 | tf_op jit(solution)/shard_map/all_to_all | solution.py:23
  67.3 1.9 %collective-permute-start.4 = (bf16[768,896]{1,0:T(8,128)(2,1)S(1)}, bf16[768,896]{1,0:T(8,128)(2,1)}, u32[]{:S(2)}, u32[]{:S(2)}) collective-permute-start(bf16[768,896]{1,0:T(8,128)(2,1)S(1)} %pad_maximum_fusion.1), channel_id=1, source_target_pairs={{0,1},{1,0},{2,3},{3,2},{4,5},{5,4},{6,7},{7,6},{8,9},{9,8},{10,11... | collective-permute-start | bytes 4128776 | tf_op jit(solution)/shard_map/ppermute | solution.py:19
  69.9 4.0 %all-to-all-start.3 = ((bf16[8,24,384]{2,1,0:T(8,128)(2,1)}), bf16[8,24,384]{2,1,0:T(8,128)(2,1)}, u32[]{:S(2)}, u32[]{:S(2)}) async-start(bf16[8,24,384]{2,1,0:T(8,128)(2,1)} %broadcast_in_dim.41), calls=%async_computation.3 | async-start | bytes 294912 | tf_op jit(solution)/shard_map/all_to_all | solution.py:23
  73.9 1.7 %pad_maximum_fusion = bf16[768,1792]{1,0:T(8,128)(2,1)S(1)} fusion(bf16[768,896]{1,0:T(8,128)(2,1)} %collective-permute-done.4, bf16[384,896]{1,0:T(8,128)(2,1)} %copy-done.1, bf16[384,896]{1,0:T(8,128)(2,1)S(1)} %bitcast.48), kind=kLoop, calls=%fused_computation | loop fusion | flops 8257536 | bytes 5505024 | tf_op jit(solution)/shard_map/concatenate | solution.py:101
  75.7 3.1 %convolution_convert_fusion = bf16[512,768]{1,0:T(8,128)(2,1)S(1)} fusion(bf16[512,1792]{1,0:T(8,128)(2,1)} %all-gather.2.cloned.1.call-done, bf16[768,1792]{1,0:T(8,128)(2,1)S(1)} %pad_maximum_fusion), kind=kOutput, calls=%fused_computation.1 | convolution fusion | flops 1409679360 | bytes 5373952 | tf_op jit(solution)/shard_map/dot_general | solution.py:31
  78.8 1.0 copy.18
  79.8 4.5 %all-to-all-done.3 = bf16[8,24,384]{2,1,0:T(8,128)(2,1)} async-done(((bf16[8,24,384]{2,1,0:T(8,128)(2,1)}), bf16[8,24,384]{2,1,0:T(8,128)(2,1)}, u32[]{:S(2)}, u32[]{:S(2)}) %all-to-all-start.3) | async-done | bytes 147488 | tf_op jit(solution)/shard_map/all_to_all | solution.py:23
  84.3 3.6 %all-to-all-start.2 = ((bf16[16,4,8,768]{3,2,1,0:T(8,128)(2,1)}), bf16[16,4,8,768]{3,2,1,0:T(8,128)(2,1)S(1)}, u32[]{:S(2)}, u32[]{:S(2)}) async-start(bf16[16,4,8,768]{3,2,1,0:T(8,128)(2,1)} %bitcast.16), calls=%async_computation.2 | async-start | bytes 1572864 | tf_op jit(solution)/shard_map/all_to_all | solution.py:23
  87.9 3.7 %collective-permute-start.6 = (bf16[8,24,384]{2,1,0:T(8,128)(2,1)}, bf16[8,24,384]{2,1,0:T(8,128)(2,1)S(1)}, u32[]{:S(2)}, u32[]{:S(2)}) collective-permute-start(bf16[8,24,384]{2,1,0:T(8,128)(2,1)} %all-to-all-done.3), channel_id=1, source_target_pairs={{0,2},{2,0},{1,3},{3,1},{4,6},{6,4},{5,7},{7,5},{8,10},{10,8},{9,1... | collective-permute-start | bytes 442376 | tf_op jit(solution)/shard_map/ppermute | solution.py:19
  91.6 4.3 %collective-permute-done.6 = bf16[8,24,384]{2,1,0:T(8,128)(2,1)S(1)} collective-permute-done((bf16[8,24,384]{2,1,0:T(8,128)(2,1)}, bf16[8,24,384]{2,1,0:T(8,128)(2,1)S(1)}, u32[]{:S(2)}, u32[]{:S(2)}) %collective-permute-start.6) | collective-permute-done | bytes 147488 | tf_op jit(solution)/shard_map/ppermute | solution.py:19
  95.9 1.1 maximum_select_fusion.1
  97.0 1.9 %collective-permute-start.7 = (bf16[2,8,24,384]{3,2,0,1:T(8,128)(2,1)S(1)}, bf16[2,8,24,384]{3,2,0,1:T(8,128)(2,1)S(1)}, u32[]{:S(2)}, u32[]{:S(2)}) collective-permute-start(bf16[2,8,24,384]{3,2,0,1:T(8,128)(2,1)S(1)} %maximum_select_fusion.1), channel_id=1, source_target_pairs={{0,1},{1,0},{2,3},{3,2},{4,5},{5,4},{6,7},{7,6},{8,9},{9,8},{10,11... | collective-permute-start | bytes 884744 | tf_op jit(solution)/shard_map/ppermute | solution.py:19
  98.9 1.1 pad_maximum_fusion.3
  100.0 11.6 %all-to-all-done.2 = bf16[16,4,8,768]{3,2,1,0:T(8,128)(2,1)S(1)} async-done(((bf16[16,4,8,768]{3,2,1,0:T(8,128)(2,1)}), bf16[16,4,8,768]{3,2,1,0:T(8,128)(2,1)S(1)}, u32[]{:S(2)}, u32[]{:S(2)}) %all-to-all-start.2) | async-done | bytes 786464 | tf_op jit(solution)/shard_map/all_to_all | solution.py:23
  111.8 2.8 %collective-permute-start.5 = (bf16[32,384]{1,0:T(8,128)(2,1)S(1)}, bf16[32,384]{1,0:T(8,128)(2,1)S(1)}, u32[]{:S(2)}, u32[]{:S(2)}) collective-permute-start(bf16[32,384]{1,0:T(8,128)(2,1)S(1)} %get-tuple-element.14), channel_id=1, source_target_pairs={{0,256},{256,0},{1,257},{257,1},{2,258},{258,2},{3,259},{259,3},{4... | collective-permute-start | bytes 73736 | tf_op jit(solution)/shard_map/ppermute | solution.py:19
  114.8 4.2 %collective-permute-done.5 = bf16[32,384]{1,0:T(8,128)(2,1)S(1)} collective-permute-done((bf16[32,384]{1,0:T(8,128)(2,1)S(1)}, bf16[32,384]{1,0:T(8,128)(2,1)S(1)}, u32[]{:S(2)}, u32[]{:S(2)}) %collective-permute-start.5) | collective-permute-done | bytes 24608 | tf_op jit(solution)/shard_map/ppermute | solution.py:19
  119.4 15.5 %all_to_all.25 = bf16[8,2,8,768]{3,2,1,0:T(8,128)(2,1)S(1)} all-to-all(bf16[8,2,8,768]{3,2,1,0:T(8,128)(2,1)S(1)} %bitcast.54), channel_id=1, replica_groups=mesh['dp'=2,'seq'=8,'z'=8,'x'=2,'c'=2] {'seq'}, dimensions={0} | all-to-all | bytes 393216 | tf_op jit(solution)/shard_map/all_to_all | solution.py:23
  135.0 3.4 %collective-permute-start.8 = (f32[8,768]{1,0:T(8,128)S(1)}, f32[8,768]{1,0:T(8,128)S(1)}, u32[]{:S(2)}, u32[]{:S(2)}) collective-permute-start(f32[8,768]{1,0:T(8,128)S(1)} %multiply_reduce_fusion), channel_id=1, source_target_pairs={{0,0},{32,2},{2,32},{34,34},{64,64},{96,66},{66,96},{98,98},{128,1... | collective-permute-start | bytes 73736 | tf_op jit(solution)/shard_map/ppermute | solution.py:44
  138.4 2.8 %collective-permute-start.9 = (f32[8,768]{1,0:T(8,128)S(1)}, f32[8,768]{1,0:T(8,128)S(1)}, u32[]{:S(2)}, u32[]{:S(2)}) collective-permute-start(f32[8,768]{1,0:T(8,128)S(1)} %multiply_reduce_fusion), channel_id=1, source_target_pairs={{0,256},{32,258},{2,288},{34,290},{64,320},{96,322},{66,352},{98,3... | collective-permute-start | bytes 73736 | tf_op jit(solution)/shard_map/ppermute | solution.py:44
  141.6 4.6 %collective-permute-done.9 = f32[8,768]{1,0:T(8,128)S(1)} collective-permute-done((f32[8,768]{1,0:T(8,128)S(1)}, f32[8,768]{1,0:T(8,128)S(1)}, u32[]{:S(2)}, u32[]{:S(2)}) %collective-permute-start.9) | collective-permute-done | bytes 24608 | tf_op jit(solution)/shard_map/ppermute | solution.py:44
  (40 shorter events, 4.8 us)
Async XLA Ops:
  6.5 16.3 %copy-start.3 = (bf16[2,192,256]{2,1,0:T(8,128)(2,1)S(1)}, bf16[2,192,256]{2,1,0:T(8,128)(2,1)}, u32[]{:S(2)}) copy-start(bf16[2,192,256]{2,1,0:T(8,128)(2,1)} %param.5) | copy-start | bytes 589828
  6.5 29.7 %copy-start = (bf16[2,192,896]{2,1,0:T(8,128)(2,1)S(1)}, bf16[2,192,896]{2,1,0:T(8,128)(2,1)}, u32[]{:S(2)}) copy-start(bf16[2,192,896]{2,1,0:T(8,128)(2,1)} %param.4) | copy-start | bytes 2064388
  6.5 69.1 %all-gather.2.cloned.1.call-start = ((), (), s32[]{:S(2)}) async-start(), calls=%async_computation.5 | async-start | bytes 2064384 | tf_op jit(solution)/shard_map/all_gather | solution.py:72
  7.9 3.2 %collective-permute-start = (bf16[64,896]{1,0:T(8,128)(2,1)S(1)}, bf16[64,896]{1,0:T(8,128)(2,1)S(1)}, u32[]{:S(2)}, u32[]{:S(2)}) collective-permute-start(bf16[64,896]{1,0:T(8,128)(2,1)S(1)} %get-tuple-element.10), channel_id=1, source_target_pairs={{0,1},{1,0},{2,3},{3,2},{4,5},{5,4},{6,7},{7,6},{8,9},{9,8},{10,11... | collective-permute-start | bytes 344072 | tf_op jit(solution)/shard_map/ppermute | solution.py:19
  13.4 27.3 %all-to-all-start = ((bf16[32,24,256]{2,1,0:T(8,128)(2,1)}), bf16[32,24,256]{2,1,0:T(8,128)(2,1)S(1)}, u32[]{:S(2)}, u32[]{:S(2)}) async-start(bf16[32,24,256]{2,1,0:T(8,128)(2,1)} %bitcast.8), calls=%async_computation | async-start | bytes 786432 | tf_op jit(solution)/shard_map/all_to_all | solution.py:23
  22.8 11.5 %collective-permute-start.1 = (bf16[384,256]{1,0:T(8,128)(2,1)S(1)}, bf16[384,256]{1,0:T(8,128)(2,1)S(1)}, u32[]{:S(2)}, u32[]{:S(2)}) collective-permute-start(bf16[384,256]{1,0:T(8,128)(2,1)S(1)} %bitcast.56), channel_id=1, source_target_pairs={{0,2},{2,0},{1,3},{3,1},{4,6},{6,4},{5,7},{7,5},{8,10},{10,8},{9,1... | collective-permute-start | bytes 589832 | tf_op jit(solution)/shard_map/ppermute | solution.py:19
  34.3 6.5 %copy-start.4 = (bf16[384,256]{1,0:T(8,128)(2,1)}, bf16[384,256]{1,0:T(8,128)(2,1)S(1)}, u32[]{:S(2)}) copy-start(bf16[384,256]{1,0:T(8,128)(2,1)S(1)} %collective-permute-done.1.beside) | copy-start | bytes 589828
  34.3 6.4 %collective-permute-start.2 = (bf16[2,384,256]{2,1,0:T(8,128)(2,1)S(1)}, bf16[2,384,256]{2,1,0:T(8,128)(2,1)S(1)}, u32[]{:S(2)}, u32[]{:S(2)}) collective-permute-start(bf16[2,384,256]{2,1,0:T(8,128)(2,1)S(1)} %pad_maximum_fusion.2), channel_id=1, source_target_pairs={{0,1},{1,0},{2,3},{3,2},{4,5},{5,4},{6,7},{7,6},{8,9},{9,8},{10,11... | collective-permute-start | bytes 1179656 | tf_op jit(solution)/shard_map/ppermute | solution.py:19
  36.2 21.2 %collective-permute-start.3 = (bf16[384,896]{1,0:T(8,128)(2,1)S(1)}, bf16[384,896]{1,0:T(8,128)(2,1)S(1)}, u32[]{:S(2)}, u32[]{:S(2)}) collective-permute-start(bf16[384,896]{1,0:T(8,128)(2,1)S(1)} %bitcast.46), channel_id=1, source_target_pairs={{0,256},{256,0},{1,257},{257,1},{2,258},{258,2},{3,259},{259,3},{4... | collective-permute-start | bytes 2064392 | tf_op jit(solution)/shard_map/ppermute | solution.py:19
  40.7 0.7 copy-start.5
  40.7 0.9 copy-start.2
  44.0 23.1 %all-to-all-start.1 = ((f32[8,24,384]{2,1,0:T(8,128)}), f32[8,24,384]{2,1,0:T(8,128)S(1)}, u32[]{:S(2)}, u32[]{:S(2)}) async-start(f32[8,24,384]{2,1,0:T(8,128)} %bitcast.51), calls=%async_computation.1 | async-start | bytes 589824 | tf_op jit(solution)/shard_map/all_to_all | solution.py:23
  57.5 16.4 %copy-start.1 = (bf16[384,896]{1,0:T(8,128)(2,1)}, bf16[384,896]{1,0:T(8,128)(2,1)S(1)}, u32[]{:S(2)}) copy-start(bf16[384,896]{1,0:T(8,128)(2,1)S(1)} %collective-permute-done.3) | copy-start | bytes 2064388
  67.3 6.7 %collective-permute-start.4 = (bf16[768,896]{1,0:T(8,128)(2,1)S(1)}, bf16[768,896]{1,0:T(8,128)(2,1)}, u32[]{:S(2)}, u32[]{:S(2)}) collective-permute-start(bf16[768,896]{1,0:T(8,128)(2,1)S(1)} %pad_maximum_fusion.1), channel_id=1, source_target_pairs={{0,1},{1,0},{2,3},{3,2},{4,5},{5,4},{6,7},{7,6},{8,9},{9,8},{10,11... | collective-permute-start | bytes 4128776 | tf_op jit(solution)/shard_map/ppermute | solution.py:19
  69.9 14.4 %all-to-all-start.3 = ((bf16[8,24,384]{2,1,0:T(8,128)(2,1)}), bf16[8,24,384]{2,1,0:T(8,128)(2,1)}, u32[]{:S(2)}, u32[]{:S(2)}) async-start(bf16[8,24,384]{2,1,0:T(8,128)(2,1)} %broadcast_in_dim.41), calls=%async_computation.3 | async-start | bytes 294912 | tf_op jit(solution)/shard_map/all_to_all | solution.py:23
  84.3 27.4 %all-to-all-start.2 = ((bf16[16,4,8,768]{3,2,1,0:T(8,128)(2,1)}), bf16[16,4,8,768]{3,2,1,0:T(8,128)(2,1)S(1)}, u32[]{:S(2)}, u32[]{:S(2)}) async-start(bf16[16,4,8,768]{3,2,1,0:T(8,128)(2,1)} %bitcast.16), calls=%async_computation.2 | async-start | bytes 1572864 | tf_op jit(solution)/shard_map/all_to_all | solution.py:23
  87.9 8.0 %collective-permute-start.6 = (bf16[8,24,384]{2,1,0:T(8,128)(2,1)}, bf16[8,24,384]{2,1,0:T(8,128)(2,1)S(1)}, u32[]{:S(2)}, u32[]{:S(2)}) collective-permute-start(bf16[8,24,384]{2,1,0:T(8,128)(2,1)} %all-to-all-done.3), channel_id=1, source_target_pairs={{0,2},{2,0},{1,3},{3,1},{4,6},{6,4},{5,7},{7,5},{8,10},{10,8},{9,1... | collective-permute-start | bytes 442376 | tf_op jit(solution)/shard_map/ppermute | solution.py:19
  97.0 17.6 %collective-permute-start.7 = (bf16[2,8,24,384]{3,2,0,1:T(8,128)(2,1)S(1)}, bf16[2,8,24,384]{3,2,0,1:T(8,128)(2,1)S(1)}, u32[]{:S(2)}, u32[]{:S(2)}) collective-permute-start(bf16[2,8,24,384]{3,2,0,1:T(8,128)(2,1)S(1)} %maximum_select_fusion.1), channel_id=1, source_target_pairs={{0,1},{1,0},{2,3},{3,2},{4,5},{5,4},{6,7},{7,6},{8,9},{9,8},{10,11... | collective-permute-start | bytes 884744 | tf_op jit(solution)/shard_map/ppermute | solution.py:19
  111.8 7.2 %collective-permute-start.5 = (bf16[32,384]{1,0:T(8,128)(2,1)S(1)}, bf16[32,384]{1,0:T(8,128)(2,1)S(1)}, u32[]{:S(2)}, u32[]{:S(2)}) collective-permute-start(bf16[32,384]{1,0:T(8,128)(2,1)S(1)} %get-tuple-element.14), channel_id=1, source_target_pairs={{0,256},{256,0},{1,257},{257,1},{2,258},{258,2},{3,259},{259,3},{4... | collective-permute-start | bytes 73736 | tf_op jit(solution)/shard_map/ppermute | solution.py:19
  135.0 6.6 %collective-permute-start.8 = (f32[8,768]{1,0:T(8,128)S(1)}, f32[8,768]{1,0:T(8,128)S(1)}, u32[]{:S(2)}, u32[]{:S(2)}) collective-permute-start(f32[8,768]{1,0:T(8,128)S(1)} %multiply_reduce_fusion), channel_id=1, source_target_pairs={{0,0},{32,2},{2,32},{34,34},{64,64},{96,66},{66,96},{98,98},{128,1... | collective-permute-start | bytes 73736 | tf_op jit(solution)/shard_map/ppermute | solution.py:44
  138.4 7.8 %collective-permute-start.9 = (f32[8,768]{1,0:T(8,128)S(1)}, f32[8,768]{1,0:T(8,128)S(1)}, u32[]{:S(2)}, u32[]{:S(2)}) collective-permute-start(f32[8,768]{1,0:T(8,128)S(1)} %multiply_reduce_fusion), channel_id=1, source_target_pairs={{0,256},{32,258},{2,288},{34,290},{64,320},{96,322},{66,352},{98,3... | collective-permute-start | bytes 73736 | tf_op jit(solution)/shard_map/ppermute | solution.py:44
Sparse Core Ops, SparseCore 0:
  12.0 48.4 all-gather.1

commit v6 on v5

--- a/solution.py
+++ b/solution.py
@@ -33,17 +33,6 @@
     )
 
 
-def to_owner(v, across):
-    pairs = []
-    for d in range(2):
-        for pair in range(4):
-            for a in range(2):
-                for b in range(2):
-                    source = (d * 8 + pair * 2 + b) * 2 + a
-                    pairs.append((source, ((d ^ across) * 8 + pair * 2 + a) * 2 + b))
-    return lax.ppermute(v, ("dp", "seq", "x"), pairs)
-
-
 def grad_kernel(place, cols, own, beside, pair, out):
     rows = cols.shape[0] * cols.shape[2]
     found = jnp.zeros(out.shape, F32)
@@ -54,7 +43,6 @@
 
 
 def body(activations, gradients, basis_in, basis_out):
-    d = lax.axis_index("dp")
     x = lax.axis_index("x")
     c = lax.axis_index("c")
     seqs, length, width = activations.shape
@@ -64,13 +52,13 @@
     g_own = gradients.reshape(tokens, narrow)
 
     shard = with_layout_constraint(basis_in.T, Layout(major_to_minor=(0, 1)))
-    shard = shard.reshape(8, 4, 8, width)
-    half = lax.dynamic_index_in_dim(shard, d * 2 + c, 1, keepdims=False).reshape(64, width)
-    other = lax.dynamic_index_in_dim(shard, d * 2 + 1 - c, 1, keepdims=False).reshape(64, width)
+    shard = shard.reshape(16, 2, 8, width)
+    half = lax.dynamic_index_in_dim(shard, c, 1, keepdims=False).reshape(128, width)
+    other = lax.dynamic_index_in_dim(shard, 1 - c, 1, keepdims=False).reshape(128, width)
     partner = exchange(other, "c")
     block = jnp.concatenate([half, partner], 1)
     columns = lax.all_gather(block, "seq", axis=0, tiled=True)
-    x_far = exchange(x_own, "dp")
+    x_other = exchange(x_own, "c")
 
     spread = jnp.broadcast_to(basis_out.T.reshape(1, 4, 24, narrow), (8, 4, 24, narrow))
     out_cols = all_to_all(spread.reshape(32, 24, narrow), ("seq", "x", "c"))
@@ -87,9 +75,6 @@
         out_shape=jax.ShapeDtypeStruct((8 * 24, tokens), F32),
     )(place, out_cols, g_own, g_beside, g_pair)
     grad_parts = all_to_all(grad_partial.reshape(8, 24, tokens), "z")
-    grad_parts, x_far = lax.optimization_barrier((grad_parts, x_far))
-    x_rows = jnp.concatenate([x_own, x_far], 0)
-    x_other = exchange(x_rows, "c")
     grad_own = grad_parts.sum(0).astype(BF16)
     grad_quarter = to_everyone(grad_own, "z")
     rest = exchange(grad_quarter, "x")
@@ -98,16 +83,11 @@
     grads = jnp.where(c == 0, jnp.stack([grad_half, rest]), jnp.stack([rest, grad_half]))
     grads = grads.transpose(2, 1, 0, 3, 4).reshape(-1, tokens)
 
-    x_rows = lax.optimization_barrier(jnp.concatenate([x_rows, x_other], 1))
+    x_rows = lax.optimization_barrier(jnp.concatenate([x_own, x_other], 1))
     parts = contract_last(columns, x_rows).astype(BF16)
-    parts = parts.reshape(4, 2, 8, 8, -1).transpose(2, 1, 0, 3, 4)
-    arrived = all_to_all(parts.reshape(16, 4, 8, -1), ("z", "x"))
-    act = arrived.astype(F32).sum(0).astype(BF16).reshape(32, -1)
-
-    mine = act[:, :tokens]
-    theirs = exchange(act[:, tokens:], "dp")
-    act = jnp.where(d == 0, jnp.stack([mine, theirs]), jnp.stack([theirs, mine]))
-    act = act.reshape(2, 4, 8, tokens).swapaxes(0, 1).reshape(64, tokens)
+    parts = parts.reshape(8, 8, 2, 8, tokens).transpose(2, 1, 0, 3, 4).reshape(16, 8, 8, tokens)
+    arrived = all_to_all(parts, ("x", "z"))
+    act = arrived.astype(F32).sum(0).astype(BF16).reshape(64, tokens)
 
     of_seq = lax.broadcasted_iota(jnp.int32, (seqs, 1, tokens), 2) // length
     chosen = of_seq == lax.broadcasted_iota(jnp.int32, (seqs, 1, tokens), 0)
@@ -116,8 +96,8 @@
     pieces = partial_blocks.astype(BF16).reshape(seqs, 8, 8, -1).swapaxes(0, 1)
     blocks = all_to_all(pieces, "seq").astype(F32).sum(0)
     squared = jnp.sum(blocks * blocks, axis=0)
-    near, far = (to_owner(squared, across) for across in (0, 1))
-    return (near + far) / (2 * seqs * 8 * length)
+    far = exchange(squared, "dp")
+    return (squared + far) / (2 * seqs * 8 * length)
 
 
 def solution(mesh):

time: 155 us -> 137 us (0.88)
  the two profiles are of different devices: /device:TPU:8 before, /device:TPU:4 now
where the time goes in v6:
time: 137 us; the launch traced here: 136 us
  starting transfers between devices  49.6 us (36%)
  waiting for transfers between devices  44.5 us (32%)
  blocking collectives  14.1 us (10%)
  between operations  13.6 us (10%)
  local copies, waits for them, and re-layouts  4.73 us (3%)
  matrix products  4.43 us (3%)
  other arithmetic  2.6 us (2%)
  Pallas kernels  2.44 us (2%)
    all_to_all x4, starting transfers between devices, all_to_all(): return lax.all_to_all(v, axis, 0, 0, tiled=True)  31.5 us
    ppermute x7, waiting for transfers between devices, exchange(): return lax.ppermute(v, axis, [(0, 1), (1, 0)])  21.8 us
    all_to_all x4, waiting for transfers between devices, all_to_all(): return lax.all_to_all(v, axis, 0, 0, tiled=True)  20.8 us
    ppermute x7, starting transfers between devices, exchange(): return lax.ppermute(v, axis, [(0, 1), (1, 0)])  18 us
    all_to_all x1, blocking collectives, all_to_all(): return lax.all_to_all(v, axis, 0, 0, tiled=True)  14.1 us
    dot_general x2, matrix products, contract_last(): lax.dot_general(a, b, (((a.ndim - 1,), (b.ndim - 1,)), ((), ())), preferr...  4.43 us
  transfers between devices with their start and end apart: 12, of which 10 were waited for; matrix products, arithmetic and copies ran while one was open for 6% of the time, Pallas kernels for 2%

profile of v6, /device:TPU:4, one launch (start us, length us, event | category | flops | bytes accessed | tf_op | source)
XLA Modules:
  0.0 136.0 jit_solution(7572192606150299173)
XLA Ops:
  6.5 1.3 copy.17
  7.9 2.1 %collective-permute-start = (bf16[128,896]{1,0:T(8,128)(2,1)S(1)}, bf16[128,896]{1,0:T(8,128)(2,1)S(1)}, u32[]{:S(2)}, u32[]{:S(2)}) collective-permute-start(bf16[128,896]{1,0:T(8,128)(2,1)S(1)} %get-tuple-element.6), channel_id=1, source_target_pairs={{0,1},{1,0},{2,3},{3,2},{4,5},{5,4},{6,7},{7,6},{8,9},{9,8},{10,11... | collective-permute-start | bytes 688136 | tf_op jit(solution)/shard_map/ppermute | solution.py:19
  10.0 1.5 %collective-permute-done = bf16[128,896]{1,0:T(8,128)(2,1)S(1)} collective-permute-done((bf16[128,896]{1,0:T(8,128)(2,1)S(1)}, bf16[128,896]{1,0:T(8,128)(2,1)S(1)}, u32[]{:S(2)}, u32[]{:S(2)}) %collective-permute-start) | collective-permute-done | bytes 229408 | tf_op jit(solution)/shard_map/ppermute | solution.py:19
  11.4 0.8 pad_maximum_fusion.1
  12.3 0.8 broadcast_in_dim.40
  13.1 8.1 %all-to-all-start.1 = ((bf16[32,24,256]{2,1,0:T(8,128)(2,1)}), bf16[32,24,256]{2,1,0:T(8,128)(2,1)S(1)}, u32[]{:S(2)}, u32[]{:S(2)}) async-start(bf16[32,24,256]{2,1,0:T(8,128)(2,1)} %bitcast.12), calls=%async_computation.1 | async-start | bytes 786432 | tf_op jit(solution)/shard_map/all_to_all | solution.py:23
  21.2 3.7 %collective-permute-start.2 = (bf16[384,256]{1,0:T(8,128)(2,1)S(1)}, bf16[384,256]{1,0:T(8,128)(2,1)S(1)}, u32[]{:S(2)}, u32[]{:S(2)}) collective-permute-start(bf16[384,256]{1,0:T(8,128)(2,1)S(1)} %bitcast.49), channel_id=1, source_target_pairs={{0,2},{2,0},{1,3},{3,1},{4,6},{6,4},{5,7},{7,5},{8,10},{10,8},{9,1... | collective-permute-start | bytes 589832 | tf_op jit(solution)/shard_map/ppermute | solution.py:19
  24.9 1.9 %collective-permute-start.1 = (bf16[384,896]{1,0:T(8,128)(2,1)S(1)}, bf16[384,896]{1,0:T(8,128)(2,1)S(1)}, u32[]{:S(2)}, u32[]{:S(2)}) collective-permute-start(bf16[384,896]{1,0:T(8,128)(2,1)S(1)} %bitcast.52), channel_id=1, source_target_pairs={{0,1},{1,0},{2,3},{3,2},{4,5},{5,4},{6,7},{7,6},{8,9},{9,8},{10,11... | collective-permute-start | bytes 2064392 | tf_op jit(solution)/shard_map/ppermute | solution.py:19
  26.8 6.8 %collective-permute-done.2.beside = bf16[384,256]{1,0:T(8,128)(2,1)S(1)} collective-permute-done((bf16[384,256]{1,0:T(8,128)(2,1)S(1)}, bf16[384,256]{1,0:T(8,128)(2,1)S(1)}, u32[]{:S(2)}, u32[]{:S(2)}) %collective-permute-start.2) | collective-permute-done | bytes 196640 | tf_op jit(solution)/shard_map/ppermute | solution.py:19
  33.6 1.9 %collective-permute-start.3 = (bf16[2,384,256]{2,1,0:T(8,128)(2,1)S(1)}, bf16[2,384,256]{2,1,0:T(8,128)(2,1)S(1)}, u32[]{:S(2)}, u32[]{:S(2)}) collective-permute-start(bf16[2,384,256]{2,1,0:T(8,128)(2,1)S(1)} %pad_maximum_fusion.2), channel_id=1, source_target_pairs={{0,1},{1,0},{2,3},{3,2},{4,5},{5,4},{6,7},{7,6},{8,9},{9,8},{10,11... | collective-permute-start | bytes 1179656 | tf_op jit(solution)/shard_map/ppermute | solution.py:19
  35.6 0.5 iota_xor_fusion.place
  36.1 1.2 collective-permute-done.3.pair
  37.3 0.7 copy-done.4
  38.1 2.4 %shard_map.46 = f32[192,384]{1,0:T(8,128)} custom-call(s32[4]{0:T(128)} %iota_xor_fusion.place, bf16[8,4,24,256]{3,2,1,0:T(8,128)(2,1)} %bitcast.42, bf16[384,256]{1,0:T(8,128)(2,1)} %bitcast.48, bf16[384,256]{1,0:T(8,128)(2,1)} %copy-done.2, bf16[2,384,256]{2,1,0:T(8,128)(2,1)} %copy-done.4), custom_call_target="tpu_custom_call" | custom-call | tf_op jit(solution)/shard_map/pallas_call | solution.py:70
  40.6 11.7 %all-to-all-start.2 = ((f32[8,24,384]{2,1,0:T(8,128)}), f32[8,24,384]{2,1,0:T(8,128)S(1)}, u32[]{:S(2)}, u32[]{:S(2)}) async-start(f32[8,24,384]{2,1,0:T(8,128)} %bitcast.45), calls=%async_computation.2 | async-start | bytes 589824 | tf_op jit(solution)/shard_map/all_to_all | solution.py:23
  52.4 11.3 %all-to-all-done.2 = f32[8,24,384]{2,1,0:T(8,128)S(1)} async-done(((f32[8,24,384]{2,1,0:T(8,128)}), f32[8,24,384]{2,1,0:T(8,128)S(1)}, u32[]{:S(2)}, u32[]{:S(2)}) %all-to-all-start.2) | async-done | bytes 294944 | tf_op jit(solution)/shard_map/all_to_all | solution.py:23
  63.7 0.7 broadcast_in_dim.41
  64.3 3.4 %all-to-all-start.3 = ((bf16[8,24,384]{2,1,0:T(8,128)(2,1)}), bf16[8,24,384]{2,1,0:T(8,128)(2,1)S(1)}, u32[]{:S(2)}, u32[]{:S(2)}) async-start(bf16[8,24,384]{2,1,0:T(8,128)(2,1)} %broadcast_in_dim.41), calls=%async_computation.3 | async-start | bytes 294912 | tf_op jit(solution)/shard_map/all_to_all | solution.py:23
  67.7 1.9 %all-gather.2.cloned.1.call-done = bf16[1024,1792]{1,0:T(8,128)(2,1)} async-done(((bf16[128,1792]{1,0:T(8,128)(2,1)}), bf16[1024,1792]{1,0:T(8,128)(2,1)}) %all-gather.2.cloned.1.call-update) | async-done | bytes 3670032 | tf_op jit(solution)/shard_map/all_gather | solution.py:60
  69.6 4.1 %convolution_convert_fusion = bf16[1024,384]{1,0:T(8,128)(2,1)S(1)} fusion(bf16[1024,1792]{1,0:T(8,128)(2,1)} %all-gather.2.cloned.1.call-done, bf16[384,1792]{1,0:T(8,128)(2,1)S(1)} %pad_maximum_fusion), kind=kOutput, calls=%fused_computation | convolution fusion | flops 1409679360 | bytes 5832704 | tf_op jit(solution)/shard_map/dot_general | solution.py:31
  73.7 1.0 copy.18
  74.7 2.2 %all-to-all-done.3 = bf16[8,24,384]{2,1,0:T(8,128)(2,1)S(1)} async-done(((bf16[8,24,384]{2,1,0:T(8,128)(2,1)}), bf16[8,24,384]{2,1,0:T(8,128)(2,1)S(1)}, u32[]{:S(2)}, u32[]{:S(2)}) %all-to-all-start.3) | async-done | bytes 147488 | tf_op jit(solution)/shard_map/all_to_all | solution.py:23
  76.9 8.4 %all-to-all-start = ((bf16[16,8,8,384]{3,2,1,0:T(8,128)(2,1)}), bf16[16,8,8,384]{3,2,1,0:T(8,128)(2,1)S(1)}, u32[]{:S(2)}, u32[]{:S(2)}) async-start(bf16[16,8,8,384]{3,2,1,0:T(8,128)(2,1)} %bitcast.8), calls=%async_computation | async-start | bytes 1572864 | tf_op jit(solution)/shard_map/all_to_all | solution.py:23
  85.3 3.8 %collective-permute-start.4 = (bf16[8,24,384]{2,1,0:T(8,128)(2,1)S(1)}, bf16[8,24,384]{2,1,0:T(8,128)(2,1)S(1)}, u32[]{:S(2)}, u32[]{:S(2)}) collective-permute-start(bf16[8,24,384]{2,1,0:T(8,128)(2,1)S(1)} %all-to-all-done.3), channel_id=1, source_target_pairs={{0,2},{2,0},{1,3},{3,1},{4,6},{6,4},{5,7},{7,5},{8,10},{10,8},{9,1... | collective-permute-start | bytes 442376 | tf_op jit(solution)/shard_map/ppermute | solution.py:19
  89.1 6.5 %collective-permute-done.4 = bf16[8,24,384]{2,1,0:T(8,128)(2,1)S(1)} collective-permute-done((bf16[8,24,384]{2,1,0:T(8,128)(2,1)S(1)}, bf16[8,24,384]{2,1,0:T(8,128)(2,1)S(1)}, u32[]{:S(2)}, u32[]{:S(2)}) %collective-permute-start.4) | collective-permute-done | bytes 147488 | tf_op jit(solution)/shard_map/ppermute | solution.py:19
  95.7 1.9 %collective-permute-start.5 = (bf16[2,8,24,384]{3,2,0,1:T(8,128)(2,1)S(1)}, bf16[2,8,24,384]{3,2,0,1:T(8,128)(2,1)S(1)}, u32[]{:S(2)}, u32[]{:S(2)}) collective-permute-start(bf16[2,8,24,384]{3,2,0,1:T(8,128)(2,1)S(1)} %maximum_select_fusion.1), channel_id=1, source_target_pairs={{0,1},{1,0},{2,3},{3,2},{4,5},{5,4},{6,7},{7,6},{8,9},{9,8},{10,11... | collective-permute-start | bytes 884744 | tf_op jit(solution)/shard_map/ppermute | solution.py:19
  97.7 1.4 %collective-permute-done.5 = bf16[2,8,24,384]{3,2,0,1:T(8,128)(2,1)S(1)} collective-permute-done((bf16[2,8,24,384]{3,2,0,1:T(8,128)(2,1)S(1)}, bf16[2,8,24,384]{3,2,0,1:T(8,128)(2,1)S(1)}, u32[]{:S(2)}, u32[]{:S(2)}) %collective-permute-start.5) | collective-permute-done | bytes 294944 | tf_op jit(solution)/shard_map/ppermute | solution.py:19
  99.3 7.4 %all-to-all-done = bf16[16,8,8,384]{3,2,1,0:T(8,128)(2,1)S(1)} async-done(((bf16[16,8,8,384]{3,2,1,0:T(8,128)(2,1)}), bf16[16,8,8,384]{3,2,1,0:T(8,128)(2,1)S(1)}, u32[]{:S(2)}, u32[]{:S(2)}) %all-to-all-start) | async-done | bytes 786464 | tf_op jit(solution)/shard_map/all_to_all | solution.py:23
  107.2 14.1 %all_to_all.25 = bf16[8,2,8,768]{3,2,1,0:T(8,128)(2,1)S(1)} all-to-all(bf16[8,2,8,768]{3,2,1,0:T(8,128)(2,1)S(1)} %bitcast.47), channel_id=1, replica_groups=mesh['dp'=2,'seq'=8,'z'=8,'x'=2,'c'=2] {'seq'}, dimensions={0} | all-to-all | bytes 393216 | tf_op jit(solution)/shard_map/all_to_all | solution.py:23
  121.3 2.7 %collective-permute-start.6 = (f32[8,768]{1,0:T(8,128)S(1)}, f32[8,768]{1,0:T(8,128)S(1)}, u32[]{:S(2)}, u32[]{:S(2)}) collective-permute-start(f32[8,768]{1,0:T(8,128)S(1)} %multiply_reduce_fusion), channel_id=1, source_target_pairs={{0,256},{256,0},{1,257},{257,1},{2,258},{258,2},{3,259},{259,3},{4... | collective-permute-start | bytes 73736 | tf_op jit(solution)/shard_map/ppermute | solution.py:19
  124.0 4.5 %collective-permute-done.6 = f32[8,768]{1,0:T(8,128)S(1)} collective-permute-done((f32[8,768]{1,0:T(8,128)S(1)}, f32[8,768]{1,0:T(8,128)S(1)}, u32[]{:S(2)}, u32[]{:S(2)}) %collective-permute-start.6) | collective-permute-done | bytes 24608 | tf_op jit(solution)/shard_map/ppermute | solution.py:19
  128.5 0.6 add_multiply_fusion
  (31 shorter events, 1.2 us)
Async XLA Ops:
  6.5 63.0 %all-gather.2.cloned.1.call-start = ((), (), s32[]{:S(2)}) async-start(), calls=%async_computation.5 | async-start | bytes 4128768 | tf_op jit(solution)/shard_map/all_gather | solution.py:60
  6.5 5.7 %copy-start.5 = (bf16[256,96]{0,1:T(8,128)(2,1)S(1)}, bf16[256,96]{0,1:T(8,128)(2,1)}, u32[]{:S(2)}) copy-start(bf16[256,96]{0,1:T(8,128)(2,1)} %param.7) | copy-start | bytes 147460
  7.8 13.4 %copy-start.1 = (bf16[2,192,256]{2,1,0:T(8,128)(2,1)S(1)}, bf16[2,192,256]{2,1,0:T(8,128)(2,1)}, u32[]{:S(2)}) copy-start(bf16[2,192,256]{2,1,0:T(8,128)(2,1)} %param.5) | copy-start | bytes 589828
  7.8 17.1 %copy-start.3 = (bf16[2,192,896]{2,1,0:T(8,128)(2,1)S(1)}, bf16[2,192,896]{2,1,0:T(8,128)(2,1)}, u32[]{:S(2)}) copy-start(bf16[2,192,896]{2,1,0:T(8,128)(2,1)} %param.4) | copy-start | bytes 2064388
  7.9 3.5 %collective-permute-start = (bf16[128,896]{1,0:T(8,128)(2,1)S(1)}, bf16[128,896]{1,0:T(8,128)(2,1)S(1)}, u32[]{:S(2)}, u32[]{:S(2)}) collective-permute-start(bf16[128,896]{1,0:T(8,128)(2,1)S(1)} %get-tuple-element.6), channel_id=1, source_target_pairs={{0,1},{1,0},{2,3},{3,2},{4,5},{5,4},{6,7},{7,6},{8,9},{9,8},{10,11... | collective-permute-start | bytes 688136 | tf_op jit(solution)/shard_map/ppermute | solution.py:19
  13.1 24.2 %all-to-all-start.1 = ((bf16[32,24,256]{2,1,0:T(8,128)(2,1)}), bf16[32,24,256]{2,1,0:T(8,128)(2,1)S(1)}, u32[]{:S(2)}, u32[]{:S(2)}) async-start(bf16[32,24,256]{2,1,0:T(8,128)(2,1)} %bitcast.12), calls=%async_computation.1 | async-start | bytes 786432 | tf_op jit(solution)/shard_map/all_to_all | solution.py:23
  21.2 12.4 %collective-permute-start.2 = (bf16[384,256]{1,0:T(8,128)(2,1)S(1)}, bf16[384,256]{1,0:T(8,128)(2,1)S(1)}, u32[]{:S(2)}, u32[]{:S(2)}) collective-permute-start(bf16[384,256]{1,0:T(8,128)(2,1)S(1)} %bitcast.49), channel_id=1, source_target_pairs={{0,2},{2,0},{1,3},{3,1},{4,6},{6,4},{5,7},{7,5},{8,10},{10,8},{9,1... | collective-permute-start | bytes 589832 | tf_op jit(solution)/shard_map/ppermute | solution.py:19
  24.9 27.3 %collective-permute-start.1 = (bf16[384,896]{1,0:T(8,128)(2,1)S(1)}, bf16[384,896]{1,0:T(8,128)(2,1)S(1)}, u32[]{:S(2)}, u32[]{:S(2)}) collective-permute-start(bf16[384,896]{1,0:T(8,128)(2,1)S(1)} %bitcast.52), channel_id=1, source_target_pairs={{0,1},{1,0},{2,3},{3,2},{4,5},{5,4},{6,7},{7,6},{8,9},{9,8},{10,11... | collective-permute-start | bytes 2064392 | tf_op jit(solution)/shard_map/ppermute | solution.py:19
  33.6 3.7 %copy-start.2 = (bf16[384,256]{1,0:T(8,128)(2,1)}, bf16[384,256]{1,0:T(8,128)(2,1)S(1)}, u32[]{:S(2)}) copy-start(bf16[384,256]{1,0:T(8,128)(2,1)S(1)} %collective-permute-done.2.beside) | copy-start | bytes 589828
  33.6 3.6 %collective-permute-start.3 = (bf16[2,384,256]{2,1,0:T(8,128)(2,1)S(1)}, bf16[2,384,256]{2,1,0:T(8,128)(2,1)S(1)}, u32[]{:S(2)}, u32[]{:S(2)}) collective-permute-start(bf16[2,384,256]{2,1,0:T(8,128)(2,1)S(1)} %pad_maximum_fusion.2), channel_id=1, source_target_pairs={{0,1},{1,0},{2,3},{3,2},{4,5},{5,4},{6,7},{7,6},{8,9},{9,8},{10,11... | collective-permute-start | bytes 1179656 | tf_op jit(solution)/shard_map/ppermute | solution.py:19
  37.3 0.8 copy-start.4
  37.3 0.9 copy-start
  40.6 23.0 %all-to-all-start.2 = ((f32[8,24,384]{2,1,0:T(8,128)}), f32[8,24,384]{2,1,0:T(8,128)S(1)}, u32[]{:S(2)}, u32[]{:S(2)}) async-start(f32[8,24,384]{2,1,0:T(8,128)} %bitcast.45), calls=%async_computation.2 | async-start | bytes 589824 | tf_op jit(solution)/shard_map/all_to_all | solution.py:23
  64.3 12.6 %all-to-all-start.3 = ((bf16[8,24,384]{2,1,0:T(8,128)(2,1)}), bf16[8,24,384]{2,1,0:T(8,128)(2,1)S(1)}, u32[]{:S(2)}, u32[]{:S(2)}) async-start(bf16[8,24,384]{2,1,0:T(8,128)(2,1)} %broadcast_in_dim.41), calls=%async_computation.3 | async-start | bytes 294912 | tf_op jit(solution)/shard_map/all_to_all | solution.py:23
  76.9 29.8 %all-to-all-start = ((bf16[16,8,8,384]{3,2,1,0:T(8,128)(2,1)}), bf16[16,8,8,384]{3,2,1,0:T(8,128)(2,1)S(1)}, u32[]{:S(2)}, u32[]{:S(2)}) async-start(bf16[16,8,8,384]{3,2,1,0:T(8,128)(2,1)} %bitcast.8), calls=%async_computation | async-start | bytes 1572864 | tf_op jit(solution)/shard_map/all_to_all | solution.py:23
  85.3 10.3 %collective-permute-start.4 = (bf16[8,24,384]{2,1,0:T(8,128)(2,1)S(1)}, bf16[8,24,384]{2,1,0:T(8,128)(2,1)S(1)}, u32[]{:S(2)}, u32[]{:S(2)}) collective-permute-start(bf16[8,24,384]{2,1,0:T(8,128)(2,1)S(1)} %all-to-all-done.3), channel_id=1, source_target_pairs={{0,2},{2,0},{1,3},{3,1},{4,6},{6,4},{5,7},{7,5},{8,10},{10,8},{9,1... | collective-permute-start | bytes 442376 | tf_op jit(solution)/shard_map/ppermute | solution.py:19
  95.7 3.5 %collective-permute-start.5 = (bf16[2,8,24,384]{3,2,0,1:T(8,128)(2,1)S(1)}, bf16[2,8,24,384]{3,2,0,1:T(8,128)(2,1)S(1)}, u32[]{:S(2)}, u32[]{:S(2)}) collective-permute-start(bf16[2,8,24,384]{3,2,0,1:T(8,128)(2,1)S(1)} %maximum_select_fusion.1), channel_id=1, source_target_pairs={{0,1},{1,0},{2,3},{3,2},{4,5},{5,4},{6,7},{7,6},{8,9},{9,8},{10,11... | collective-permute-start | bytes 884744 | tf_op jit(solution)/shard_map/ppermute | solution.py:19
  121.3 7.2 %collective-permute-start.6 = (f32[8,768]{1,0:T(8,128)S(1)}, f32[8,768]{1,0:T(8,128)S(1)}, u32[]{:S(2)}, u32[]{:S(2)}) collective-permute-start(f32[8,768]{1,0:T(8,128)S(1)} %multiply_reduce_fusion), channel_id=1, source_target_pairs={{0,256},{256,0},{1,257},{257,1},{2,258},{258,2},{3,259},{259,3},{4... | collective-permute-start | bytes 73736 | tf_op jit(solution)/shard_map/ppermute | solution.py:19
Sparse Core Ops, SparseCore 0:
  12.4 57.1 all-gather.1

commit v7 on v6

--- a/solution.py
+++ b/solution.py
@@ -34,10 +34,10 @@
 
 
 def grad_kernel(place, cols, own, beside, pair, out):
-    rows = cols.shape[0] * cols.shape[2]
+    rows = cols.shape[1] * cols.shape[2]
     found = jnp.zeros(out.shape, F32)
     for k, features in enumerate((own[...], pair[0], beside[...], pair[1])):
-        columns = cols[:, pl.ds(place[k], 1)].astype(F32).reshape(rows, -1).astype(BF16)
+        columns = cols[pl.ds(place[k], 1)].astype(F32).reshape(rows, -1).astype(BF16)
         found = found + contract_last(columns, features)
     out[...] = found
 
@@ -60,9 +60,9 @@
     columns = lax.all_gather(block, "seq", axis=0, tiled=True)
     x_other = exchange(x_own, "c")
 
-    spread = jnp.broadcast_to(basis_out.T.reshape(1, 4, 24, narrow), (8, 4, 24, narrow))
-    out_cols = all_to_all(spread.reshape(32, 24, narrow), ("seq", "x", "c"))
-    out_cols = out_cols.reshape(8, 4, 24, narrow)
+    spread = jnp.broadcast_to(basis_out.T.reshape(4, 1, 24, narrow), (4, 8, 24, narrow))
+    out_cols = all_to_all(spread.reshape(32, 24, narrow), ("x", "c", "seq"))
+    out_cols = out_cols.reshape(4, 8, 24, narrow)
     g_beside = exchange(g_own, "x")
     g_pair = exchange(jnp.stack([g_own, g_beside]), "c")
 

time: 137 us -> 137 us (level)
  starting transfers between devices: 49.6 us -> 48.2 us
  waiting for transfers between devices: 44.5 us -> 45.9 us
    all_to_all x4, waiting for transfers between devices: 20.8 us -> 22.3 us  [all_to_all(): return lax.all_to_all(v, axis, 0, 0, tiled=True)]
where the time goes in v7:
time: 137 us; the launch traced here: 136 us
  starting transfers between devices  48.2 us (35%)
  waiting for transfers between devices  45.9 us (34%)
  blocking collectives  14.1 us (10%)
  between operations  13.6 us (10%)
  local copies, waits for them, and re-layouts  4.73 us (3%)
  matrix products  4.43 us (3%)
  other arithmetic  2.6 us (2%)
  Pallas kernels  2.43 us (2%)
    all_to_all x4, starting transfers between devices, all_to_all(): return lax.all_to_all(v, axis, 0, 0, tiled=True)  30.2 us
    all_to_all x4, waiting for transfers between devices, all_to_all(): return lax.all_to_all(v, axis, 0, 0, tiled=True)  22.3 us
    ppermute x7, waiting for transfers between devices, exchange(): return lax.ppermute(v, axis, [(0, 1), (1, 0)])  21.6 us
    ppermute x7, starting transfers between devices, exchange(): return lax.ppermute(v, axis, [(0, 1), (1, 0)])  18.1 us
    all_to_all x1, blocking collectives, all_to_all(): return lax.all_to_all(v, axis, 0, 0, tiled=True)  14.1 us
    dot_general x2, matrix products, contract_last(): lax.dot_general(a, b, (((a.ndim - 1,), (b.ndim - 1,)), ((), ())), preferr...  4.43 us
  transfers between devices with their start and end apart: 12, of which 10 were waited for; matrix products, arithmetic and copies ran while one was open for 6% of the time, Pallas kernels for 2%

profile of v7, /device:TPU:4, one launch (start us, length us, event | category | flops | bytes accessed | tf_op | source)
XLA Modules:
  0.0 136.0 jit_solution(14598247323824260448)
XLA Ops:
  6.5 1.3 copy.17
  7.9 2.1 %collective-permute-start = (bf16[128,896]{1,0:T(8,128)(2,1)S(1)}, bf16[128,896]{1,0:T(8,128)(2,1)S(1)}, u32[]{:S(2)}, u32[]{:S(2)}) collective-permute-start(bf16[128,896]{1,0:T(8,128)(2,1)S(1)} %get-tuple-element.6), channel_id=1, source_target_pairs={{0,1},{1,0},{2,3},{3,2},{4,5},{5,4},{6,7},{7,6},{8,9},{9,8},{10,11... | collective-permute-start | bytes 688136 | tf_op jit(solution)/shard_map/ppermute | solution.py:19
  10.0 1.5 %collective-permute-done = bf16[128,896]{1,0:T(8,128)(2,1)S(1)} collective-permute-done((bf16[128,896]{1,0:T(8,128)(2,1)S(1)}, bf16[128,896]{1,0:T(8,128)(2,1)S(1)}, u32[]{:S(2)}, u32[]{:S(2)}) %collective-permute-start) | collective-permute-done | bytes 229408 | tf_op jit(solution)/shard_map/ppermute | solution.py:19
  11.4 0.8 pad_maximum_fusion.1
  12.3 0.8 broadcast_in_dim.40
  13.1 8.1 %all-to-all-start.1 = ((bf16[32,24,256]{2,1,0:T(8,128)(2,1)}), bf16[32,24,256]{2,1,0:T(8,128)(2,1)S(1)}, u32[]{:S(2)}, u32[]{:S(2)}) async-start(bf16[32,24,256]{2,1,0:T(8,128)(2,1)} %bitcast.12), calls=%async_computation.1 | async-start | bytes 786432 | tf_op jit(solution)/shard_map/all_to_all | solution.py:23
  21.2 3.7 %collective-permute-start.2 = (bf16[384,256]{1,0:T(8,128)(2,1)S(1)}, bf16[384,256]{1,0:T(8,128)(2,1)S(1)}, u32[]{:S(2)}, u32[]{:S(2)}) collective-permute-start(bf16[384,256]{1,0:T(8,128)(2,1)S(1)} %bitcast.49), channel_id=1, source_target_pairs={{0,2},{2,0},{1,3},{3,1},{4,6},{6,4},{5,7},{7,5},{8,10},{10,8},{9,1... | collective-permute-start | bytes 589832 | tf_op jit(solution)/shard_map/ppermute | solution.py:19
  24.9 1.9 %collective-permute-start.1 = (bf16[384,896]{1,0:T(8,128)(2,1)S(1)}, bf16[384,896]{1,0:T(8,128)(2,1)S(1)}, u32[]{:S(2)}, u32[]{:S(2)}) collective-permute-start(bf16[384,896]{1,0:T(8,128)(2,1)S(1)} %bitcast.52), channel_id=1, source_target_pairs={{0,1},{1,0},{2,3},{3,2},{4,5},{5,4},{6,7},{7,6},{8,9},{9,8},{10,11... | collective-permute-start | bytes 2064392 | tf_op jit(solution)/shard_map/ppermute | solution.py:19
  26.9 6.6 %collective-permute-done.2.beside = bf16[384,256]{1,0:T(8,128)(2,1)S(1)} collective-permute-done((bf16[384,256]{1,0:T(8,128)(2,1)S(1)}, bf16[384,256]{1,0:T(8,128)(2,1)S(1)}, u32[]{:S(2)}, u32[]{:S(2)}) %collective-permute-start.2) | collective-permute-done | bytes 196640 | tf_op jit(solution)/shard_map/ppermute | solution.py:19
  33.5 1.9 %collective-permute-start.3 = (bf16[2,384,256]{2,1,0:T(8,128)(2,1)S(1)}, bf16[2,384,256]{2,1,0:T(8,128)(2,1)S(1)}, u32[]{:S(2)}, u32[]{:S(2)}) collective-permute-start(bf16[2,384,256]{2,1,0:T(8,128)(2,1)S(1)} %pad_maximum_fusion.2), channel_id=1, source_target_pairs={{0,1},{1,0},{2,3},{3,2},{4,5},{5,4},{6,7},{7,6},{8,9},{9,8},{10,11... | collective-permute-start | bytes 1179656 | tf_op jit(solution)/shard_map/ppermute | solution.py:19
  35.5 0.5 iota_xor_fusion.place
  36.0 1.2 collective-permute-done.3.pair
  37.1 0.7 copy-done.4
  38.0 2.4 %shard_map.46 = f32[192,384]{1,0:T(8,128)} custom-call(s32[4]{0:T(128)} %iota_xor_fusion.place, bf16[4,8,24,256]{3,2,1,0:T(8,128)(2,1)} %bitcast.42, bf16[384,256]{1,0:T(8,128)(2,1)} %bitcast.48, bf16[384,256]{1,0:T(8,128)(2,1)} %copy-done.2, bf16[2,384,256]{2,1,0:T(8,128)(2,1)} %copy-done.4), custom_call_target="tpu_custom_call" | custom-call | tf_op jit(solution)/shard_map/pallas_call | solution.py:70
  40.4 10.0 %all-to-all-start.2 = ((f32[8,24,384]{2,1,0:T(8,128)}), f32[8,24,384]{2,1,0:T(8,128)S(1)}, u32[]{:S(2)}, u32[]{:S(2)}) async-start(f32[8,24,384]{2,1,0:T(8,128)} %bitcast.45), calls=%async_computation.2 | async-start | bytes 589824 | tf_op jit(solution)/shard_map/all_to_all | solution.py:23
  50.6 12.8 %all-to-all-done.2 = f32[8,24,384]{2,1,0:T(8,128)S(1)} async-done(((f32[8,24,384]{2,1,0:T(8,128)}), f32[8,24,384]{2,1,0:T(8,128)S(1)}, u32[]{:S(2)}, u32[]{:S(2)}) %all-to-all-start.2) | async-done | bytes 294944 | tf_op jit(solution)/shard_map/all_to_all | solution.py:23
  63.4 0.7 broadcast_in_dim.41
  64.0 3.4 %all-to-all-start.3 = ((bf16[8,24,384]{2,1,0:T(8,128)(2,1)}), bf16[8,24,384]{2,1,0:T(8,128)(2,1)S(1)}, u32[]{:S(2)}, u32[]{:S(2)}) async-start(bf16[8,24,384]{2,1,0:T(8,128)(2,1)} %broadcast_in_dim.41), calls=%async_computation.3 | async-start | bytes 294912 | tf_op jit(solution)/shard_map/all_to_all | solution.py:23
  67.4 1.9 %all-gather.2.cloned.1.call-done = bf16[1024,1792]{1,0:T(8,128)(2,1)} async-done(((bf16[128,1792]{1,0:T(8,128)(2,1)}), bf16[1024,1792]{1,0:T(8,128)(2,1)}) %all-gather.2.cloned.1.call-update) | async-done | bytes 3670032 | tf_op jit(solution)/shard_map/all_gather | solution.py:60
  69.3 4.1 %convolution_convert_fusion = bf16[1024,384]{1,0:T(8,128)(2,1)S(1)} fusion(bf16[1024,1792]{1,0:T(8,128)(2,1)} %all-gather.2.cloned.1.call-done, bf16[384,1792]{1,0:T(8,128)(2,1)S(1)} %pad_maximum_fusion), kind=kOutput, calls=%fused_computation | convolution fusion | flops 1409679360 | bytes 5832704 | tf_op jit(solution)/shard_map/dot_general | solution.py:31
  73.4 1.0 copy.18
  74.5 2.1 %all-to-all-done.3 = bf16[8,24,384]{2,1,0:T(8,128)(2,1)S(1)} async-done(((bf16[8,24,384]{2,1,0:T(8,128)(2,1)}), bf16[8,24,384]{2,1,0:T(8,128)(2,1)S(1)}, u32[]{:S(2)}, u32[]{:S(2)}) %all-to-all-start.3) | async-done | bytes 147488 | tf_op jit(solution)/shard_map/all_to_all | solution.py:23
  76.6 8.7 %all-to-all-start = ((bf16[16,8,8,384]{3,2,1,0:T(8,128)(2,1)}), bf16[16,8,8,384]{3,2,1,0:T(8,128)(2,1)S(1)}, u32[]{:S(2)}, u32[]{:S(2)}) async-start(bf16[16,8,8,384]{3,2,1,0:T(8,128)(2,1)} %bitcast.8), calls=%async_computation | async-start | bytes 1572864 | tf_op jit(solution)/shard_map/all_to_all | solution.py:23
  85.3 3.8 %collective-permute-start.4 = (bf16[8,24,384]{2,1,0:T(8,128)(2,1)S(1)}, bf16[8,24,384]{2,1,0:T(8,128)(2,1)S(1)}, u32[]{:S(2)}, u32[]{:S(2)}) collective-permute-start(bf16[8,24,384]{2,1,0:T(8,128)(2,1)S(1)} %all-to-all-done.3), channel_id=1, source_target_pairs={{0,2},{2,0},{1,3},{3,1},{4,6},{6,4},{5,7},{7,5},{8,10},{10,8},{9,1... | collective-permute-start | bytes 442376 | tf_op jit(solution)/shard_map/ppermute | solution.py:19
  89.1 6.5 %collective-permute-done.4 = bf16[8,24,384]{2,1,0:T(8,128)(2,1)S(1)} collective-permute-done((bf16[8,24,384]{2,1,0:T(8,128)(2,1)S(1)}, bf16[8,24,384]{2,1,0:T(8,128)(2,1)S(1)}, u32[]{:S(2)}, u32[]{:S(2)}) %collective-permute-start.4) | collective-permute-done | bytes 147488 | tf_op jit(solution)/shard_map/ppermute | solution.py:19
  95.7 1.9 %collective-permute-start.5 = (bf16[2,8,24,384]{3,2,0,1:T(8,128)(2,1)S(1)}, bf16[2,8,24,384]{3,2,0,1:T(8,128)(2,1)S(1)}, u32[]{:S(2)}, u32[]{:S(2)}) collective-permute-start(bf16[2,8,24,384]{3,2,0,1:T(8,128)(2,1)S(1)} %maximum_select_fusion.1), channel_id=1, source_target_pairs={{0,1},{1,0},{2,3},{3,2},{4,5},{5,4},{6,7},{7,6},{8,9},{9,8},{10,11... | collective-permute-start | bytes 884744 | tf_op jit(solution)/shard_map/ppermute | solution.py:19
  97.7 1.4 %collective-permute-done.5 = bf16[2,8,24,384]{3,2,0,1:T(8,128)(2,1)S(1)} collective-permute-done((bf16[2,8,24,384]{3,2,0,1:T(8,128)(2,1)S(1)}, bf16[2,8,24,384]{3,2,0,1:T(8,128)(2,1)S(1)}, u32[]{:S(2)}, u32[]{:S(2)}) %collective-permute-start.5) | collective-permute-done | bytes 294944 | tf_op jit(solution)/shard_map/ppermute | solution.py:19
  99.3 7.4 %all-to-all-done = bf16[16,8,8,384]{3,2,1,0:T(8,128)(2,1)S(1)} async-done(((bf16[16,8,8,384]{3,2,1,0:T(8,128)(2,1)}), bf16[16,8,8,384]{3,2,1,0:T(8,128)(2,1)S(1)}, u32[]{:S(2)}, u32[]{:S(2)}) %all-to-all-start) | async-done | bytes 786464 | tf_op jit(solution)/shard_map/all_to_all | solution.py:23
  107.2 14.1 %all_to_all.25 = bf16[8,2,8,768]{3,2,1,0:T(8,128)(2,1)S(1)} all-to-all(bf16[8,2,8,768]{3,2,1,0:T(8,128)(2,1)S(1)} %bitcast.47), channel_id=1, replica_groups=mesh['dp'=2,'seq'=8,'z'=8,'x'=2,'c'=2] {'seq'}, dimensions={0} | all-to-all | bytes 393216 | tf_op jit(solution)/shard_map/all_to_all | solution.py:23
  121.3 2.7 %collective-permute-start.6 = (f32[8,768]{1,0:T(8,128)S(1)}, f32[8,768]{1,0:T(8,128)S(1)}, u32[]{:S(2)}, u32[]{:S(2)}) collective-permute-start(f32[8,768]{1,0:T(8,128)S(1)} %multiply_reduce_fusion), channel_id=1, source_target_pairs={{0,256},{256,0},{1,257},{257,1},{2,258},{258,2},{3,259},{259,3},{4... | collective-permute-start | bytes 73736 | tf_op jit(solution)/shard_map/ppermute | solution.py:19
  124.1 4.5 %collective-permute-done.6 = f32[8,768]{1,0:T(8,128)S(1)} collective-permute-done((f32[8,768]{1,0:T(8,128)S(1)}, f32[8,768]{1,0:T(8,128)S(1)}, u32[]{:S(2)}, u32[]{:S(2)}) %collective-permute-start.6) | collective-permute-done | bytes 24608 | tf_op jit(solution)/shard_map/ppermute | solution.py:19
  128.6 0.6 add_multiply_fusion
  (31 shorter events, 1.2 us)
Async XLA Ops:
  6.5 62.8 %all-gather.2.cloned.1.call-start = ((), (), s32[]{:S(2)}) async-start(), calls=%async_computation.5 | async-start | bytes 4128768 | tf_op jit(solution)/shard_map/all_gather | solution.py:60
  6.5 5.7 %copy-start.5 = (bf16[256,96]{0,1:T(8,128)(2,1)S(1)}, bf16[256,96]{0,1:T(8,128)(2,1)}, u32[]{:S(2)}) copy-start(bf16[256,96]{0,1:T(8,128)(2,1)} %param.7) | copy-start | bytes 147460
  7.8 13.4 %copy-start.1 = (bf16[2,192,256]{2,1,0:T(8,128)(2,1)S(1)}, bf16[2,192,256]{2,1,0:T(8,128)(2,1)}, u32[]{:S(2)}) copy-start(bf16[2,192,256]{2,1,0:T(8,128)(2,1)} %param.5) | copy-start | bytes 589828
  7.8 17.1 %copy-start.3 = (bf16[2,192,896]{2,1,0:T(8,128)(2,1)S(1)}, bf16[2,192,896]{2,1,0:T(8,128)(2,1)}, u32[]{:S(2)}) copy-start(bf16[2,192,896]{2,1,0:T(8,128)(2,1)} %param.4) | copy-start | bytes 2064388
  7.9 3.5 %collective-permute-start = (bf16[128,896]{1,0:T(8,128)(2,1)S(1)}, bf16[128,896]{1,0:T(8,128)(2,1)S(1)}, u32[]{:S(2)}, u32[]{:S(2)}) collective-permute-start(bf16[128,896]{1,0:T(8,128)(2,1)S(1)} %get-tuple-element.6), channel_id=1, source_target_pairs={{0,1},{1,0},{2,3},{3,2},{4,5},{5,4},{6,7},{7,6},{8,9},{9,8},{10,11... | collective-permute-start | bytes 688136 | tf_op jit(solution)/shard_map/ppermute | solution.py:19
  13.1 24.1 %all-to-all-start.1 = ((bf16[32,24,256]{2,1,0:T(8,128)(2,1)}), bf16[32,24,256]{2,1,0:T(8,128)(2,1)S(1)}, u32[]{:S(2)}, u32[]{:S(2)}) async-start(bf16[32,24,256]{2,1,0:T(8,128)(2,1)} %bitcast.12), calls=%async_computation.1 | async-start | bytes 786432 | tf_op jit(solution)/shard_map/all_to_all | solution.py:23
  21.2 12.3 %collective-permute-start.2 = (bf16[384,256]{1,0:T(8,128)(2,1)S(1)}, bf16[384,256]{1,0:T(8,128)(2,1)S(1)}, u32[]{:S(2)}, u32[]{:S(2)}) collective-permute-start(bf16[384,256]{1,0:T(8,128)(2,1)S(1)} %bitcast.49), channel_id=1, source_target_pairs={{0,2},{2,0},{1,3},{3,1},{4,6},{6,4},{5,7},{7,5},{8,10},{10,8},{9,1... | collective-permute-start | bytes 589832 | tf_op jit(solution)/shard_map/ppermute | solution.py:19
  24.9 25.5 %collective-permute-start.1 = (bf16[384,896]{1,0:T(8,128)(2,1)S(1)}, bf16[384,896]{1,0:T(8,128)(2,1)S(1)}, u32[]{:S(2)}, u32[]{:S(2)}) collective-permute-start(bf16[384,896]{1,0:T(8,128)(2,1)S(1)} %bitcast.52), channel_id=1, source_target_pairs={{0,1},{1,0},{2,3},{3,2},{4,5},{5,4},{6,7},{7,6},{8,9},{9,8},{10,11... | collective-permute-start | bytes 2064392 | tf_op jit(solution)/shard_map/ppermute | solution.py:19
  33.5 3.7 %copy-start.2 = (bf16[384,256]{1,0:T(8,128)(2,1)}, bf16[384,256]{1,0:T(8,128)(2,1)S(1)}, u32[]{:S(2)}) copy-start(bf16[384,256]{1,0:T(8,128)(2,1)S(1)} %collective-permute-done.2.beside) | copy-start | bytes 589828
  33.5 3.6 %collective-permute-start.3 = (bf16[2,384,256]{2,1,0:T(8,128)(2,1)S(1)}, bf16[2,384,256]{2,1,0:T(8,128)(2,1)S(1)}, u32[]{:S(2)}, u32[]{:S(2)}) collective-permute-start(bf16[2,384,256]{2,1,0:T(8,128)(2,1)S(1)} %pad_maximum_fusion.2), channel_id=1, source_target_pairs={{0,1},{1,0},{2,3},{3,2},{4,5},{5,4},{6,7},{7,6},{8,9},{9,8},{10,11... | collective-permute-start | bytes 1179656 | tf_op jit(solution)/shard_map/ppermute | solution.py:19
  37.1 0.8 copy-start.4
  37.1 0.9 copy-start
  40.4 22.9 %all-to-all-start.2 = ((f32[8,24,384]{2,1,0:T(8,128)}), f32[8,24,384]{2,1,0:T(8,128)S(1)}, u32[]{:S(2)}, u32[]{:S(2)}) async-start(f32[8,24,384]{2,1,0:T(8,128)} %bitcast.45), calls=%async_computation.2 | async-start | bytes 589824 | tf_op jit(solution)/shard_map/all_to_all | solution.py:23
  64.0 12.6 %all-to-all-start.3 = ((bf16[8,24,384]{2,1,0:T(8,128)(2,1)}), bf16[8,24,384]{2,1,0:T(8,128)(2,1)S(1)}, u32[]{:S(2)}, u32[]{:S(2)}) async-start(bf16[8,24,384]{2,1,0:T(8,128)(2,1)} %broadcast_in_dim.41), calls=%async_computation.3 | async-start | bytes 294912 | tf_op jit(solution)/shard_map/all_to_all | solution.py:23
  76.6 30.1 %all-to-all-start = ((bf16[16,8,8,384]{3,2,1,0:T(8,128)(2,1)}), bf16[16,8,8,384]{3,2,1,0:T(8,128)(2,1)S(1)}, u32[]{:S(2)}, u32[]{:S(2)}) async-start(bf16[16,8,8,384]{3,2,1,0:T(8,128)(2,1)} %bitcast.8), calls=%async_computation | async-start | bytes 1572864 | tf_op jit(solution)/shard_map/all_to_all | solution.py:23
  85.3 10.3 %collective-permute-start.4 = (bf16[8,24,384]{2,1,0:T(8,128)(2,1)S(1)}, bf16[8,24,384]{2,1,0:T(8,128)(2,1)S(1)}, u32[]{:S(2)}, u32[]{:S(2)}) collective-permute-start(bf16[8,24,384]{2,1,0:T(8,128)(2,1)S(1)} %all-to-all-done.3), channel_id=1, source_target_pairs={{0,2},{2,0},{1,3},{3,1},{4,6},{6,4},{5,7},{7,5},{8,10},{10,8},{9,1... | collective-permute-start | bytes 442376 | tf_op jit(solution)/shard_map/ppermute | solution.py:19
  95.7 3.5 %collective-permute-start.5 = (bf16[2,8,24,384]{3,2,0,1:T(8,128)(2,1)S(1)}, bf16[2,8,24,384]{3,2,0,1:T(8,128)(2,1)S(1)}, u32[]{:S(2)}, u32[]{:S(2)}) collective-permute-start(bf16[2,8,24,384]{3,2,0,1:T(8,128)(2,1)S(1)} %maximum_select_fusion.1), channel_id=1, source_target_pairs={{0,1},{1,0},{2,3},{3,2},{4,5},{5,4},{6,7},{7,6},{8,9},{9,8},{10,11... | collective-permute-start | bytes 884744 | tf_op jit(solution)/shard_map/ppermute | solution.py:19
  121.3 7.2 %collective-permute-start.6 = (f32[8,768]{1,0:T(8,128)S(1)}, f32[8,768]{1,0:T(8,128)S(1)}, u32[]{:S(2)}, u32[]{:S(2)}) collective-permute-start(f32[8,768]{1,0:T(8,128)S(1)} %multiply_reduce_fusion), channel_id=1, source_target_pairs={{0,256},{256,0},{1,257},{257,1},{2,258},{258,2},{3,259},{259,3},{4... | collective-permute-start | bytes 73736 | tf_op jit(solution)/shard_map/ppermute | solution.py:19
Sparse Core Ops, SparseCore 0:
  12.4 56.8 all-gather.1
